TPU v7x, 512 devices: a 4x2x32 block of a 4x8x32 slice. The times are simulated.
512 devices in a mesh: groups: 2 (over y), pair: 32 (over z), vir: 4 (over x), sub: 2 (over core).
Axes of the slice: x: 4, y: 2, z: 32, core: 2. Of those that a mesh axis runs over, the one named last changes fastest.
The devices are a block of a 4x8x32 slice.
Arguments:
- amplitudes: bfloat16 [64, 36, 128, 128], P(('groups', 'pair'), 'vir', 'sub'), parts along dimension 0, may hold values from -1 to 1
- pair_list: int32 [64, 2], P(('groups', 'pair')), parts along dimension 0, may hold values from 0 to 255, as said below
- tile_list: int32 [36, 2], replicated, may hold values from 0 to 7, as said below
Outputs:
- p_virt: float32 [72, 128, 128], P(('groups', 'vir'), 'sub'), parts along dimension 0
- p_occ: float32 [512, 256], P('groups'), parts along dimension 0
There are 2 independent parts, one for each index of `groups`. A program takes and returns all parts, laid end to end along the dimension named above; an argument that names none is the same for every part. Nothing has to cross between parts.
Inputs may be any that keep to these rules, and one draw needn't show every extreme that they name: `pair_list`: each row holds two different occupied orbitals in increasing order; no two rows are equal. `tile_list`: each row holds a tile row and a tile column, row <= column; every such couple of the 8 x 8 tile grid appears exactly once.
All inputs are finite; a program needn't handle non-finite values.
Results may differ from a plain program's by a relative error of at most 0.0003.
Values may be sent and summed in bfloat16 or wider, within the bound.
No kernel may reach another device: no remote copies, remote signals or barrier semaphores. Data moves between devices by JAX's collectives and lax.ppermute only.
A program may use at most 64 MiB of HBM per device.

v0:
```python
import functools

import jax
import jax.numpy as jnp
from jax import lax
from jax.sharding import PartitionSpec as P

OCC = 256
NTV = 8
NT = 36


def laid_out(blocks, dim):
    blocks = jnp.moveaxis(blocks, 0, dim)
    lengths = blocks.shape
    return blocks.reshape(*lengths[:dim], lengths[dim] * lengths[dim + 1], *lengths[dim + 2 :])


def sent_to_all(array, axis):
    copies = jnp.broadcast_to(array, (lax.axis_size(axis), *array.shape))
    return lax.all_to_all(copies, axis, split_axis=0, concat_axis=0, tiled=True)


def gather_directly(array, axis, dim):
    return laid_out(sent_to_all(array, axis), dim)


def one_axis_at_a_time(array, axes):
    return functools.reduce(lax.psum, axes, array)


def total_of_pieces(array, axis):
    blocks = lax.all_gather(array, axis)
    return blocks.sum(axis=0)


def slot_table(tile_list):
    tile_grid = jnp.arange(NTV, dtype=jnp.int32)
    upper_hit = (tile_list[:, 0][None, None, :] == tile_grid[:, None, None]) & (
        tile_list[:, 1][None, None, :] == tile_grid[None, :, None]
    )
    either_hit = upper_hit | jnp.transpose(upper_hit, (1, 0, 2))
    slot_ids = jnp.arange(NT, dtype=jnp.int32)
    return jnp.sum(jnp.where(either_hit, slot_ids[None, None, :], 0), axis=2)


def occurrences(pair_rows):
    orbital = jnp.concatenate([pair_rows[:, 0], pair_rows[:, 1]])
    partner = jnp.concatenate([pair_rows[:, 1], pair_rows[:, 0]])
    pair_count = pair_rows.shape[0]
    parity = jnp.concatenate(
        [jnp.ones((pair_count,), jnp.float32), -jnp.ones((pair_count,), jnp.float32)]
    )
    return (orbital, partner, parity)


def occ_density(pair_gram, left_pairs, right_pairs):
    left_orb, left_partner, left_sign = occurrences(left_pairs)
    right_orb, right_partner, right_sign = occurrences(right_pairs)
    doubled = jnp.tile(pair_gram, (2, 2))
    couple = jnp.where(
        left_partner[:, None] == right_partner[None, :],
        left_sign[:, None] * right_sign[None, :] * doubled,
        0.0,
    )
    orbitals = jnp.arange(OCC, dtype=jnp.int32)
    left_hot = (left_orb[:, None] == orbitals[None, :]).astype(jnp.float32)
    right_hot = (right_orb[:, None] == orbitals[None, :]).astype(jnp.float32)
    inner_sum = jnp.dot(couple, right_hot, precision=lax.Precision.HIGHEST)
    return -jnp.dot(left_hot.T, inner_sum, precision=lax.Precision.HIGHEST)


def oriented(packed, slot_grid, tile_ids, column):
    gathered = packed[:, slot_grid[tile_ids, column]]
    turned = jnp.swapaxes(gathered, 2, 3)
    on_or_above = (tile_ids <= column)[None, :, None, None]
    on_or_below = (tile_ids >= column)[None, :, None, None]
    nothing = jnp.zeros_like(gathered)
    return jnp.where(on_or_above, gathered, nothing) - jnp.where(on_or_below, turned, nothing)


def shards(amplitudes, pair_list, tile_list):
    pair_dev, slot_dev, row_dev, tile_width = amplitudes.shape
    vir_at = lax.axis_index("vir")
    sub_at = lax.axis_index("sub")
    nothing = jnp.zeros((), jnp.bfloat16)
    in_tile = jnp.arange(tile_width, dtype=jnp.int32)
    own_list = lax.dynamic_slice_in_dim(tile_list, vir_at * slot_dev, slot_dev, 0)
    own_rows = sub_at * row_dev + jnp.arange(row_dev, dtype=jnp.int32)
    own_diagonal = own_list[:, 0] == own_list[:, 1]
    own_lower = in_tile[None, :] <= own_rows[:, None]
    own_keep = jnp.logical_not(own_diagonal[:, None, None] & own_lower[None])
    masked = jnp.where(own_keep[None], amplitudes, nothing)
    all_pairs = gather_directly(pair_list, "pair", 0)
    flat_count = slot_dev * row_dev * tile_width
    mine_masked = masked.reshape(pair_dev, flat_count)
    mine_whole = amplitudes.reshape(pair_dev, flat_count)
    got_masked, got_whole = (
        lax.all_to_all(mine_masked, "pair", split_axis=1, concat_axis=0, tiled=True),
        lax.all_to_all(mine_whole, "pair", split_axis=1, concat_axis=0, tiled=True),
    )
    local_gram = lax.dot_general(
        got_masked, got_whole, (((1,), (1,)), ((), ())), preferred_element_type=jnp.float32
    )
    full_gram = one_axis_at_a_time(local_gram, ("pair", "vir", "sub"))
    p_occ = occ_density(full_gram, all_pairs, all_pairs)
    rows_whole = gather_directly(amplitudes, "sub", 2)
    packed = gather_directly(rows_whole, "vir", 1)
    all_diagonal = tile_list[:, 0] == tile_list[:, 1]
    all_lower = in_tile[None, :] <= in_tile[:, None]
    all_keep = jnp.logical_not(all_diagonal[:, None, None] & all_lower[None])
    packed = jnp.where(all_keep[None], packed, nothing)
    slot_grid = slot_table(tile_list)
    left_ids = own_list[:, 0]
    right_ids = own_list[:, 1]
    virt_part = jnp.zeros((slot_dev, row_dev, tile_width), jnp.float32)
    for column in range(NTV):
        left_block = oriented(packed, slot_grid, left_ids, column)
        left_block = lax.dynamic_slice_in_dim(left_block, sub_at * row_dev, row_dev, 2)
        right_block = oriented(packed, slot_grid, right_ids, column)
        virt_part = virt_part + jnp.einsum(
            "psxz,psyz->sxy", left_block, right_block, preferred_element_type=jnp.float32
        )
    p_virt = total_of_pieces(virt_part, "pair")
    return (p_virt, p_occ)


def solution(mesh):
    in_specs = (P(("groups", "pair"), "vir", "sub", None), P(("groups", "pair"), None), P())
    out_specs = (P(("groups", "vir"), "sub", None), P("groups", None))
    return jax.shard_map(shards, mesh=mesh, in_specs=in_specs, out_specs=out_specs, check_vma=False)
```

profile of v0, /device:TPU:33, one launch (start us, length us, event | category | flops | bytes accessed | tf_op | source)
XLA Modules:
  0.0 348.1 jit_solution(7277669529020630974)
XLA Ops:
  7.2 1.0 broadcast_in_dim.281
  8.1 45.0 %all_to_all.49 = bf16[2,1,9,64,128]{4,3,2,1,0:T(8,128)(2,1)S(1)} all-to-all(bf16[2,1,9,64,128]{4,3,2,1,0:T(8,128)(2,1)S(1)} %broadcast_in_dim.281), channel_id=1, replica_groups=mesh['groups'=2,'pair'=32,'vir'=4,'sub'=2] {'sub'}, dimensions={0} | all-to-all | bytes 589824 | tf_op jit(solution)/shard_map/all_to_all | solution.py:21
  53.2 1.3 broadcast_in_dim.282
  54.5 3.8 %all-to-all-start.1 = ((bf16[4,1,9,128,128]{4,3,2,1,0:T(8,128)(2,1)}), bf16[4,1,9,128,128]{4,3,2,1,0:T(8,128)(2,1)S(1)}, u32[]{:S(2)}, u32[]{:S(2)}) async-start(bf16[4,1,9,128,128]{4,3,2,1,0:T(8,128)(2,1)} %broadcast_in_dim.282), calls=%async_computation.1 | async-start | bytes 2359296 | tf_op jit(solution)/shard_map/all_to_all | solution.py:21
  60.8 0.7 gather_fusion.6
  61.5 0.7 gather_fusion.8
  62.2 0.7 gather_fusion.10
  62.9 0.7 gather_fusion.12
  63.6 0.7 gather_fusion.14
  64.3 0.7 gather_fusion.16
  65.0 0.7 gather_fusion.18
  65.7 0.7 gather_fusion.20
  66.4 0.7 gather_fusion.22
  71.2 3.2 all-to-all-done.1
  75.5 0.9 copy.142
  77.0 0.9 copy.144
  78.5 0.9 copy.146
  80.1 0.9 copy.148
  81.6 0.9 copy.150
  83.1 0.9 copy.152
  84.7 0.9 copy.154
  86.2 0.9 copy.156
  87.7 0.9 copy.158
  89.3 0.9 copy.160
  90.8 0.9 copy.162
  92.3 0.9 copy.164
  93.8 0.9 copy.166
  95.3 0.9 copy.168
  96.8 0.9 copy.170
  98.6 1.1 select_bitcast_fusion.7
  99.7 0.8 select_bitcast_fusion.6
  100.5 0.7 select_bitcast_fusion.5
  106.3 1.0 convolution_add_fusion
  108.0 6.0 %all-to-all-start.2 = ((s32[32,1,2]{2,1,0:T(1,128)}), s32[32,1,2]{2,1,0:T(1,128)S(1)}, u32[]{:S(2)}, u32[]{:S(2)}) async-start(s32[32,1,2]{2,1,0:T(1,128)} %broadcast_in_dim.316), calls=%async_computation.2 | async-start | bytes 32768 | tf_op jit(solution)/shard_map/all_to_all | solution.py:21
  114.8 1.4 reduce.1
  116.2 0.7 reshape.1107
  116.9 17.6 %all-to-all-done.2 = s32[32,1,2]{2,1,0:T(1,128)S(1)} async-done(((s32[32,1,2]{2,1,0:T(1,128)}), s32[32,1,2]{2,1,0:T(1,128)S(1)}, u32[]{:S(2)}, u32[]{:S(2)}) %all-to-all-start.2) | async-done | bytes 288 | tf_op jit(solution)/shard_map/all_to_all | solution.py:21
  134.5 5.0 %all-to-all-start.3 = ((bf16[32,2,1152]{2,1,0:T(2,128)(2,1)}), bf16[32,2,1152]{2,1,0:T(2,128)(2,1)S(1)}, u32[]{:S(2)}, u32[]{:S(2)}) async-start(bf16[32,2,1152]{2,1,0:T(2,128)(2,1)} %reshape.1107), calls=%async_computation.3 | async-start | bytes 294912 | tf_op jit(solution)/shard_map/all_to_all | solution.py:99
  139.5 1.4 reduce
  141.0 0.7 reshape.1105
  141.7 28.4 %all-to-all-done.3 = bf16[32,2,1152]{2,1,0:T(2,128)(2,1)S(1)} async-done(((bf16[32,2,1152]{2,1,0:T(2,128)(2,1)}), bf16[32,2,1152]{2,1,0:T(2,128)(2,1)S(1)}, u32[]{:S(2)}, u32[]{:S(2)}) %all-to-all-start.3) | async-done | bytes 147488 | tf_op jit(solution)/shard_map/all_to_all | solution.py:99
  170.0 5.1 %all-to-all-start.4 = ((bf16[32,2,1152]{2,1,0:T(2,128)(2,1)}), bf16[32,2,1152]{2,1,0:T(2,128)(2,1)S(1)}, u32[]{:S(2)}, u32[]{:S(2)}) async-start(bf16[32,2,1152]{2,1,0:T(2,128)(2,1)} %reshape.1105), calls=%async_computation.4 | async-start | bytes 294912 | tf_op jit(solution)/shard_map/all_to_all | solution.py:100
  175.4 29.6 %all-to-all-done.4 = bf16[32,2,1152]{2,1,0:T(2,128)(2,1)S(1)} async-done(((bf16[32,2,1152]{2,1,0:T(2,128)(2,1)}), bf16[32,2,1152]{2,1,0:T(2,128)(2,1)S(1)}, u32[]{:S(2)}, u32[]{:S(2)}) %all-to-all-start.4) | async-done | bytes 147488 | tf_op jit(solution)/shard_map/all_to_all | solution.py:100
  205.3 83.8 %psum.21 = f32[32,32]{1,0:T(8,128)S(1)} all-reduce(f32[32,32]{1,0:T(8,128)S(1)} %fusion.66), channel_id=1, replica_groups=mesh['groups'=2,'pair'=32,'vir'=4,'sub'=2] {'pair'}, use_global_device_ids=true, to_apply=%region_2.3 | all-reduce | flops 1024 | bytes 8192 | tf_op jit(solution)/shard_map/psum | solution.py:29
  289.0 11.3 %psum.22 = f32[32,32]{1,0:T(8,128)S(1)} all-reduce(f32[32,32]{1,0:T(8,128)S(1)} %psum.21), channel_id=1, replica_groups=mesh['groups'=2,'pair'=32,'vir'=4,'sub'=2] {'vir'}, use_global_device_ids=true, to_apply=%region_3.4 | all-reduce | flops 1024 | bytes 8192 | tf_op jit(solution)/shard_map/psum | solution.py:29
  300.3 34.3 %psum.23 = f32[32,32]{1,0:T(8,128)S(1)} all-reduce(f32[32,32]{1,0:T(8,128)S(1)} %psum.22), channel_id=1, replica_groups=mesh['groups'=2,'pair'=32,'vir'=4,'sub'=2] {'sub'}, use_global_device_ids=true, to_apply=%region_4.5 | all-reduce | flops 1024 | bytes 8192 | tf_op jit(solution)/shard_map/psum | solution.py:29
  335.0 1.1 convolution_negate_fusion
  336.1 5.1 %reduce_sum.19 = f32[9,64,128]{2,1,0:T(8,128)} reduce(f32[32,9,64,128]{3,2,1,0:T(8,128)} %bitcast.349, f32[]{:T(128)} %constant.8.clone.1), dimensions={0}, to_apply=%region_1.2 | reduce | flops 2285568 | bytes 9732100 | tf_op jit(solution)/shard_map/reduce_sum | solution.py:34
  (221 shorter events, 24.0 us)
Async XLA Ops:
  54.5 3.8 %copy-start.31 = (s32[36,2]{0,1:T(2,128)S(1)}, s32[36,2]{0,1:T(2,128)}, u32[]{:S(2)}) copy-start(s32[36,2]{0,1:T(2,128)} %param.5) | copy-start | bytes 868
  54.5 19.9 %all-to-all-start.1 = ((bf16[4,1,9,128,128]{4,3,2,1,0:T(8,128)(2,1)}), bf16[4,1,9,128,128]{4,3,2,1,0:T(8,128)(2,1)S(1)}, u32[]{:S(2)}, u32[]{:S(2)}) async-start(bf16[4,1,9,128,128]{4,3,2,1,0:T(8,128)(2,1)} %broadcast_in_dim.282), calls=%async_computation.1 | async-start | bytes 2359296 | tf_op jit(solution)/shard_map/all_to_all | solution.py:21
  58.3 277.8 %all-gather.3.cloned.1.call-start = ((), (), s32[]{:S(2)}) async-start(), calls=%async_computation.5 | async-start | bytes 9732096 | tf_op jit(solution)/shard_map/all_gather | solution.py:33
  75.5 1.5 copy-start.11
  77.0 1.5 copy-start.15
  78.5 1.5 copy-start.9
  80.1 1.5 copy-start.13
  81.6 1.6 copy-start.5
  83.1 1.6 copy-start.7
  84.7 3.1 copy-start.1
  86.2 3.1 copy-start.3
  98.3 1.4 copy-start.17
  98.3 2.2 copy-start.18
  98.3 2.9 copy-start.19
  98.6 2.7 copy-start.34
  98.6 2.8 copy-start.20
  98.6 2.8 copy-start.33
  99.7 1.9 copy-start.21
  99.7 1.9 copy-start.32
  100.5 1.1 copy-start.22
  101.4 1.1 copy-start.16
  101.4 1.2 copy-start.30
  101.4 1.2 copy-start.55
  101.5 1.1 copy-start.56
  101.5 1.1 copy-start.57
  101.7 1.4 copy-start.10
  101.7 1.3 copy-start.14
  101.7 1.4 copy-start.29
  101.7 1.4 copy-start.52
  101.7 1.4 copy-start.53
  101.7 1.4 copy-start.59
  102.6 1.1 copy-start.8
  102.6 1.2 copy-start.28
  102.6 1.2 copy-start.49
  102.6 1.2 copy-start.50
  102.6 1.2 copy-start.58
  103.1 1.2 copy-start.2
  103.1 1.1 copy-start.4
  103.1 1.2 copy-start.27
  103.1 1.2 copy-start.46
  103.1 1.2 copy-start.47
  103.2 1.2 copy-start.54
  106.2 1.1 copy-start.35
  106.2 7.8 %copy-start = (bf16[1,9,64,128]{3,2,1,0:T(8,128)(2,1)S(1)}, bf16[1,9,64,128]{3,2,1,0:T(8,128)(2,1)}, u32[]{:S(2)}) copy-start(bf16[1,9,64,128]{3,2,1,0:T(8,128)(2,1)} %param.3) | copy-start | bytes 442372
  108.0 26.5 %all-to-all-start.2 = ((s32[32,1,2]{2,1,0:T(1,128)}), s32[32,1,2]{2,1,0:T(1,128)S(1)}, u32[]{:S(2)}, u32[]{:S(2)}) async-start(s32[32,1,2]{2,1,0:T(1,128)} %broadcast_in_dim.316), calls=%async_computation.2 | async-start | bytes 32768 | tf_op jit(solution)/shard_map/all_to_all | solution.py:21
  134.5 35.5 %all-to-all-start.3 = ((bf16[32,2,1152]{2,1,0:T(2,128)(2,1)}), bf16[32,2,1152]{2,1,0:T(2,128)(2,1)S(1)}, u32[]{:S(2)}, u32[]{:S(2)}) async-start(bf16[32,2,1152]{2,1,0:T(2,128)(2,1)} %reshape.1107), calls=%async_computation.3 | async-start | bytes 294912 | tf_op jit(solution)/shard_map/all_to_all | solution.py:99
  140.9 193.8 %copy-start.60 = (f32[64]{0:T(128)S(1)}, f32[64]{0:T(128)}, u32[]{:S(2)}) copy-start(f32[64]{0:T(128)} %constant.9.clone.1) | copy-start | bytes 772
  170.0 35.0 %all-to-all-start.4 = ((bf16[32,2,1152]{2,1,0:T(2,128)(2,1)}), bf16[32,2,1152]{2,1,0:T(2,128)(2,1)S(1)}, u32[]{:S(2)}, u32[]{:S(2)}) async-start(bf16[32,2,1152]{2,1,0:T(2,128)(2,1)} %reshape.1105), calls=%async_computation.4 | async-start | bytes 294912 | tf_op jit(solution)/shard_map/all_to_all | solution.py:100
  (18 other events, 17.7 us)
Sparse Core Ops, SparseCore 0:
  107.5 146.7 all-gather.2
where the time goes:
time: 349 us; the launch traced here: 348 us
  blocking collectives  174 us (50%)
  waiting for transfers between devices  78.8 us (23%)
  local copies, waits for them, and re-layouts  41 us (12%)
  starting transfers between devices  19.9 us (6%)
  between operations  15.2 us (4%)
  other arithmetic  13.5 us (4%)
  matrix products  5.32 us (2%)
    psum x3, blocking collectives, one_axis_at_a_time(): return functools.reduce(lax.psum, axes, array)  129 us
    all_to_all x1, blocking collectives, sent_to_all(): return lax.all_to_all(copies, axis, split_axis=0, concat_axis=0, tiled=True)  45 us
    gather x48, local copies, waits for them, and re-layouts, oriented(): gathered = packed[:, slot_grid[tile_ids, column]]  34.2 us
    all_to_all x1, waiting for transfers between devices, shards(): lax.all_to_all(mine_whole, 'pair', split_axis=1, concat_axis=0, tiled=True)  29.6 us
    all_to_all x1, waiting for transfers between devices, shards(): lax.all_to_all(mine_masked, 'pair', split_axis=1, concat_axis=0, tiled=True)  28.4 us
    all_to_all x2, waiting for transfers between devices, sent_to_all(): return lax.all_to_all(copies, axis, split_axis=0, concat_axis=0, tiled=True)  20.8 us
    all_to_all x2, starting transfers between devices, sent_to_all(): return lax.all_to_all(copies, axis, split_axis=0, concat_axis=0, tiled=True)  9.72 us
  transfers between devices with their start and end apart: 5, of which 4 were waited for; matrix products, arithmetic and copies ran while one was open for 6% of the time, Pallas kernels for 0%

commit v1 on v0

v1 whole, which is shorter than its diff:
```python
import functools

import jax
import jax.numpy as jnp
from jax import lax
from jax.experimental import pallas as pl
from jax.experimental.pallas import tpu as pltpu
from jax.sharding import Mesh
from jax.sharding import PartitionSpec as P

OCC = 256
NTV = 8
NEAR = 8


def sent_to_all(array, axis):
    copies = jnp.broadcast_to(array, (lax.axis_size(axis), *array.shape))
    return lax.all_to_all(copies, axis, split_axis=0, concat_axis=0, tiled=True)


def occurrences(pair_rows):
    orbital = jnp.concatenate([pair_rows[:, 0], pair_rows[:, 1]])
    partner = jnp.concatenate([pair_rows[:, 1], pair_rows[:, 0]])
    pair_count = pair_rows.shape[0]
    parity = jnp.concatenate(
        [jnp.ones((pair_count,), jnp.float32), -jnp.ones((pair_count,), jnp.float32)]
    )
    return (orbital, partner, parity)


def occ_density(pair_gram, pairs):
    orb, partner, sign = occurrences(pairs)
    doubled = jnp.tile(pair_gram, (2, 2))
    couple = jnp.where(
        partner[:, None] == partner[None, :], sign[:, None] * sign[None, :] * doubled, 0.0
    )
    orbitals = jnp.arange(OCC, dtype=jnp.int32)
    hot = (orb[:, None] == orbitals[None, :]).astype(jnp.float32)
    inner_sum = jnp.dot(couple, hot, precision=lax.Precision.HIGHEST)
    return -jnp.dot(hot.T, inner_sum, precision=lax.Precision.HIGHEST)


def virt_kernel(tiles_ref, place_ref, packed_ref, out_ref, whole_ref, slot_ref):
    slot_count, width, _ = packed_ref.shape
    own_count, own_rows, _ = out_ref.shape

    def note(s, carry):
        slot_ref[tiles_ref[s, 0] * NTV + tiles_ref[s, 1]] = s
        return carry

    lax.fori_loop(0, slot_count, note, 0)
    for r in range(NTV):
        for c in range(r, NTV):
            tile = packed_ref[slot_ref[r * NTV + c]]
            turned = tile.T
            if r == c:
                whole_ref[r, :, c * width : (c + 1) * width] = tile - turned
            else:
                whole_ref[r, :, c * width : (c + 1) * width] = tile
                whole_ref[c, :, r * width : (r + 1) * width] = -turned
    first = place_ref[0]
    half = place_ref[1]
    for i in range(own_count):
        left = whole_ref[tiles_ref[first + i, 0], pl.ds(half * own_rows, own_rows), :]
        right = whole_ref[tiles_ref[first + i, 1]]
        out_ref[i] = lax.dot_general(
            left, right, (((1,), (1,)), ((), ())), preferred_element_type=jnp.float32
        )


def virt_partial(tile_list, place, packed, own_count, own_rows):
    width = packed.shape[2]
    smem = pl.BlockSpec(memory_space=pltpu.SMEM)
    vmem = pl.BlockSpec(memory_space=pltpu.VMEM)
    return pl.pallas_call(
        virt_kernel,
        out_shape=jax.ShapeDtypeStruct((own_count, own_rows, width), jnp.float32),
        in_specs=[smem, smem, vmem],
        out_specs=vmem,
        scratch_shapes=[
            pltpu.VMEM((NTV, width, NTV * width), jnp.bfloat16),
            pltpu.SMEM((NTV * NTV,), jnp.int32),
        ],
        compiler_params=pltpu.CompilerParams(vmem_limit_bytes=24 * 1024 * 1024),
        name="virt_partial",
    )(tile_list, place, packed)


def shards(amplitudes, pair_list, tile_list):
    _, slot_dev, row_dev, width = amplitudes.shape
    far = lax.axis_size("far")
    near = lax.axis_size("near")
    pair_count = far * near
    vir_at = lax.axis_index("vir")
    sub_at = lax.axis_index("sub")
    in_tile = jnp.arange(width, dtype=jnp.int32)
    own_list = lax.dynamic_slice_in_dim(tile_list, vir_at * slot_dev, slot_dev, 0)
    own_rows = sub_at * row_dev + jnp.arange(row_dev, dtype=jnp.int32)
    own_lower = in_tile[None, :] <= own_rows[:, None]
    own_diagonal = own_list[:, 0] == own_list[:, 1]
    keep = jnp.logical_not(own_diagonal[:, None, None] & own_lower[None])
    masked = jnp.where(keep, amplitudes[0], jnp.zeros((), jnp.bfloat16))

    other = lax.ppermute(masked, "sub", [(0, 1), (1, 0)])
    is_first = sub_at == 0
    tiles = jnp.concatenate(
        [jnp.where(is_first, masked, other), jnp.where(is_first, other, masked)], axis=1
    )
    packed = sent_to_all(tiles, "vir").reshape(-1, width, width)

    chunk = slot_dev * row_dev * width // pair_count
    share = masked.reshape(pair_count, chunk // width, width)
    ids = jnp.pad(pair_list.astype(jnp.bfloat16), ((0, 0), (0, width - 2)))
    ids = jnp.broadcast_to(ids[None], (pair_count, 1, width))
    got = lax.all_to_all(
        jnp.concatenate([share, ids], axis=1), ("far", "near"), split_axis=0, concat_axis=0, tiled=True
    )
    pairs = got[:, -1, :2].astype(jnp.int32)
    rows = got[:, :-1].reshape(pair_count, chunk)
    local_gram = lax.dot_general(
        rows, rows, (((1,), (1,)), ((), ())), preferred_element_type=jnp.float32
    )
    gram_rows = local_gram.reshape(-1, width)

    place = jnp.stack([vir_at * slot_dev, sub_at]).astype(jnp.int32)
    part = virt_partial(tile_list, place, packed, slot_dev, row_dev)
    part = part.reshape(near, slot_dev * row_dev // near, width)
    gram_copies = jnp.broadcast_to(gram_rows, (near, *gram_rows.shape))
    near_parts = lax.all_to_all(
        jnp.concatenate([part, gram_copies], axis=1), "near", split_axis=0, concat_axis=0, tiled=True
    )
    near_sum = near_parts.sum(axis=0)
    total = sent_to_all(near_sum, "far").sum(axis=0)
    virt_rows = total[: -gram_rows.shape[0]]
    p_virt = sent_to_all(virt_rows, "near").reshape(slot_dev, row_dev, width)
    gram = lax.psum(total[-gram_rows.shape[0] :], ("vir", "sub")).reshape(pair_count, pair_count)
    return (p_virt, occ_density(gram, pairs))


def solution(mesh):
    groups, pair, vir, sub = (mesh.shape[name] for name in ("groups", "pair", "vir", "sub"))
    split = Mesh(
        mesh.devices.reshape(groups, pair // NEAR, NEAR, vir, sub),
        ("groups", "far", "near", "vir", "sub"),
    )
    in_specs = (
        P(("groups", "far", "near"), "vir", "sub", None),
        P(("groups", "far", "near"), None),
        P(),
    )
    out_specs = (P(("groups", "vir"), "sub", None), P("groups", None))
    return jax.shard_map(shards, mesh=split, in_specs=in_specs, out_specs=out_specs, check_vma=False)
```

time: 349 us -> 205 us (0.59)
  blocking collectives: 174 us -> 76 us
  starting transfers between devices: 19.9 us -> 67.3 us
  local copies, waits for them, and re-layouts: 41 us -> 4.37 us
  waiting for transfers between devices: 78.8 us -> 46.6 us
  between operations: 15.2 us -> 0.84 us
  other arithmetic: 13.5 us -> 3.35 us
  matrix products: 5.32 us -> 1.48 us
    psum x3 -> x1, blocking collectives: 129 us -> 22.3 us  [shards(): lax.psum(total[-gram_rows.shape[0]:], ('vir', 'sub'))]
    ppermute x0 -> x1, starting transfers between devices: none -> 43.4 us  [shards(): other = lax.ppermute(masked, 'sub', [(0, 1), (1, 0)])]
    gather x48 -> x0, local copies, waits for them, and re-layouts: 34.2 us -> none  [oriented(): gathered = packed[:, slot_grid[tile_ids, column]]]
    all_to_all x2 -> x1, waiting for transfers between devices: 57.9 us -> 30.8 us  [shards(): lax.all_to_all(jnp.concatenate([share, ids], axis=1), ('far', 'near'), sp...]
    all_to_all x0 -> x1, blocking collectives: none -> 20 us  [shards(): lax.all_to_all(jnp.concatenate([part, gram_copies], axis=1), 'near', spli...]
    all_to_all x1, blocking collectives: 45 us -> 33.8 us  [sent_to_all(): return lax.all_to_all(copies, axis, split_axis=0, concat_axis=0, tiled=True)]
    all_to_all x2, starting transfers between devices: 9.72 us -> 18 us  [sent_to_all(): return lax.all_to_all(copies, axis, split_axis=0, concat_axis=0, tiled=True)]
    all_to_all x2, waiting for transfers between devices: 20.8 us -> 14.8 us  [sent_to_all(): return lax.all_to_all(copies, axis, split_axis=0, concat_axis=0, tiled=True)]
  transfers between devices with their start and end apart: 5 -> 4, of which waited for: 4 -> 3; matrix products, arithmetic and copies ran while one was open for 6% -> 2% of each run, Pallas kernels for 0% -> 1%
where the time goes in v1:
time: 205 us; the launch traced here: 203 us
  blocking collectives  76 us (37%)
  starting transfers between devices  67.3 us (33%)
  waiting for transfers between devices  46.6 us (23%)
  local copies, waits for them, and re-layouts  4.37 us (2%)
  other arithmetic  3.35 us (2%)
  Pallas kernels  2.64 us (1%)
    ppermute x1, starting transfers between devices, shards(): other = lax.ppermute(masked, 'sub', [(0, 1), (1, 0)])  43.4 us
    all_to_all x1, blocking collectives, sent_to_all(): return lax.all_to_all(copies, axis, split_axis=0, concat_axis=0, tiled=True)  33.8 us
    all_to_all x1, waiting for transfers between devices, shards(): lax.all_to_all(jnp.concatenate([share, ids], axis=1), ('far', 'near'), sp...  30.8 us
    psum x1, blocking collectives, shards(): lax.psum(total[-gram_rows.shape[0]:], ('vir', 'sub'))  22.3 us
    all_to_all x1, blocking collectives, shards(): lax.all_to_all(jnp.concatenate([part, gram_copies], axis=1), 'near', spli...  20 us
    all_to_all x2, starting transfers between devices, sent_to_all(): return lax.all_to_all(copies, axis, split_axis=0, concat_axis=0, tiled=True)  18 us
    all_to_all x2, waiting for transfers between devices, sent_to_all(): return lax.all_to_all(copies, axis, split_axis=0, concat_axis=0, tiled=True)  14.8 us
    all_to_all x1, starting transfers between devices, shards(): lax.all_to_all(jnp.concatenate([share, ids], axis=1), ('far', 'near'), sp...  5.97 us
  transfers between devices with their start and end apart: 4, of which 3 were waited for; matrix products, arithmetic and copies ran while one was open for 2% of the time, Pallas kernels for 1%

profile of v1, /device:TPU:33, one launch (start us, length us, event | category | flops | bytes accessed | tf_op | source)
XLA Modules:
  0.0 202.7 jit_solution(16752800920438019736)
XLA Ops:
  0.6 0.8 constant_dynamic-slice_fusion
  1.4 0.1 iota_compare_fusion.3
  1.5 1.0 and_select_fusion.1
  2.5 43.4 %collective-permute-start = (bf16[9,64,128]{2,1,0:T(8,128)(2,1)S(1)}, bf16[9,64,128]{2,1,0:T(8,128)(2,1)S(1)}, u32[]{:S(2)}, u32[]{:S(2)}) collective-permute-start(bf16[9,64,128]{2,1,0:T(8,128)(2,1)S(1)} %and_select_fusion.1), channel_id=1, source_target_pairs={{0,1},{1,0},{2,3},{3,2},{4,5},{5,4},{6,7},{7,6},{8,9},{9,8},{10,11... | collective-permute-start | bytes 442376 | tf_op jit(solution)/shard_map/ppermute | solution.py:104
  45.9 1.0 collective-permute-done
  46.9 1.1 broadcast_select_fusion.1
  48.0 1.3 broadcast_in_dim.39
  49.3 0.0 copy-start
  49.3 0.0 copy-start.2
  49.3 3.8 %all-to-all-start = ((bf16[4,9,128,128]{3,2,1,0:T(8,128)(2,1)}), bf16[4,9,128,128]{3,2,1,0:T(8,128)(2,1)S(1)}, u32[]{:S(2)}, u32[]{:S(2)}) async-start(bf16[4,9,128,128]{3,2,1,0:T(8,128)(2,1)} %broadcast_in_dim.39), calls=%async_computation | async-start | bytes 2359296 | tf_op jit(solution)/shard_map/all_to_all | solution.py:18
  53.0 0.0 copy-done
  53.0 0.0 copy-start.1
  53.1 0.1 and.29
  53.2 0.1 and.30
  53.3 0.1 and.32
  53.4 0.0 copy-done.2
  53.4 0.2 and_select_fusion
  53.6 0.7 pad_maximum_fusion.2
  54.4 14.8 %all-to-all-done = bf16[4,9,128,128]{3,2,1,0:T(8,128)(2,1)S(1)} async-done(((bf16[4,9,128,128]{3,2,1,0:T(8,128)(2,1)}), bf16[4,9,128,128]{3,2,1,0:T(8,128)(2,1)S(1)}, u32[]{:S(2)}, u32[]{:S(2)}) %all-to-all-start) | async-done | bytes 1179680 | tf_op jit(solution)/shard_map/all_to_all | solution.py:18
  69.2 6.0 %all-to-all-start.1 = ((bf16[32,19,128]{2,1,0:T(8,128)(2,1)}), bf16[32,19,128]{2,1,0:T(8,128)(2,1)S(1)}, u32[]{:S(2)}, u32[]{:S(2)}) async-start(bf16[32,19,128]{2,1,0:T(8,128)(2,1)} %pad_maximum_fusion.2), calls=%async_computation.1 | async-start | bytes 393216 | tf_op jit(solution)/shard_map/all_to_all | solution.py:115
  75.2 0.0 copy-done.1
  75.2 0.1 copy.18.tiles_ref
  75.3 0.1 pad_add_fusion.place_ref
  75.3 2.6 %virt_partial.1 = f32[9,64,128]{2,1,0:T(8,128)S(1)} custom-call(s32[36,2]{1,0:T(8,128)S(1)} %copy.18.tiles_ref, s32[2]{0:T(128)S(1)} %pad_add_fusion.place_ref, bf16[36,128,128]{2,1,0:T(8,128)(2,1)S(1)} %bitcast.26), custom_call_target="tpu_custom_call" | custom-call | tf_op jit(solution)/shard_map/virt_partial/pallas_call | solution.py:75
  78.0 30.8 %all-to-all-done.1 = bf16[32,19,128]{2,1,0:T(8,128)(2,1)S(1)} async-done(((bf16[32,19,128]{2,1,0:T(8,128)(2,1)}), bf16[32,19,128]{2,1,0:T(8,128)(2,1)S(1)}, u32[]{:S(2)}, u32[]{:S(2)}) %all-to-all-start.1) | async-done | bytes 155680 | tf_op jit(solution)/shard_map/all_to_all | solution.py:115
  108.8 0.1 convolution_bitcast_fusion
  109.0 0.1 reshape.65
  109.1 20.0 %all_to_all.25 = f32[8,80,128]{2,1,0:T(8,128)S(1)} all-to-all(f32[8,80,128]{2,1,0:T(8,128)S(1)} %pad_maximum_fusion), channel_id=1, replica_groups=mesh['groups'=2,'far'=4,'near'=8,'vir'=4,'sub'=2] {'near'}, dimensions={0} | all-to-all | bytes 655360 | tf_op jit(solution)/shard_map/all_to_all | solution.py:129
  129.1 0.0 copy-start.3
  129.1 33.8 %all_to_all.26 = f32[4,80,128]{2,1,0:T(8,128)S(1)} all-to-all(f32[4,80,128]{2,1,0:T(8,128)S(1)} %broadcast_in_dim.44), channel_id=1, replica_groups=mesh['groups'=2,'far'=4,'near'=8,'vir'=4,'sub'=2] {'far'}, dimensions={0} | all-to-all | bytes 327680 | tf_op jit(solution)/shard_map/all_to_all | solution.py:18
  162.9 0.7 broadcast_in_dim.45
  163.7 14.2 %all-to-all-start.4 = ((f32[8,72,128]{2,1,0:T(8,128)}), f32[8,72,128]{2,1,0:T(8,128)S(1)}, u32[]{:S(2)}, u32[]{:S(2)}) async-start(f32[8,72,128]{2,1,0:T(8,128)} %broadcast_in_dim.45), calls=%async_computation.4 | async-start | bytes 589824 | tf_op jit(solution)/shard_map/all_to_all | solution.py:18
  177.9 0.1 copy.22
  178.0 0.1 pad_add_fusion.2
  178.1 0.1 tile.10
  178.2 22.3 %psum.7 = f32[32,32]{1,0:T(8,128)S(1)} all-reduce(f32[32,32]{1,0:T(8,128)S(1)} %tile.10), channel_id=1, replica_groups=mesh['groups'=2,'far'=4,'near'=8,'vir'=4,'sub'=2] {'vir','sub'}, use_global_device_ids=true, to_apply=%region_2.3 | all-reduce | flops 1024 | bytes 8192 | tf_op jit(solution)/shard_map/psum | solution.py:136
  200.5 0.1 tile.12
  200.6 0.0 copy-done.3
  200.6 0.2 fusion.1
  200.9 1.1 convolution_negate_fusion
  202.0 0.0 all-to-all-done.4
  202.0 0.7 copy.26
  (19 shorter events, 0.3 us)
Async XLA Ops:
  2.5 44.4 %collective-permute-start = (bf16[9,64,128]{2,1,0:T(8,128)(2,1)S(1)}, bf16[9,64,128]{2,1,0:T(8,128)(2,1)S(1)}, u32[]{:S(2)}, u32[]{:S(2)}) collective-permute-start(bf16[9,64,128]{2,1,0:T(8,128)(2,1)S(1)} %and_select_fusion.1), channel_id=1, source_target_pairs={{0,1},{1,0},{2,3},{3,2},{4,5},{5,4},{6,7},{7,6},{8,9},{9,8},{10,11... | collective-permute-start | bytes 442376 | tf_op jit(solution)/shard_map/ppermute | solution.py:104
  49.3 3.8 %copy-start = (bf16[1,9,64,128]{3,2,1,0:T(8,128)(2,1)S(1)}, bf16[1,9,64,128]{3,2,1,0:T(8,128)(2,1)}, u32[]{:S(2)}) copy-start(bf16[1,9,64,128]{3,2,1,0:T(8,128)(2,1)} %param.3) | copy-start | bytes 442372
  49.3 4.1 %copy-start.2 = (s32[1,2]{1,0:T(1,128)S(1)}, s32[1,2]{1,0:T(1,128)}, u32[]{:S(2)}) copy-start(s32[1,2]{1,0:T(1,128)} %param.4) | copy-start | bytes 28
  49.3 19.9 %all-to-all-start = ((bf16[4,9,128,128]{3,2,1,0:T(8,128)(2,1)}), bf16[4,9,128,128]{3,2,1,0:T(8,128)(2,1)S(1)}, u32[]{:S(2)}, u32[]{:S(2)}) async-start(bf16[4,9,128,128]{3,2,1,0:T(8,128)(2,1)} %broadcast_in_dim.39), calls=%async_computation | async-start | bytes 2359296 | tf_op jit(solution)/shard_map/all_to_all | solution.py:18
  53.0 22.1 %copy-start.1 = (s32[36,2]{0,1:T(2,128)S(1)}, s32[36,2]{0,1:T(2,128)}, u32[]{:S(2)}) copy-start(s32[36,2]{0,1:T(2,128)} %param.5) | copy-start | bytes 868
  69.2 39.6 %all-to-all-start.1 = ((bf16[32,19,128]{2,1,0:T(8,128)(2,1)}), bf16[32,19,128]{2,1,0:T(8,128)(2,1)S(1)}, u32[]{:S(2)}, u32[]{:S(2)}) async-start(bf16[32,19,128]{2,1,0:T(8,128)(2,1)} %pad_maximum_fusion.2), calls=%async_computation.1 | async-start | bytes 393216 | tf_op jit(solution)/shard_map/all_to_all | solution.py:115
  129.1 71.5 %copy-start.3 = (f32[64]{0:T(128)S(1)}, f32[64]{0:T(128)}, u32[]{:S(2)}) copy-start(f32[64]{0:T(128)} %constant.25.clone.1) | copy-start | bytes 772
  163.7 38.3 %all-to-all-start.4 = ((f32[8,72,128]{2,1,0:T(8,128)}), f32[8,72,128]{2,1,0:T(8,128)S(1)}, u32[]{:S(2)}, u32[]{:S(2)}) async-start(f32[8,72,128]{2,1,0:T(8,128)} %broadcast_in_dim.45), calls=%async_computation.4 | async-start | bytes 589824 | tf_op jit(solution)/shard_map/all_to_all | solution.py:18

commit v2 on v1

v2 whole, which is shorter than its diff:
```python
import jax
import jax.numpy as jnp
from jax import lax
from jax.experimental import pallas as pl
from jax.experimental.pallas import tpu as pltpu
from jax.sharding import Mesh
from jax.sharding import PartitionSpec as P


OCC = 256
NTV = 8
NEAR = 8


def sent_to_all(array, axis):
    copies = jnp.broadcast_to(array, (lax.axis_size(axis), *array.shape))
    return lax.all_to_all(copies, axis, split_axis=0, concat_axis=0, tiled=True)


def occurrences(pair_rows):
    orbital = jnp.concatenate([pair_rows[:, 0], pair_rows[:, 1]])
    partner = jnp.concatenate([pair_rows[:, 1], pair_rows[:, 0]])
    pair_count = pair_rows.shape[0]
    parity = jnp.concatenate(
        [jnp.ones((pair_count,), jnp.float32), -jnp.ones((pair_count,), jnp.float32)]
    )
    return (orbital, partner, parity)


def occ_density(pair_gram, pairs):
    orb, partner, sign = occurrences(pairs)
    doubled = jnp.tile(pair_gram, (2, 2))
    couple = jnp.where(
        partner[:, None] == partner[None, :], sign[:, None] * sign[None, :] * doubled, 0.0
    )
    orbitals = jnp.arange(OCC, dtype=jnp.int32)
    hot = (orb[:, None] == orbitals[None, :]).astype(jnp.float32)
    inner_sum = jnp.dot(couple, hot, precision=lax.Precision.HIGHEST)
    return -jnp.dot(hot.T, inner_sum, precision=lax.Precision.HIGHEST)


def virt_kernel(tiles_ref, place_ref, own_ref, other_ref, out_ref, whole_ref, slot_ref):
    slot_count, half_rows, width = own_ref.shape
    own_count = out_ref.shape[0]
    first = place_ref[0]
    half = place_ref[1]

    def note(s, carry):
        slot_ref[tiles_ref[s, 0] * NTV + tiles_ref[s, 1]] = s
        return carry

    lax.fori_loop(0, slot_count, note, 0)
    is_first = half == 0
    for r in range(NTV):
        for c in range(r, NTV):
            slot = slot_ref[r * NTV + c]
            mine = own_ref[slot]
            theirs = other_ref[slot]
            tile = jnp.concatenate(
                [jnp.where(is_first, mine, theirs), jnp.where(is_first, theirs, mine)], axis=0
            )
            turned = tile.T
            if r == c:
                whole_ref[r, :, c * width : (c + 1) * width] = tile - turned
            else:
                whole_ref[r, :, c * width : (c + 1) * width] = tile
                whole_ref[c, :, r * width : (r + 1) * width] = -turned
    for i in range(own_count):
        left = whole_ref[tiles_ref[first + i, 0], pl.ds(half * half_rows, half_rows), :]
        right = whole_ref[tiles_ref[first + i, 1]]
        out_ref[i] = lax.dot_general(
            left, right, (((1,), (1,)), ((), ())), preferred_element_type=jnp.float32
        )


def virt_partial(tile_list, place, own, other, own_count):
    _, half_rows, width = own.shape
    smem = pl.BlockSpec(memory_space=pltpu.SMEM)
    vmem = pl.BlockSpec(memory_space=pltpu.VMEM)
    return pl.pallas_call(
        virt_kernel,
        out_shape=jax.ShapeDtypeStruct((own_count, half_rows, width), jnp.float32),
        in_specs=[smem, smem, vmem, vmem],
        out_specs=vmem,
        scratch_shapes=[
            pltpu.VMEM((NTV, width, NTV * width), jnp.bfloat16),
            pltpu.SMEM((NTV * NTV,), jnp.int32),
        ],
        compiler_params=pltpu.CompilerParams(vmem_limit_bytes=24 * 1024 * 1024),
        name="virt_partial",
    )(tile_list, place, own, other)


def shards(amplitudes, pair_list, tile_list):
    _, slot_dev, row_dev, width = amplitudes.shape
    far = lax.axis_size("far")
    near = lax.axis_size("near")
    pair_count = far * near
    vir_at = lax.axis_index("vir")
    sub_at = lax.axis_index("sub")
    in_tile = jnp.arange(width, dtype=jnp.int32)
    own_list = lax.dynamic_slice_in_dim(tile_list, vir_at * slot_dev, slot_dev, 0)
    own_rows = sub_at * row_dev + jnp.arange(row_dev, dtype=jnp.int32)
    own_lower = in_tile[None, :] <= own_rows[:, None]
    own_diagonal = own_list[:, 0] == own_list[:, 1]
    keep = jnp.logical_not(own_diagonal[:, None, None] & own_lower[None])
    masked = jnp.where(keep, amplitudes[0], jnp.zeros((), jnp.bfloat16))

    share_rows = row_dev // pair_count
    share = masked.reshape(slot_dev, pair_count, share_rows, width)
    share = jnp.transpose(share, (1, 2, 0, 3)).reshape(pair_count, share_rows, slot_dev * width)
    ids = jnp.pad(pair_list.astype(jnp.bfloat16), ((0, share_rows - 1), (0, width - 2)))
    ids = jnp.broadcast_to(ids[None], (pair_count, share_rows, width))
    got = lax.all_to_all(
        jnp.concatenate([share, ids], axis=2),
        ("far", "near"),
        split_axis=0,
        concat_axis=0,
        tiled=True,
    )
    own = lax.all_gather(masked, "vir", axis=0, tiled=True)
    other = lax.ppermute(own, "sub", [(0, 1), (1, 0)])
    place = jnp.stack([vir_at * slot_dev, sub_at]).astype(jnp.int32)
    part = virt_partial(tile_list, place, own, other, slot_dev)
    chunk = slot_dev * row_dev // near
    near_parts = lax.all_to_all(
        part.reshape(near, chunk, width), "near", split_axis=0, concat_axis=0, tiled=True
    )
    near_sum = near_parts.sum(axis=0)

    pairs = got[:, 0, slot_dev * width : slot_dev * width + 2].astype(jnp.int32)
    rows = got[:, :, : slot_dev * width].reshape(pair_count, share_rows * slot_dev * width)
    local_gram = lax.dot_general(
        rows, rows, (((1,), (1,)), ((), ())), preferred_element_type=jnp.float32
    )
    gram_rows = lax.psum(local_gram.reshape(-1, width), ("vir", "sub"))

    total = sent_to_all(jnp.concatenate([near_sum, gram_rows], axis=0), "far").sum(axis=0)
    spread = sent_to_all(total, "near")
    p_virt = spread[:, :chunk].reshape(slot_dev, row_dev, width)
    gram = spread[:, chunk:].sum(axis=0).reshape(pair_count, pair_count)
    return (p_virt, occ_density(gram, pairs))


def solution(mesh):
    groups, pair, vir, sub = (mesh.shape[name] for name in ("groups", "pair", "vir", "sub"))
    split = Mesh(
        mesh.devices.reshape(groups, pair // NEAR, NEAR, vir, sub),
        ("groups", "far", "near", "vir", "sub"),
    )
    in_specs = (
        P(("groups", "far", "near"), "vir", "sub", None),
        P(("groups", "far", "near"), None),
        P(),
    )
    out_specs = (P(("groups", "vir"), "sub", None), P("groups", None))
    return jax.shard_map(shards, mesh=split, in_specs=in_specs, out_specs=out_specs, check_vma=False)
```

time: 205 us -> 175 us (0.85)
  the two profiles are of different devices: /device:TPU:33 before, /device:TPU:40 now
where the time goes in v2:
time: 175 us
  blocking collectives  64.5 us (37%)
  starting transfers between devices  62.3 us (36%)
  waiting for transfers between devices  35.5 us (20%)
  local copies, waits for them, and re-layouts  4.98 us (3%)
  Pallas kernels  3.39 us (2%)
    all_to_all x1, starting transfers between devices, shards(): lax.all_to_all(jnp.concatenate([share, ids], axis=2), ('far', 'near'), sp...  45.9 us
    all_to_all x1, blocking collectives, sent_to_all(): return lax.all_to_all(copies, axis, split_axis=0, concat_axis=0, tiled=True)  37.5 us
    all_to_all x1, waiting for transfers between devices, sent_to_all(): return lax.all_to_all(copies, axis, split_axis=0, concat_axis=0, tiled=True)  18.5 us
    all_gather x1, blocking collectives, shards(): own = lax.all_gather(masked, 'vir', axis=0, tiled=True)  13.6 us
    psum x1, blocking collectives, shards(): gram_rows = lax.psum(local_gram.reshape(-1, width), ('vir', 'sub'))  13.4 us
    all_to_all x1, waiting for transfers between devices, shards(): lax.all_to_all(jnp.concatenate([share, ids], axis=2), ('far', 'near'), sp...  12.6 us
    all_to_all x1, starting transfers between devices, sent_to_all(): return lax.all_to_all(copies, axis, split_axis=0, concat_axis=0, tiled=True)  10.9 us
    all_to_all x1, starting transfers between devices, shards(): lax.all_to_all(part.reshape(near, chunk, width), 'near', split_axis=0, co...  3.63 us
  transfers between devices with their start and end apart: 4, of which 4 were waited for; matrix products, arithmetic and copies ran while one was open for 1% of the time, Pallas kernels for 2%

profile of v2, /device:TPU:40, one launch (start us, length us, event | category | flops | bytes accessed | tf_op | source)
XLA Modules:
  0.0 174.5 jit_solution(7154224281750891398)
XLA Ops:
  0.6 0.0 copy-start.1
  0.6 0.7 copy-done.1
  1.3 0.1 constant_dynamic-slice_fusion
  1.4 0.1 iota_compare_fusion.3
  1.5 1.1 fusion
  2.6 0.0 copy-start.2
  2.6 0.1 reshape.67
  2.7 0.6 copy-done.2
  3.3 0.8 copy.23
  4.1 0.0 copy-start
  4.1 45.9 %all-to-all-start.1 = ((bf16[32,2,1280]{2,1,0:T(2,128)(2,1)}), bf16[32,2,1280]{2,1,0:T(2,128)(2,1)S(1)}, u32[]{:S(2)}, u32[]{:S(2)}) async-start(bf16[32,2,1280]{2,1,0:T(2,128)(2,1)} %copy.23), calls=%async_computation.1 | async-start | bytes 327680 | tf_op jit(solution)/shard_map/all_to_all | solution.py:114
  50.0 0.1 iota_compare_fusion.4
  50.1 0.0 copy-done
  50.1 0.1 and_select_fusion.1
  50.2 13.6 %all_gather.3.own_ref = bf16[36,64,128]{2,1,0:T(8,128)(2,1)S(1)} all-gather(bf16[9,64,128]{2,1,0:T(8,128)(2,1)S(1)} %and_select_fusion.1), channel_id=1, replica_groups=mesh['groups'=2,'far'=4,'near'=8,'vir'=4,'sub'=2] {'vir'}, dimensions={0}, use_global_device_ids=true | all-gather | bytes 737280 | tf_op jit(solution)/shard_map/all_gather | solution.py:121
  63.8 1.9 %collective-permute-start = (bf16[36,64,128]{2,1,0:T(8,128)(2,1)S(1)}, bf16[36,64,128]{2,1,0:T(8,128)(2,1)S(1)}, u32[]{:S(2)}, u32[]{:S(2)}) collective-permute-start(bf16[36,64,128]{2,1,0:T(8,128)(2,1)S(1)} %all_gather.3.own_ref), channel_id=1, source_target_pairs={{0,1},{1,0},{2,3},{3,2},{4,5},{5,4},{6,7},{7,6},{8,9},{9,8},{10,11... | collective-permute-start | bytes 1769480 | tf_op jit(solution)/shard_map/ppermute | solution.py:122
  65.8 0.1 copy.21.tiles_ref
  65.9 0.1 pad_add_fusion.place_ref
  65.9 1.8 %collective-permute-done.other_ref = bf16[36,64,128]{2,1,0:T(8,128)(2,1)S(1)} collective-permute-done((bf16[36,64,128]{2,1,0:T(8,128)(2,1)S(1)}, bf16[36,64,128]{2,1,0:T(8,128)(2,1)S(1)}, u32[]{:S(2)}, u32[]{:S(2)}) %collective-permute-start) | collective-permute-done | bytes 589856 | tf_op jit(solution)/shard_map/ppermute | solution.py:122
  67.7 3.4 %virt_partial.1 = f32[9,64,128]{2,1,0:T(8,128)} custom-call(s32[36,2]{1,0:T(8,128)S(1)} %copy.21.tiles_ref, s32[2]{0:T(128)S(1)} %pad_add_fusion.place_ref, bf16[36,64,128]{2,1,0:T(8,128)(2,1)S(1)} %all_gather.3.own_ref, bf16[36,64,128]{2,1,0:T(8,128)(2,1)S(1)} %collective-permute-done.other_ref), custom_call_target="tpu_custom_call" | custom-call | tf_op jit(solution)/shard_map/virt_partial/pallas_call | solution.py:80
  71.1 12.6 %all-to-all-done.1 = bf16[32,2,1280]{2,1,0:T(2,128)(2,1)S(1)} async-done(((bf16[32,2,1280]{2,1,0:T(2,128)(2,1)}), bf16[32,2,1280]{2,1,0:T(2,128)(2,1)S(1)}, u32[]{:S(2)}, u32[]{:S(2)}) %all-to-all-start.1) | async-done | bytes 163872 | tf_op jit(solution)/shard_map/all_to_all | solution.py:114
  83.7 3.6 %all-to-all-start = ((f32[8,72,128]{2,1,0:T(8,128)}), f32[8,72,128]{2,1,0:T(8,128)S(1)}, u32[]{:S(2)}, u32[]{:S(2)}) async-start(f32[8,72,128]{2,1,0:T(8,128)} %bitcast.4), calls=%async_computation | async-start | bytes 589824 | tf_op jit(solution)/shard_map/all_to_all | solution.py:126
  87.4 0.1 slice.34
  87.5 0.2 convolution_bitcast_fusion
  87.6 0.1 reshape.68
  87.7 13.4 %psum.7 = f32[8,128]{1,0:T(8,128)S(1)} all-reduce(f32[8,128]{1,0:T(8,128)S(1)} %reshape.68), channel_id=1, replica_groups=mesh['groups'=2,'far'=4,'near'=8,'vir'=4,'sub'=2] {'vir','sub'}, use_global_device_ids=true, to_apply=%region_1.2 | all-reduce | flops 1024 | bytes 8192 | tf_op jit(solution)/shard_map/psum | solution.py:136
  101.1 2.6 %all-to-all-done = f32[8,72,128]{2,1,0:T(8,128)S(1)} async-done(((f32[8,72,128]{2,1,0:T(8,128)}), f32[8,72,128]{2,1,0:T(8,128)S(1)}, u32[]{:S(2)}, u32[]{:S(2)}) %all-to-all-start) | async-done | bytes 294944 | tf_op jit(solution)/shard_map/all_to_all | solution.py:126
  103.7 37.5 %all_to_all.20 = f32[4,80,128]{2,1,0:T(8,128)S(1)} all-to-all(f32[4,80,128]{2,1,0:T(8,128)S(1)} %broadcast_in_dim.33), channel_id=1, replica_groups=mesh['groups'=2,'far'=4,'near'=8,'vir'=4,'sub'=2] {'far'}, dimensions={0} | all-to-all | bytes 327680 | tf_op jit(solution)/shard_map/all_to_all | solution.py:17
  141.3 0.7 broadcast_in_dim.34
  142.0 10.9 %all-to-all-start.3 = ((f32[8,80,128]{2,1,0:T(8,128)}), f32[8,80,128]{2,1,0:T(8,128)S(1)}, u32[]{:S(2)}, u32[]{:S(2)}) async-start(f32[8,80,128]{2,1,0:T(8,128)} %broadcast_in_dim.34), calls=%async_computation.3 | async-start | bytes 655360 | tf_op jit(solution)/shard_map/all_to_all | solution.py:17
  152.9 0.1 copy.27
  153.0 0.1 pad_add_fusion.2
  153.1 18.5 %all-to-all-done.3 = f32[8,80,128]{2,1,0:T(8,128)S(1)} async-done(((f32[8,80,128]{2,1,0:T(8,128)}), f32[8,80,128]{2,1,0:T(8,128)S(1)}, u32[]{:S(2)}, u32[]{:S(2)}) %all-to-all-start.3) | async-done | bytes 327712 | tf_op jit(solution)/shard_map/all_to_all | solution.py:17
  171.6 0.1 tile.10
  171.7 0.1 tile.12
  171.8 0.0 copy-start.3
  171.8 0.7 copy-done.3
  172.5 0.2 fusion.2
  172.7 1.1 convolution_negate_fusion
  173.8 0.7 slice.35
  (16 shorter events, 0.2 us)
Async XLA Ops:
  0.6 0.7 copy-start.1
  2.6 0.7 copy-start.2
  4.1 46.0 %copy-start = (bf16[1,9,64,128]{3,2,1,0:T(8,128)(2,1)S(1)}, bf16[1,9,64,128]{3,2,1,0:T(8,128)(2,1)}, u32[]{:S(2)}) copy-start(bf16[1,9,64,128]{3,2,1,0:T(8,128)(2,1)} %param.3) | copy-start | bytes 442372
  4.1 79.6 %all-to-all-start.1 = ((bf16[32,2,1280]{2,1,0:T(2,128)(2,1)}), bf16[32,2,1280]{2,1,0:T(2,128)(2,1)S(1)}, u32[]{:S(2)}, u32[]{:S(2)}) async-start(bf16[32,2,1280]{2,1,0:T(2,128)(2,1)} %copy.23), calls=%async_computation.1 | async-start | bytes 327680 | tf_op jit(solution)/shard_map/all_to_all | solution.py:114
  63.8 3.9 %collective-permute-start = (bf16[36,64,128]{2,1,0:T(8,128)(2,1)S(1)}, bf16[36,64,128]{2,1,0:T(8,128)(2,1)S(1)}, u32[]{:S(2)}, u32[]{:S(2)}) collective-permute-start(bf16[36,64,128]{2,1,0:T(8,128)(2,1)S(1)} %all_gather.3.own_ref), channel_id=1, source_target_pairs={{0,1},{1,0},{2,3},{3,2},{4,5},{5,4},{6,7},{7,6},{8,9},{9,8},{10,11... | collective-permute-start | bytes 1769480 | tf_op jit(solution)/shard_map/ppermute | solution.py:122
  83.7 19.9 %all-to-all-start = ((f32[8,72,128]{2,1,0:T(8,128)}), f32[8,72,128]{2,1,0:T(8,128)S(1)}, u32[]{:S(2)}, u32[]{:S(2)}) async-start(f32[8,72,128]{2,1,0:T(8,128)} %bitcast.4), calls=%async_computation | async-start | bytes 589824 | tf_op jit(solution)/shard_map/all_to_all | solution.py:126
  142.0 29.6 %all-to-all-start.3 = ((f32[8,80,128]{2,1,0:T(8,128)}), f32[8,80,128]{2,1,0:T(8,128)S(1)}, u32[]{:S(2)}, u32[]{:S(2)}) async-start(f32[8,80,128]{2,1,0:T(8,128)} %broadcast_in_dim.34), calls=%async_computation.3 | async-start | bytes 655360 | tf_op jit(solution)/shard_map/all_to_all | solution.py:17
  171.8 0.7 copy-start.3

commit v3 on v2

--- a/solution.py
+++ b/solution.py
@@ -17,26 +17,49 @@
     return lax.all_to_all(copies, axis, split_axis=0, concat_axis=0, tiled=True)
 
 
-def occurrences(pair_rows):
-    orbital = jnp.concatenate([pair_rows[:, 0], pair_rows[:, 1]])
-    partner = jnp.concatenate([pair_rows[:, 1], pair_rows[:, 0]])
-    pair_count = pair_rows.shape[0]
-    parity = jnp.concatenate(
-        [jnp.ones((pair_count,), jnp.float32), -jnp.ones((pair_count,), jnp.float32)]
+def finish_kernel(spread_ref, columns_ref, rows_ref, virt_ref, occ_ref):
+    near, _, width = spread_ref.shape
+    chunk = virt_ref.shape[0] // near
+    pair_count = columns_ref.shape[0]
+    packed = spread_ref[0, chunk:, :]
+    for k in range(1, near):
+        packed = packed + spread_ref[k, chunk:, :]
+    gram = jnp.concatenate(
+        [packed[:, k : k + pair_count] for k in range(0, width, pair_count)], axis=0
     )
-    return (orbital, partner, parity)
+    signed = jnp.concatenate(
+        [jnp.concatenate([gram, -gram], axis=1), jnp.concatenate([-gram, gram], axis=1)], axis=0
+    )
+    columns = columns_ref[...]
+    rows = rows_ref[...]
+    orb_column = jnp.concatenate([columns[:, 0:1], columns[:, 1:2]], axis=0)
+    partner_column = jnp.concatenate([columns[:, 1:2], columns[:, 0:1]], axis=0)
+    orb_row = jnp.concatenate([rows[0:1], rows[1:2]], axis=1)
+    partner_row = jnp.concatenate([rows[1:2], rows[0:1]], axis=1)
+    couple = jnp.where(partner_column == partner_row, signed, 0.0)
+    hot_shape = (2 * pair_count, OCC)
+    hot = (orb_column == lax.broadcasted_iota(jnp.int32, hot_shape, 1)).astype(jnp.float32)
+    turned = (orb_row == lax.broadcasted_iota(jnp.int32, hot_shape[::-1], 0)).astype(jnp.float32)
+    inner = jnp.dot(couple, hot, precision=lax.Precision.HIGHEST)
+    occ_ref[...] = -jnp.dot(turned, inner, precision=lax.Precision.HIGHEST)
+    for k in range(near):
+        virt_ref[k * chunk : (k + 1) * chunk] = spread_ref[k, :chunk, :]
 
 
-def occ_density(pair_gram, pairs):
-    orb, partner, sign = occurrences(pairs)
-    doubled = jnp.tile(pair_gram, (2, 2))
-    couple = jnp.where(
-        partner[:, None] == partner[None, :], sign[:, None] * sign[None, :] * doubled, 0.0
-    )
-    orbitals = jnp.arange(OCC, dtype=jnp.int32)
-    hot = (orb[:, None] == orbitals[None, :]).astype(jnp.float32)
-    inner_sum = jnp.dot(couple, hot, precision=lax.Precision.HIGHEST)
-    return -jnp.dot(hot.T, inner_sum, precision=lax.Precision.HIGHEST)
+def finish(spread, pairs, chunk):
+    near, _, width = spread.shape
+    vmem = pl.BlockSpec(memory_space=pltpu.VMEM)
+    return pl.pallas_call(
+        finish_kernel,
+        out_shape=(
+            jax.ShapeDtypeStruct((near * chunk, width), jnp.float32),
+            jax.ShapeDtypeStruct((OCC, OCC), jnp.float32),
+        ),
+        in_specs=[vmem, vmem, vmem],
+        out_specs=(vmem, vmem),
+        compiler_params=pltpu.CompilerParams(vmem_limit_bytes=8 * 1024 * 1024),
+        name="finish",
+    )(spread, *pairs)
 
 
 def virt_kernel(tiles_ref, place_ref, own_ref, other_ref, out_ref, whole_ref, slot_ref):
@@ -122,24 +145,27 @@
     other = lax.ppermute(own, "sub", [(0, 1), (1, 0)])
     place = jnp.stack([vir_at * slot_dev, sub_at]).astype(jnp.int32)
     part = virt_partial(tile_list, place, own, other, slot_dev)
+    pairs = got[:, 0, slot_dev * width : slot_dev * width + 2].astype(jnp.int32)
+    rows = got[:, :, : slot_dev * width].reshape(pair_count, share_rows * slot_dev * width)
+    local_gram = lax.dot_general(
+        rows, rows, (((1,), (1,)), ((), ())), preferred_element_type=jnp.float32
+    )
+    blocks = width // pair_count
+    packed_gram = local_gram.reshape(blocks, pair_count // blocks, pair_count)
+    packed_gram = jnp.transpose(packed_gram, (1, 0, 2)).reshape(-1, width)
+    packed_gram, *pairs = lax.optimization_barrier((packed_gram, pairs, pairs.T))
+    gram_rows = sent_to_all(packed_gram, ("vir", "sub")).sum(axis=0)
+
+    part, gram_rows = lax.optimization_barrier((part, gram_rows))
     chunk = slot_dev * row_dev // near
     near_parts = lax.all_to_all(
         part.reshape(near, chunk, width), "near", split_axis=0, concat_axis=0, tiled=True
     )
     near_sum = near_parts.sum(axis=0)
-
-    pairs = got[:, 0, slot_dev * width : slot_dev * width + 2].astype(jnp.int32)
-    rows = got[:, :, : slot_dev * width].reshape(pair_count, share_rows * slot_dev * width)
-    local_gram = lax.dot_general(
-        rows, rows, (((1,), (1,)), ((), ())), preferred_element_type=jnp.float32
-    )
-    gram_rows = lax.psum(local_gram.reshape(-1, width), ("vir", "sub"))
-
     total = sent_to_all(jnp.concatenate([near_sum, gram_rows], axis=0), "far").sum(axis=0)
     spread = sent_to_all(total, "near")
-    p_virt = spread[:, :chunk].reshape(slot_dev, row_dev, width)
-    gram = spread[:, chunk:].sum(axis=0).reshape(pair_count, pair_count)
-    return (p_virt, occ_density(gram, pairs))
+    virt_rows, p_occ = finish(spread, pairs, chunk)
+    return (virt_rows.reshape(slot_dev, row_dev, width), p_occ)
 
 
 def solution(mesh):

time: 175 us -> 183 us (1.046)
  the two profiles are of different devices: /device:TPU:40 before, /device:TPU:33 now
where the time goes in v3:
time: 183 us; the launch traced here: 179 us
  starting transfers between devices  71.6 us (39%)
  blocking collectives  63.5 us (35%)
  waiting for transfers between devices  33.2 us (18%)
  local copies, waits for them, and re-layouts  4.38 us (2%)
  Pallas kernels  4.19 us (2%)
    all_to_all x1, starting transfers between devices, shards(): lax.all_to_all(jnp.concatenate([share, ids], axis=2), ('far', 'near'), sp...  46.4 us
    all_to_all x1, blocking collectives, sent_to_all(): return lax.all_to_all(copies, axis, split_axis=0, concat_axis=0, tiled=True)  30.7 us
    all_to_all x2, starting transfers between devices, sent_to_all(): return lax.all_to_all(copies, axis, split_axis=0, concat_axis=0, tiled=True)  21.2 us
    all_to_all x1, blocking collectives, shards(): lax.all_to_all(part.reshape(near, chunk, width), 'near', split_axis=0, co...  20.3 us
    all_to_all x2, waiting for transfers between devices, sent_to_all(): return lax.all_to_all(copies, axis, split_axis=0, concat_axis=0, tiled=True)  17.5 us
    all_to_all x1, waiting for transfers between devices, shards(): lax.all_to_all(jnp.concatenate([share, ids], axis=2), ('far', 'near'), sp...  15.7 us
    all_gather x1, blocking collectives, shards(): own = lax.all_gather(masked, 'vir', axis=0, tiled=True)  12.4 us
    ppermute x1, starting transfers between devices, shards(): other = lax.ppermute(own, 'sub', [(0, 1), (1, 0)])  3.96 us
  transfers between devices with their start and end apart: 4, of which 3 were waited for; matrix products, arithmetic and copies ran while one was open for 1% of the time, Pallas kernels for 1%

profile of v3, /device:TPU:33, one launch (start us, length us, event | category | flops | bytes accessed | tf_op | source)
XLA Modules:
  0.0 179.4 jit_solution(6071091322521505283)
XLA Ops:
  0.6 0.0 copy-start.1
  0.6 0.7 copy-done.1
  1.3 0.1 constant_dynamic-slice_fusion
  1.4 0.0 copy-start.2
  1.4 0.6 copy-done.2
  2.1 0.1 iota_compare_fusion
  2.1 1.1 fusion
  3.2 0.1 reshape.67
  3.4 0.8 copy.36
  4.2 0.0 copy-start
  4.2 46.4 %all-to-all-start = ((bf16[32,2,1280]{2,1,0:T(2,128)(2,1)}), bf16[32,2,1280]{2,1,0:T(2,128)(2,1)S(1)}, u32[]{:S(2)}, u32[]{:S(2)}) async-start(bf16[32,2,1280]{2,1,0:T(2,128)(2,1)} %copy.36), calls=%async_computation | async-start | bytes 327680 | tf_op jit(solution)/shard_map/all_to_all | solution.py:137
  50.7 0.1 iota_compare_fusion.1
  50.7 0.0 copy-done
  50.7 0.1 and_select_fusion.1
  50.9 12.4 %all_gather.3.own_ref = bf16[36,64,128]{2,1,0:T(8,128)(2,1)S(1)} all-gather(bf16[9,64,128]{2,1,0:T(8,128)(2,1)S(1)} %and_select_fusion.1), channel_id=1, replica_groups=mesh['groups'=2,'far'=4,'near'=8,'vir'=4,'sub'=2] {'vir'}, dimensions={0}, use_global_device_ids=true | all-gather | bytes 737280 | tf_op jit(solution)/shard_map/all_gather | solution.py:144
  63.3 4.0 %collective-permute-start = (bf16[36,64,128]{2,1,0:T(8,128)(2,1)S(1)}, bf16[36,64,128]{2,1,0:T(8,128)(2,1)S(1)}, u32[]{:S(2)}, u32[]{:S(2)}) collective-permute-start(bf16[36,64,128]{2,1,0:T(8,128)(2,1)S(1)} %all_gather.3.own_ref), channel_id=1, source_target_pairs={{0,1},{1,0},{2,3},{3,2},{4,5},{5,4},{6,7},{7,6},{8,9},{9,8},{10,11... | collective-permute-start | bytes 1769480 | tf_op jit(solution)/shard_map/ppermute | solution.py:145
  67.3 15.7 %all-to-all-done = bf16[32,2,1280]{2,1,0:T(2,128)(2,1)S(1)} async-done(((bf16[32,2,1280]{2,1,0:T(2,128)(2,1)}), bf16[32,2,1280]{2,1,0:T(2,128)(2,1)S(1)}, u32[]{:S(2)}, u32[]{:S(2)}) %all-to-all-start) | async-done | bytes 163872 | tf_op jit(solution)/shard_map/all_to_all | solution.py:137
  82.9 0.1 slice.16
  83.0 0.1 dot_general.5
  83.1 0.1 reshape.73
  83.2 0.2 convolution_bitcast_fusion
  83.4 0.1 reshape.69
  83.5 0.1 copy.40
  83.6 0.6 broadcast_in_dim.28
  84.3 6.9 %all-to-all-start.1 = ((f32[8,8,128]{2,1,0:T(8,128)}), f32[8,8,128]{2,1,0:T(8,128)S(1)}, u32[]{:S(2)}, u32[]{:S(2)}) async-start(f32[8,8,128]{2,1,0:T(8,128)} %broadcast_in_dim.28), calls=%async_computation.1 | async-start | bytes 65536 | tf_op jit(solution)/shard_map/all_to_all | solution.py:17
  91.2 0.1 pad_add_fusion.place_ref
  91.2 0.1 copy.34.tiles_ref
  91.3 0.0 collective-permute-done.other_ref
  91.3 2.7 %virt_partial.1 = f32[9,64,128]{2,1,0:T(8,128)S(1)} custom-call(s32[36,2]{1,0:T(8,128)S(1)} %copy.34.tiles_ref, s32[2]{0:T(128)S(1)} %pad_add_fusion.place_ref, bf16[36,64,128]{2,1,0:T(8,128)(2,1)S(1)} %all_gather.3.own_ref, bf16[36,64,128]{2,1,0:T(8,128)(2,1)S(1)} %collective-permute-done.other_ref), custom_call_target="tpu_custom_call" | custom-call | tf_op jit(solution)/shard_map/virt_partial/pallas_call | solution.py:103
  94.0 1.9 %all-to-all-done.1 = f32[8,8,128]{2,1,0:T(8,128)S(1)} async-done(((f32[8,8,128]{2,1,0:T(8,128)}), f32[8,8,128]{2,1,0:T(8,128)S(1)}, u32[]{:S(2)}, u32[]{:S(2)}) %all-to-all-start.1) | async-done | bytes 32800 | tf_op jit(solution)/shard_map/all_to_all | solution.py:17
  95.9 20.3 %all_to_all.25 = f32[8,72,128]{2,1,0:T(8,128)S(1)} all-to-all(f32[8,72,128]{2,1,0:T(8,128)S(1)} %bitcast.24), channel_id=1, replica_groups=mesh['groups'=2,'far'=4,'near'=8,'vir'=4,'sub'=2] {'near'}, dimensions={0} | all-to-all | bytes 589824 | tf_op jit(solution)/shard_map/all_to_all | solution.py:161
  116.3 30.7 %all_to_all.26 = f32[4,80,128]{2,1,0:T(8,128)S(1)} all-to-all(f32[4,80,128]{2,1,0:T(8,128)S(1)} %broadcast_in_dim.29), channel_id=1, replica_groups=mesh['groups'=2,'far'=4,'near'=8,'vir'=4,'sub'=2] {'far'}, dimensions={0} | all-to-all | bytes 327680 | tf_op jit(solution)/shard_map/all_to_all | solution.py:17
  147.0 0.7 broadcast_in_dim.30
  147.7 14.3 %all-to-all-start.4 = ((f32[8,80,128]{2,1,0:T(8,128)}), f32[8,80,128]{2,1,0:T(8,128)S(1)}, u32[]{:S(2)}, u32[]{:S(2)}) async-start(f32[8,80,128]{2,1,0:T(8,128)} %broadcast_in_dim.30), calls=%async_computation.4 | async-start | bytes 655360 | tf_op jit(solution)/shard_map/all_to_all | solution.py:17
  162.1 0.1 copy.39.columns_ref
  162.2 15.7 %all-to-all-done.4.spread_ref = f32[8,80,128]{2,1,0:T(8,128)S(1)} async-done(((f32[8,80,128]{2,1,0:T(8,128)}), f32[8,80,128]{2,1,0:T(8,128)S(1)}, u32[]{:S(2)}, u32[]{:S(2)}) %all-to-all-start.4) | async-done | bytes 327712 | tf_op jit(solution)/shard_map/all_to_all | solution.py:17
  177.8 1.5 finish.1
  (15 shorter events, 0.1 us)
Async XLA Ops:
  0.6 0.7 copy-start.1
  1.4 0.7 copy-start.2
  4.2 46.5 %copy-start = (bf16[1,9,64,128]{3,2,1,0:T(8,128)(2,1)S(1)}, bf16[1,9,64,128]{3,2,1,0:T(8,128)(2,1)}, u32[]{:S(2)}) copy-start(bf16[1,9,64,128]{3,2,1,0:T(8,128)(2,1)} %param.3) | copy-start | bytes 442372
  4.2 78.7 %all-to-all-start = ((bf16[32,2,1280]{2,1,0:T(2,128)(2,1)}), bf16[32,2,1280]{2,1,0:T(2,128)(2,1)S(1)}, u32[]{:S(2)}, u32[]{:S(2)}) async-start(bf16[32,2,1280]{2,1,0:T(2,128)(2,1)} %copy.36), calls=%async_computation | async-start | bytes 327680 | tf_op jit(solution)/shard_map/all_to_all | solution.py:137
  63.3 28.0 %collective-permute-start = (bf16[36,64,128]{2,1,0:T(8,128)(2,1)S(1)}, bf16[36,64,128]{2,1,0:T(8,128)(2,1)S(1)}, u32[]{:S(2)}, u32[]{:S(2)}) collective-permute-start(bf16[36,64,128]{2,1,0:T(8,128)(2,1)S(1)} %all_gather.3.own_ref), channel_id=1, source_target_pairs={{0,1},{1,0},{2,3},{3,2},{4,5},{5,4},{6,7},{7,6},{8,9},{9,8},{10,11... | collective-permute-start | bytes 1769480 | tf_op jit(solution)/shard_map/ppermute | solution.py:145
  84.3 11.6 %all-to-all-start.1 = ((f32[8,8,128]{2,1,0:T(8,128)}), f32[8,8,128]{2,1,0:T(8,128)S(1)}, u32[]{:S(2)}, u32[]{:S(2)}) async-start(f32[8,8,128]{2,1,0:T(8,128)} %broadcast_in_dim.28), calls=%async_computation.1 | async-start | bytes 65536 | tf_op jit(solution)/shard_map/all_to_all | solution.py:17
  147.7 30.1 %all-to-all-start.4 = ((f32[8,80,128]{2,1,0:T(8,128)}), f32[8,80,128]{2,1,0:T(8,128)S(1)}, u32[]{:S(2)}, u32[]{:S(2)}) async-start(f32[8,80,128]{2,1,0:T(8,128)} %broadcast_in_dim.30), calls=%async_computation.4 | async-start | bytes 655360 | tf_op jit(solution)/shard_map/all_to_all | solution.py:17

commit v4 on v3

--- a/solution.py
+++ b/solution.py
@@ -10,20 +10,95 @@
 OCC = 256
 NTV = 8
 NEAR = 8
-
-
-def sent_to_all(array, axis):
-    copies = jnp.broadcast_to(array, (lax.axis_size(axis), *array.shape))
-    return lax.all_to_all(copies, axis, split_axis=0, concat_axis=0, tiled=True)
+GRAIN = 8
+STEPS = 256.0
+TOP = 32767.0
+FLOOR = 2.0**-120
+
+
+def coded(values):
+    largest = jnp.max(jnp.abs(values), axis=1, keepdims=True)
+    k = jnp.floor(jnp.log2(jnp.maximum(largest, FLOOR)) * STEPS) + 2.0
+    return (values * (jnp.exp2(k * (-1.0 / STEPS)) * TOP), k)
+
+
+def rounded(values):
+    return jnp.clip(jnp.floor(values + 0.5), -TOP, TOP)
+
+
+def as_row(column, width):
+    shape = (column.shape[0], width)
+    here = lax.broadcasted_iota(jnp.int32, shape, 0) == lax.broadcasted_iota(jnp.int32, shape, 1)
+    return jnp.sum(jnp.where(here, column, 0.0), axis=0, keepdims=True)
+
+
+def as_column(row, count):
+    shape = (count, row.shape[1])
+    here = lax.broadcasted_iota(jnp.int32, shape, 0) == lax.broadcasted_iota(jnp.int32, shape, 1)
+    return jnp.sum(jnp.where(here, row, 0.0), axis=1, keepdims=True)
+
+
+def scale_of(row, count):
+    return jnp.exp2(as_column(row, count) * (1.0 / STEPS)) * (1.0 / TOP)
+
+
+def message(values, gram=None):
+    _, width = values.shape
+    codes, k = coded(values)
+    parts = [rounded(codes)]
+    scales = [as_row(k, width)]
+    if gram is not None:
+        gram_codes, gram_k = coded(gram)
+        high = rounded(gram_codes)
+        parts += [high, rounded((gram_codes - high) * TOP)]
+        scales.append(as_row(gram_k, width))
+    spare = jnp.zeros((GRAIN - len(scales), width), jnp.float32)
+    whole = jnp.concatenate([parts[0], jnp.concatenate([*scales, spare], axis=0), *parts[1:]], axis=0)
+    return whole.astype(jnp.int32).astype(jnp.int16)
+
+
+def opened(block, count, with_gram):
+    words = block.astype(jnp.int32).astype(jnp.float32)
+    values = words[:count] * scale_of(words[count : count + 1], count)
+    if not with_gram:
+        return (values, None)
+    high = words[count + GRAIN : count + 2 * GRAIN]
+    low = words[count + 2 * GRAIN : count + 3 * GRAIN]
+    gram = (high + low * (1.0 / TOP)) * scale_of(words[count + 1 : count + 2], GRAIN)
+    return (values, gram)
+
+
+def near_kernel(parts_ref, gram_ref, out_ref):
+    count = parts_ref.shape[1] - GRAIN
+    total, _ = opened(parts_ref[0], count, False)
+    for k in range(1, parts_ref.shape[0]):
+        total = total + opened(parts_ref[k], count, False)[0]
+    block = message(total, gram_ref[...])
+    for k in range(out_ref.shape[0]):
+        out_ref[k] = block
+
+
+def far_kernel(parts_ref, out_ref):
+    count = parts_ref.shape[1] - 3 * GRAIN
+    total, gram = opened(parts_ref[0], count, True)
+    for k in range(1, parts_ref.shape[0]):
+        more, more_gram = opened(parts_ref[k], count, True)
+        total = total + more
+        gram = gram + more_gram
+    block = message(total, gram)
+    for k in range(out_ref.shape[0]):
+        out_ref[k] = block
 
 
 def finish_kernel(spread_ref, columns_ref, rows_ref, virt_ref, occ_ref):
     near, _, width = spread_ref.shape
     chunk = virt_ref.shape[0] // near
     pair_count = columns_ref.shape[0]
-    packed = spread_ref[0, chunk:, :]
-    for k in range(1, near):
-        packed = packed + spread_ref[k, chunk:, :]
+    packed = None
+    for k in range(near):
+        values, gram = opened(spread_ref[k], chunk, True)
+        virt_ref[k * chunk : (k + 1) * chunk] = values
+        packed = gram if packed is None else packed + gram
     gram = jnp.concatenate(
         [packed[:, k : k + pair_count] for k in range(0, width, pair_count)], axis=0
     )
@@ -42,29 +117,22 @@
     turned = (orb_row == lax.broadcasted_iota(jnp.int32, hot_shape[::-1], 0)).astype(jnp.float32)
     inner = jnp.dot(couple, hot, precision=lax.Precision.HIGHEST)
     occ_ref[...] = -jnp.dot(turned, inner, precision=lax.Precision.HIGHEST)
-    for k in range(near):
-        virt_ref[k * chunk : (k + 1) * chunk] = spread_ref[k, :chunk, :]
-
-
-def finish(spread, pairs, chunk):
-    near, _, width = spread.shape
+
+
+def in_vmem(kernel, out_shape, *operands):
     vmem = pl.BlockSpec(memory_space=pltpu.VMEM)
     return pl.pallas_call(
-        finish_kernel,
-        out_shape=(
-            jax.ShapeDtypeStruct((near * chunk, width), jnp.float32),
-            jax.ShapeDtypeStruct((OCC, OCC), jnp.float32),
-        ),
-        in_specs=[vmem, vmem, vmem],
-        out_specs=(vmem, vmem),
+        kernel,
+        out_shape=out_shape,
+        in_specs=[vmem] * len(operands),
+        out_specs=jax.tree.map(lambda _: vmem, out_shape),
         compiler_params=pltpu.CompilerParams(vmem_limit_bytes=8 * 1024 * 1024),
-        name="finish",
-    )(spread, *pairs)
-
-
-def virt_kernel(tiles_ref, place_ref, own_ref, other_ref, out_ref, whole_ref, slot_ref):
+    )(*operands)
+
+
+def virt_kernel(tiles_ref, place_ref, own_ref, other_ref, out_ref, whole_ref, part_ref, slot_ref):
     slot_count, half_rows, width = own_ref.shape
-    own_count = out_ref.shape[0]
+    own_count = part_ref.shape[0] // half_rows
     first = place_ref[0]
     half = place_ref[1]
 
@@ -91,22 +159,27 @@
     for i in range(own_count):
         left = whole_ref[tiles_ref[first + i, 0], pl.ds(half * half_rows, half_rows), :]
         right = whole_ref[tiles_ref[first + i, 1]]
-        out_ref[i] = lax.dot_general(
+        part_ref[i * half_rows : (i + 1) * half_rows] = lax.dot_general(
             left, right, (((1,), (1,)), ((), ())), preferred_element_type=jnp.float32
         )
-
-
-def virt_partial(tile_list, place, own, other, own_count):
+    chunk = part_ref.shape[0] // out_ref.shape[0]
+    for k in range(out_ref.shape[0]):
+        out_ref[k] = message(part_ref[k * chunk : (k + 1) * chunk])
+
+
+def virt_partial(tile_list, place, own, other, own_count, near):
     _, half_rows, width = own.shape
+    rows = own_count * half_rows
     smem = pl.BlockSpec(memory_space=pltpu.SMEM)
     vmem = pl.BlockSpec(memory_space=pltpu.VMEM)
     return pl.pallas_call(
         virt_kernel,
-        out_shape=jax.ShapeDtypeStruct((own_count, half_rows, width), jnp.float32),
+        out_shape=jax.ShapeDtypeStruct((near, rows // near + GRAIN, width), jnp.int16),
         in_specs=[smem, smem, vmem, vmem],
         out_specs=vmem,
         scratch_shapes=[
             pltpu.VMEM((NTV, width, NTV * width), jnp.bfloat16),
+            pltpu.VMEM((rows, width), jnp.float32),
             pltpu.SMEM((NTV * NTV,), jnp.int32),
         ],
         compiler_params=pltpu.CompilerParams(vmem_limit_bytes=24 * 1024 * 1024),
@@ -144,7 +217,7 @@
     own = lax.all_gather(masked, "vir", axis=0, tiled=True)
     other = lax.ppermute(own, "sub", [(0, 1), (1, 0)])
     place = jnp.stack([vir_at * slot_dev, sub_at]).astype(jnp.int32)
-    part = virt_partial(tile_list, place, own, other, slot_dev)
+    part = virt_partial(tile_list, place, own, other, slot_dev, near)
     pairs = got[:, 0, slot_dev * width : slot_dev * width + 2].astype(jnp.int32)
     rows = got[:, :, : slot_dev * width].reshape(pair_count, share_rows * slot_dev * width)
     local_gram = lax.dot_general(
@@ -153,18 +226,30 @@
     blocks = width // pair_count
     packed_gram = local_gram.reshape(blocks, pair_count // blocks, pair_count)
     packed_gram = jnp.transpose(packed_gram, (1, 0, 2)).reshape(-1, width)
-    packed_gram, *pairs = lax.optimization_barrier((packed_gram, pairs, pairs.T))
-    gram_rows = sent_to_all(packed_gram, ("vir", "sub")).sum(axis=0)
-
-    part, gram_rows = lax.optimization_barrier((part, gram_rows))
+    columns, rows = pairs, pairs.T
     chunk = slot_dev * row_dev // near
-    near_parts = lax.all_to_all(
-        part.reshape(near, chunk, width), "near", split_axis=0, concat_axis=0, tiled=True
-    )
-    near_sum = near_parts.sum(axis=0)
-    total = sent_to_all(jnp.concatenate([near_sum, gram_rows], axis=0), "far").sum(axis=0)
-    spread = sent_to_all(total, "near")
-    virt_rows, p_occ = finish(spread, pairs, chunk)
+    near_parts = lax.all_to_all(part, "near", split_axis=0, concat_axis=0, tiled=True)
+    gram_rows = lax.psum(packed_gram, ("vir", "sub"))
+    long_rows = chunk + 3 * GRAIN
+    far_block = in_vmem(
+        near_kernel, jax.ShapeDtypeStruct((far, long_rows, width), jnp.int16), near_parts, gram_rows
+    )
+    far_block, columns, rows = lax.optimization_barrier((far_block, columns, rows))
+    far_parts = lax.all_to_all(far_block, "far", split_axis=0, concat_axis=0, tiled=True)
+    last_block = in_vmem(
+        far_kernel, jax.ShapeDtypeStruct((near, long_rows, width), jnp.int16), far_parts
+    )
+    spread = lax.all_to_all(last_block, "near", split_axis=0, concat_axis=0, tiled=True)
+    virt_rows, p_occ = in_vmem(
+        finish_kernel,
+        (
+            jax.ShapeDtypeStruct((near * chunk, width), jnp.float32),
+            jax.ShapeDtypeStruct((OCC, OCC), jnp.float32),
+        ),
+        spread,
+        columns,
+        rows,
+    )
     return (virt_rows.reshape(slot_dev, row_dev, width), p_occ)
 
 

time: 183 us -> 162 us (0.89)
  the two profiles are of different devices: /device:TPU:33 before, /device:TPU:40 now
where the time goes in v4:
time: 162 us; the launch traced here: 161 us
  blocking collectives  62.1 us (38%)
  starting transfers between devices  61.3 us (38%)
  waiting for transfers between devices  26.3 us (16%)
  Pallas kernels  6.27 us (4%)
  local copies, waits for them, and re-layouts  2.92 us (2%)
    all_to_all x1, starting transfers between devices, shards(): lax.all_to_all(jnp.concatenate([share, ids], axis=2), ('far', 'near'), sp...  45.9 us
    all_to_all x1, blocking collectives, shards(): lax.all_to_all(far_block, 'far', split_axis=0, concat_axis=0, tiled=True)  34.9 us
    psum x1, blocking collectives, shards(): gram_rows = lax.psum(packed_gram, ('vir', 'sub'))  13.7 us
    all_gather x1, blocking collectives, shards(): own = lax.all_gather(masked, 'vir', axis=0, tiled=True)  13.6 us
    all_to_all x1, waiting for transfers between devices, shards(): lax.all_to_all(jnp.concatenate([share, ids], axis=2), ('far', 'near'), sp...  12.5 us
    all_to_all x1, waiting for transfers between devices, shards(): lax.all_to_all(last_block, 'near', split_axis=0, concat_axis=0, tiled=True)  12 us
    all_to_all x1, starting transfers between devices, shards(): lax.all_to_all(last_block, 'near', split_axis=0, concat_axis=0, tiled=True)  9.83 us
    all_to_all x1, starting transfers between devices, shards(): lax.all_to_all(part, 'near', split_axis=0, concat_axis=0, tiled=True)  3.59 us
  transfers between devices with their start and end apart: 4, of which 3 were waited for; matrix products, arithmetic and copies ran while one was open for 1% of the time, Pallas kernels for 2%

profile of v4, /device:TPU:40, one launch (start us, length us, event | category | flops | bytes accessed | tf_op | source)
XLA Modules:
  0.0 161.3 jit_solution(12051853729444804318)
XLA Ops:
  0.6 0.0 copy-start.1
  0.6 0.7 copy-done.1
  1.3 0.1 constant_dynamic-slice_fusion
  1.4 0.1 iota_compare_fusion
  1.5 1.1 fusion
  2.6 0.0 copy-start.2
  2.6 0.1 reshape.64
  2.7 0.6 copy-done.2
  3.3 0.8 copy.25
  4.1 0.0 copy-start
  4.1 45.9 %all-to-all-start.1 = ((bf16[32,2,1280]{2,1,0:T(2,128)(2,1)}), bf16[32,2,1280]{2,1,0:T(2,128)(2,1)S(1)}, u32[]{:S(2)}, u32[]{:S(2)}) async-start(bf16[32,2,1280]{2,1,0:T(2,128)(2,1)} %copy.25), calls=%async_computation.1 | async-start | bytes 327680 | tf_op jit(solution)/shard_map/all_to_all | solution.py:210
  50.0 0.1 iota_compare_fusion.1
  50.1 0.0 copy-done
  50.1 0.1 and_select_fusion.1
  50.2 13.6 %all_gather.3.own_ref = bf16[36,64,128]{2,1,0:T(8,128)(2,1)S(1)} all-gather(bf16[9,64,128]{2,1,0:T(8,128)(2,1)S(1)} %and_select_fusion.1), channel_id=1, replica_groups=mesh['groups'=2,'far'=4,'near'=8,'vir'=4,'sub'=2] {'vir'}, dimensions={0}, use_global_device_ids=true | all-gather | bytes 737280 | tf_op jit(solution)/shard_map/all_gather | solution.py:217
  63.8 1.9 %collective-permute-start = (bf16[36,64,128]{2,1,0:T(8,128)(2,1)S(1)}, bf16[36,64,128]{2,1,0:T(8,128)(2,1)S(1)}, u32[]{:S(2)}, u32[]{:S(2)}) collective-permute-start(bf16[36,64,128]{2,1,0:T(8,128)(2,1)S(1)} %all_gather.3.own_ref), channel_id=1, source_target_pairs={{0,1},{1,0},{2,3},{3,2},{4,5},{5,4},{6,7},{7,6},{8,9},{9,8},{10,11... | collective-permute-start | bytes 1769480 | tf_op jit(solution)/shard_map/ppermute | solution.py:218
  65.8 0.1 copy.23.tiles_ref
  65.9 0.1 pad_add_fusion.place_ref
  65.9 1.8 %collective-permute-done.other_ref = bf16[36,64,128]{2,1,0:T(8,128)(2,1)S(1)} collective-permute-done((bf16[36,64,128]{2,1,0:T(8,128)(2,1)S(1)}, bf16[36,64,128]{2,1,0:T(8,128)(2,1)S(1)}, u32[]{:S(2)}, u32[]{:S(2)}) %collective-permute-start) | collective-permute-done | bytes 589856 | tf_op jit(solution)/shard_map/ppermute | solution.py:218
  67.7 3.5 %virt_partial.1 = s16[8,80,128]{2,1,0:T(8,128)(2,1)} custom-call(s32[36,2]{1,0:T(8,128)S(1)} %copy.23.tiles_ref, s32[2]{0:T(128)S(1)} %pad_add_fusion.place_ref, bf16[36,64,128]{2,1,0:T(8,128)(2,1)S(1)} %all_gather.3.own_ref, bf16[36,64,128]{2,1,0:T(8,128)(2,1)S(1)} %collective-permute-done.other_ref), custom_call_target="tpu_custom_call" | custom-call | tf_op jit(solution)/shard_map/virt_partial/pallas_call | solution.py:175
  71.2 12.5 %all-to-all-done.1 = bf16[32,2,1280]{2,1,0:T(2,128)(2,1)S(1)} async-done(((bf16[32,2,1280]{2,1,0:T(2,128)(2,1)}), bf16[32,2,1280]{2,1,0:T(2,128)(2,1)S(1)}, u32[]{:S(2)}, u32[]{:S(2)}) %all-to-all-start.1) | async-done | bytes 163872 | tf_op jit(solution)/shard_map/all_to_all | solution.py:210
  83.7 3.6 %all-to-all-start = ((s16[8,80,128]{2,1,0:T(8,128)(2,1)}), s16[8,80,128]{2,1,0:T(8,128)(2,1)S(1)}, u32[]{:S(2)}, u32[]{:S(2)}) async-start(s16[8,80,128]{2,1,0:T(8,128)(2,1)} %virt_partial.1), calls=%async_computation | async-start | bytes 327680 | tf_op jit(solution)/shard_map/all_to_all | solution.py:231
  87.3 0.1 slice.16
  87.4 0.1 dot_general.5
  87.5 0.1 reshape.69
  87.6 0.2 convolution_bitcast_fusion
  87.8 0.1 reshape.66
  87.9 0.1 copy.29
  88.0 13.7 %psum.7.gram_ref = f32[8,128]{1,0:T(8,128)S(1)} all-reduce(f32[8,128]{1,0:T(8,128)S(1)} %reshape.66), channel_id=1, replica_groups=mesh['groups'=2,'far'=4,'near'=8,'vir'=4,'sub'=2] {'vir','sub'}, use_global_device_ids=true, to_apply=%region_0.1 | all-reduce | flops 1024 | bytes 8192 | tf_op jit(solution)/shard_map/psum | solution.py:232
  101.7 0.0 all-to-all-done.parts_ref
  101.7 0.3 shard_map.50
  102.0 34.9 %all_to_all.20.parts_ref = s16[4,96,128]{2,1,0:T(8,128)(2,1)S(1)} all-to-all(s16[4,96,128]{2,1,0:T(8,128)(2,1)S(1)} %shard_map.50), channel_id=1, replica_groups=mesh['groups'=2,'far'=4,'near'=8,'vir'=4,'sub'=2] {'far'}, dimensions={0} | all-to-all | bytes 196608 | tf_op jit(solution)/shard_map/all_to_all | solution.py:238
  136.9 0.9 shard_map.51
  137.8 9.8 %all-to-all-start.3 = ((s16[8,96,128]{2,1,0:T(8,128)(2,1)}), s16[8,96,128]{2,1,0:T(8,128)(2,1)S(1)}, u32[]{:S(2)}, u32[]{:S(2)}) async-start(s16[8,96,128]{2,1,0:T(8,128)(2,1)} %shard_map.51), calls=%async_computation.3 | async-start | bytes 393216 | tf_op jit(solution)/shard_map/all_to_all | solution.py:242
  147.6 0.1 copy.28.columns_ref
  147.7 12.0 %all-to-all-done.3.spread_ref = s16[8,96,128]{2,1,0:T(8,128)(2,1)S(1)} async-done(((s16[8,96,128]{2,1,0:T(8,128)(2,1)}), s16[8,96,128]{2,1,0:T(8,128)(2,1)S(1)}, u32[]{:S(2)}, u32[]{:S(2)}) %all-to-all-start.3) | async-done | bytes 196640 | tf_op jit(solution)/shard_map/all_to_all | solution.py:242
  159.7 1.6 %shard_map.52 = (f32[576,128]{1,0:T(8,128)}, f32[256,256]{1,0:T(8,128)}) custom-call(s16[8,96,128]{2,1,0:T(8,128)(2,1)S(1)} %all-to-all-done.3.spread_ref, s32[32,2]{1,0:T(8,128)S(1)} %copy.28.columns_ref, s32[2,32]{1,0:T(2,128)S(1)} %get-tuple-element.9.rows_ref), custom_call_target="tpu_custom_call" | custom-call | tf_op jit(solution)/shard_map/pallas_call | solution.py:124
  (10 shorter events, 0.1 us)
Async XLA Ops:
  0.6 0.7 copy-start.1
  2.6 0.7 copy-start.2
  4.1 46.0 %copy-start = (bf16[1,9,64,128]{3,2,1,0:T(8,128)(2,1)S(1)}, bf16[1,9,64,128]{3,2,1,0:T(8,128)(2,1)}, u32[]{:S(2)}) copy-start(bf16[1,9,64,128]{3,2,1,0:T(8,128)(2,1)} %param.3) | copy-start | bytes 442372
  4.1 79.6 %all-to-all-start.1 = ((bf16[32,2,1280]{2,1,0:T(2,128)(2,1)}), bf16[32,2,1280]{2,1,0:T(2,128)(2,1)S(1)}, u32[]{:S(2)}, u32[]{:S(2)}) async-start(bf16[32,2,1280]{2,1,0:T(2,128)(2,1)} %copy.25), calls=%async_computation.1 | async-start | bytes 327680 | tf_op jit(solution)/shard_map/all_to_all | solution.py:210
  63.8 3.9 %collective-permute-start = (bf16[36,64,128]{2,1,0:T(8,128)(2,1)S(1)}, bf16[36,64,128]{2,1,0:T(8,128)(2,1)S(1)}, u32[]{:S(2)}, u32[]{:S(2)}) collective-permute-start(bf16[36,64,128]{2,1,0:T(8,128)(2,1)S(1)} %all_gather.3.own_ref), channel_id=1, source_target_pairs={{0,1},{1,0},{2,3},{3,2},{4,5},{5,4},{6,7},{7,6},{8,9},{9,8},{10,11... | collective-permute-start | bytes 1769480 | tf_op jit(solution)/shard_map/ppermute | solution.py:218
  83.7 18.0 %all-to-all-start = ((s16[8,80,128]{2,1,0:T(8,128)(2,1)}), s16[8,80,128]{2,1,0:T(8,128)(2,1)S(1)}, u32[]{:S(2)}, u32[]{:S(2)}) async-start(s16[8,80,128]{2,1,0:T(8,128)(2,1)} %virt_partial.1), calls=%async_computation | async-start | bytes 327680 | tf_op jit(solution)/shard_map/all_to_all | solution.py:231
  137.8 21.9 %all-to-all-start.3 = ((s16[8,96,128]{2,1,0:T(8,128)(2,1)}), s16[8,96,128]{2,1,0:T(8,128)(2,1)S(1)}, u32[]{:S(2)}, u32[]{:S(2)}) async-start(s16[8,96,128]{2,1,0:T(8,128)(2,1)} %shard_map.51), calls=%async_computation.3 | async-start | bytes 393216 | tf_op jit(solution)/shard_map/all_to_all | solution.py:242

commit v5 on v4

--- a/solution.py
+++ b/solution.py
@@ -42,7 +42,7 @@
     return jnp.exp2(as_column(row, count) * (1.0 / STEPS)) * (1.0 / TOP)
 
 
-def message(values, gram=None):
+def message(values, gram=None, ids=None):
     _, width = values.shape
     codes, k = coded(values)
     parts = [rounded(codes)]
@@ -51,7 +51,7 @@
         gram_codes, gram_k = coded(gram)
         high = rounded(gram_codes)
         parts += [high, rounded((gram_codes - high) * TOP)]
-        scales.append(as_row(gram_k, width))
+        scales += [as_row(gram_k, width), ids]
     spare = jnp.zeros((GRAIN - len(scales), width), jnp.float32)
     whole = jnp.concatenate([parts[0], jnp.concatenate([*scales, spare], axis=0), *parts[1:]], axis=0)
     return whole.astype(jnp.int32).astype(jnp.int16)
@@ -61,60 +61,62 @@
     words = block.astype(jnp.int32).astype(jnp.float32)
     values = words[:count] * scale_of(words[count : count + 1], count)
     if not with_gram:
-        return (values, None)
+        return (values, None, None)
     high = words[count + GRAIN : count + 2 * GRAIN]
     low = words[count + 2 * GRAIN : count + 3 * GRAIN]
     gram = (high + low * (1.0 / TOP)) * scale_of(words[count + 1 : count + 2], GRAIN)
-    return (values, gram)
-
-
-def near_kernel(parts_ref, gram_ref, out_ref):
+    return (values, gram, words[count + 2 : count + 3])
+
+
+def near_kernel(parts_ref, gram_ref, ids_ref, out_ref):
     count = parts_ref.shape[1] - GRAIN
-    total, _ = opened(parts_ref[0], count, False)
+    total, _, _ = opened(parts_ref[0], count, False)
     for k in range(1, parts_ref.shape[0]):
         total = total + opened(parts_ref[k], count, False)[0]
-    block = message(total, gram_ref[...])
+    block = message(total, gram_ref[...], ids_ref[...])
     for k in range(out_ref.shape[0]):
         out_ref[k] = block
 
 
 def far_kernel(parts_ref, out_ref):
     count = parts_ref.shape[1] - 3 * GRAIN
-    total, gram = opened(parts_ref[0], count, True)
+    total, gram, ids = opened(parts_ref[0], count, True)
     for k in range(1, parts_ref.shape[0]):
-        more, more_gram = opened(parts_ref[k], count, True)
+        more, more_gram, more_ids = opened(parts_ref[k], count, True)
         total = total + more
         gram = gram + more_gram
-    block = message(total, gram)
+        ids = ids + more_ids
+    block = message(total, gram, ids)
     for k in range(out_ref.shape[0]):
         out_ref[k] = block
 
 
-def finish_kernel(spread_ref, columns_ref, rows_ref, virt_ref, occ_ref):
+def finish_kernel(spread_ref, virt_ref, occ_ref):
     near, _, width = spread_ref.shape
     chunk = virt_ref.shape[0] // near
-    pair_count = columns_ref.shape[0]
-    packed = None
+    pair_count = width // 4
+    packed, ids = 0.0, 0.0
     for k in range(near):
-        values, gram = opened(spread_ref[k], chunk, True)
+        values, gram, some_ids = opened(spread_ref[k], chunk, True)
         virt_ref[k * chunk : (k + 1) * chunk] = values
-        packed = gram if packed is None else packed + gram
+        packed = packed + gram
+        ids = ids + some_ids
     gram = jnp.concatenate(
         [packed[:, k : k + pair_count] for k in range(0, width, pair_count)], axis=0
     )
     signed = jnp.concatenate(
         [jnp.concatenate([gram, -gram], axis=1), jnp.concatenate([-gram, gram], axis=1)], axis=0
     )
-    columns = columns_ref[...]
-    rows = rows_ref[...]
-    orb_column = jnp.concatenate([columns[:, 0:1], columns[:, 1:2]], axis=0)
-    partner_column = jnp.concatenate([columns[:, 1:2], columns[:, 0:1]], axis=0)
-    orb_row = jnp.concatenate([rows[0:1], rows[1:2]], axis=1)
-    partner_row = jnp.concatenate([rows[1:2], rows[0:1]], axis=1)
+    orb_row = ids[:, : 2 * pair_count]
+    partner_row = ids[:, 2 * pair_count :]
+    orb_column = as_column(orb_row, 2 * pair_count)
+    partner_column = as_column(partner_row, 2 * pair_count)
     couple = jnp.where(partner_column == partner_row, signed, 0.0)
     hot_shape = (2 * pair_count, OCC)
-    hot = (orb_column == lax.broadcasted_iota(jnp.int32, hot_shape, 1)).astype(jnp.float32)
-    turned = (orb_row == lax.broadcasted_iota(jnp.int32, hot_shape[::-1], 0)).astype(jnp.float32)
+    across = lax.broadcasted_iota(jnp.int32, hot_shape, 1).astype(jnp.float32)
+    down = lax.broadcasted_iota(jnp.int32, hot_shape[::-1], 0).astype(jnp.float32)
+    hot = (orb_column == across).astype(jnp.float32)
+    turned = (orb_row == down).astype(jnp.float32)
     inner = jnp.dot(couple, hot, precision=lax.Precision.HIGHEST)
     occ_ref[...] = -jnp.dot(turned, inner, precision=lax.Precision.HIGHEST)
 
@@ -133,15 +135,22 @@
 def virt_kernel(tiles_ref, place_ref, own_ref, other_ref, out_ref, whole_ref, part_ref, slot_ref):
     slot_count, half_rows, width = own_ref.shape
     own_count = part_ref.shape[0] // half_rows
-    first = place_ref[0]
+    vir_at = place_ref[0]
     half = place_ref[1]
+    own_tiles = own_count
+    holders = slot_count // own_tiles
+    first = vir_at * own_tiles
 
     def note(s, carry):
-        slot_ref[tiles_ref[s, 0] * NTV + tiles_ref[s, 1]] = s
+        steps = lax.rem(vir_at + holders - s // own_tiles, holders)
+        where = steps * own_tiles + lax.rem(s, own_tiles)
+        slot_ref[tiles_ref[s, 0] * NTV + tiles_ref[s, 1]] = where
         return carry
 
     lax.fori_loop(0, slot_count, note, 0)
     is_first = half == 0
+    shape = (width, width)
+    upper = lax.broadcasted_iota(jnp.int32, shape, 0) < lax.broadcasted_iota(jnp.int32, shape, 1)
     for r in range(NTV):
         for c in range(r, NTV):
             slot = slot_ref[r * NTV + c]
@@ -150,6 +159,8 @@
             tile = jnp.concatenate(
                 [jnp.where(is_first, mine, theirs), jnp.where(is_first, theirs, mine)], axis=0
             )
+            if r == c:
+                tile = jnp.where(upper, tile, jnp.zeros_like(tile))
             turned = tile.T
             if r == c:
                 whole_ref[r, :, c * width : (c + 1) * width] = tile - turned
@@ -194,47 +205,54 @@
     pair_count = far * near
     vir_at = lax.axis_index("vir")
     sub_at = lax.axis_index("sub")
-    in_tile = jnp.arange(width, dtype=jnp.int32)
+    pair_at = lax.axis_index(("far", "near"))
+    mine = amplitudes[0]
+    holders = lax.axis_size("vir")
+
+    pieces = [mine]
+    for step in range(1, holders):
+        hops = [(k, (k + step) % holders) for k in range(holders)]
+        pieces.append(lax.ppermute(mine, "vir", hops))
+    share_rows = row_dev // pair_count
+    share = mine.reshape(slot_dev, pair_count, share_rows, width)
+    share = jnp.transpose(share, (1, 2, 0, 3)).reshape(pair_count, share_rows, slot_dev * width)
+    got = lax.all_to_all(share, ("far", "near"), split_axis=0, concat_axis=0, tiled=True)
+    own = jnp.concatenate(pieces, axis=0)
+    other = lax.ppermute(own, "sub", [(0, 1), (1, 0)])
+    place = jnp.stack([vir_at, sub_at]).astype(jnp.int32)
+    part = virt_partial(tile_list, place, own, other, slot_dev, near)
     own_list = lax.dynamic_slice_in_dim(tile_list, vir_at * slot_dev, slot_dev, 0)
-    own_rows = sub_at * row_dev + jnp.arange(row_dev, dtype=jnp.int32)
-    own_lower = in_tile[None, :] <= own_rows[:, None]
-    own_diagonal = own_list[:, 0] == own_list[:, 1]
-    keep = jnp.logical_not(own_diagonal[:, None, None] & own_lower[None])
-    masked = jnp.where(keep, amplitudes[0], jnp.zeros((), jnp.bfloat16))
-
-    share_rows = row_dev // pair_count
-    share = masked.reshape(slot_dev, pair_count, share_rows, width)
-    share = jnp.transpose(share, (1, 2, 0, 3)).reshape(pair_count, share_rows, slot_dev * width)
-    ids = jnp.pad(pair_list.astype(jnp.bfloat16), ((0, share_rows - 1), (0, width - 2)))
-    ids = jnp.broadcast_to(ids[None], (pair_count, share_rows, width))
-    got = lax.all_to_all(
-        jnp.concatenate([share, ids], axis=2),
-        ("far", "near"),
-        split_axis=0,
-        concat_axis=0,
-        tiled=True,
-    )
-    own = lax.all_gather(masked, "vir", axis=0, tiled=True)
-    other = lax.ppermute(own, "sub", [(0, 1), (1, 0)])
-    place = jnp.stack([vir_at * slot_dev, sub_at]).astype(jnp.int32)
-    part = virt_partial(tile_list, place, own, other, slot_dev, near)
-    pairs = got[:, 0, slot_dev * width : slot_dev * width + 2].astype(jnp.int32)
-    rows = got[:, :, : slot_dev * width].reshape(pair_count, share_rows * slot_dev * width)
+    row = sub_at * row_dev + pair_at * share_rows + jnp.arange(share_rows, dtype=jnp.int32)
+    column = jnp.arange(width, dtype=jnp.int32)
+    lower = column[None, None, :] <= row[:, None, None]
+    diagonal = (own_list[:, 0] == own_list[:, 1])[None, :, None]
+    keep = jnp.logical_not(diagonal & lower).reshape(1, share_rows * slot_dev * width)
+    rows = got.reshape(pair_count, share_rows * slot_dev * width)
     local_gram = lax.dot_general(
-        rows, rows, (((1,), (1,)), ((), ())), preferred_element_type=jnp.float32
-    )
+        jnp.where(keep, rows, jnp.zeros((), rows.dtype)),
+        rows,
+        (((1,), (1,)), ((), ())),
+        preferred_element_type=jnp.float32,
+    )
+    lane = jnp.arange(width, dtype=jnp.int32)
+    quarter = lane // pair_count
+    swapped = (quarter == 1) | (quarter == 2)
+    own_ids = jnp.where(swapped, pair_list[0, 1], pair_list[0, 0]).astype(jnp.float32)
+    ids = jnp.where(lane % pair_count == pair_at, own_ids, 0.0)[None]
     blocks = width // pair_count
     packed_gram = local_gram.reshape(blocks, pair_count // blocks, pair_count)
     packed_gram = jnp.transpose(packed_gram, (1, 0, 2)).reshape(-1, width)
-    columns, rows = pairs, pairs.T
     chunk = slot_dev * row_dev // near
     near_parts = lax.all_to_all(part, "near", split_axis=0, concat_axis=0, tiled=True)
     gram_rows = lax.psum(packed_gram, ("vir", "sub"))
     long_rows = chunk + 3 * GRAIN
     far_block = in_vmem(
-        near_kernel, jax.ShapeDtypeStruct((far, long_rows, width), jnp.int16), near_parts, gram_rows
-    )
-    far_block, columns, rows = lax.optimization_barrier((far_block, columns, rows))
+        near_kernel,
+        jax.ShapeDtypeStruct((far, long_rows, width), jnp.int16),
+        near_parts,
+        gram_rows,
+        ids,
+    )
     far_parts = lax.all_to_all(far_block, "far", split_axis=0, concat_axis=0, tiled=True)
     last_block = in_vmem(
         far_kernel, jax.ShapeDtypeStruct((near, long_rows, width), jnp.int16), far_parts
@@ -247,8 +265,6 @@
             jax.ShapeDtypeStruct((OCC, OCC), jnp.float32),
         ),
         spread,
-        columns,
-        rows,
     )
     return (virt_rows.reshape(slot_dev, row_dev, width), p_occ)
 

time: 162 us -> 168 us (1.037)
  the two profiles are of different devices: /device:TPU:40 before, /device:TPU:33 now
where the time goes in v5:
time: 168 us; the launch traced here: 165 us
  blocking collectives  67.8 us (40%)
  starting transfers between devices  64.6 us (38%)
  waiting for transfers between devices  20.2 us (12%)
  Pallas kernels  5.9 us (4%)
  local copies, waits for them, and re-layouts  4.26 us (3%)
    all_to_all x1, starting transfers between devices, shards(): lax.all_to_all(share, ('far', 'near'), split_axis=0, concat_axis=0, tiled...  45.6 us
    all_to_all x1, blocking collectives, shards(): lax.all_to_all(far_block, 'far', split_axis=0, concat_axis=0, tiled=True)  29.3 us
    all_to_all x1, blocking collectives, shards(): lax.all_to_all(last_block, 'near', split_axis=0, concat_axis=0, tiled=True)  23.4 us
    all_to_all x1, waiting for transfers between devices, shards(): lax.all_to_all(share, ('far', 'near'), split_axis=0, concat_axis=0, tiled...  20 us
    psum x1, blocking collectives, shards(): gram_rows = lax.psum(packed_gram, ('vir', 'sub'))  15 us
    ppermute x3, starting transfers between devices, shards(): pieces.append(lax.ppermute(mine, 'vir', hops))  11.7 us
    ppermute x1, starting transfers between devices, shards(): other = lax.ppermute(own, 'sub', [(0, 1), (1, 0)])  3.67 us
    pallas_call x1, Pallas kernels, virt_partial(): pl.pallas_call(virt_kernel, out_shape=jax.ShapeDtypeStruct((near, rows //...  3.66 us
  transfers between devices with their start and end apart: 6, of which 2 were waited for; matrix products, arithmetic and copies ran while one was open for 3% of the time, Pallas kernels for 2%

profile of v5, /device:TPU:33, one launch (start us, length us, event | category | flops | bytes accessed | tf_op | source)
XLA Modules:
  0.0 165.4 jit_solution(18295812771824622422)
XLA Ops:
  0.6 4.1 %collective-permute-start = (bf16[9,64,128]{2,1,0:T(8,128)(2,1)}, bf16[9,64,128]{2,1,0:T(8,128)(2,1)S(1)}, u32[]{:S(2)}, u32[]{:S(2)}) collective-permute-start(bf16[9,64,128]{2,1,0:T(8,128)(2,1)} %bitcast.27), channel_id=1, source_target_pairs={{0,2},{2,4},{4,6},{6,0},{1,3},{3,5},{5,7},{7,1},{8,10},{10,12},{12... | collective-permute-start | bytes 442376 | tf_op jit(solution)/shard_map/ppermute | solution.py:215
  4.7 4.7 %collective-permute-start.1 = (bf16[9,64,128]{2,1,0:T(8,128)(2,1)}, bf16[9,64,128]{2,1,0:T(8,128)(2,1)S(1)}, u32[]{:S(2)}, u32[]{:S(2)}) collective-permute-start(bf16[9,64,128]{2,1,0:T(8,128)(2,1)} %bitcast.28), channel_id=1, source_target_pairs={{0,4},{2,6},{4,0},{6,2},{1,5},{3,7},{5,1},{7,3},{8,12},{10,14},{12... | collective-permute-start | bytes 442376 | tf_op jit(solution)/shard_map/ppermute | solution.py:215
  9.4 3.0 %collective-permute-start.2 = (bf16[9,64,128]{2,1,0:T(8,128)(2,1)}, bf16[9,64,128]{2,1,0:T(8,128)(2,1)S(1)}, u32[]{:S(2)}, u32[]{:S(2)}) collective-permute-start(bf16[9,64,128]{2,1,0:T(8,128)(2,1)} %bitcast.29), channel_id=1, source_target_pairs={{0,6},{2,0},{4,2},{6,4},{1,7},{3,1},{5,3},{7,5},{8,14},{10,8},{12,... | collective-permute-start | bytes 442376 | tf_op jit(solution)/shard_map/ppermute | solution.py:215
  12.4 1.0 copy.24
  13.4 0.1 reshape.151
  13.5 0.8 copy.19
  14.3 0.0 copy-start
  14.3 45.6 %all-to-all-start.1 = ((bf16[32,2,1152]{2,1,0:T(2,128)(2,1)}), bf16[32,2,1152]{2,1,0:T(2,128)(2,1)S(1)}, u32[]{:S(2)}, u32[]{:S(2)}) async-start(bf16[32,2,1152]{2,1,0:T(2,128)(2,1)} %copy.19), calls=%async_computation.1 | async-start | bytes 294912 | tf_op jit(solution)/shard_map/all_to_all | solution.py:219
  59.9 0.0 copy-start.1
  59.9 0.7 copy-done.1
  60.6 0.1 constant_dynamic-slice_fusion
  60.7 0.1 iota_compare_fusion
  60.8 0.0 collective-permute-done
  60.8 0.0 collective-permute-done.1
  60.8 0.0 collective-permute-done.2
  60.8 0.0 copy-done
  60.8 0.1 pad_maximum_fusion.own_ref
  60.9 3.7 %collective-permute-start.3 = (bf16[36,64,128]{2,1,0:T(8,128)(2,1)S(1)}, bf16[36,64,128]{2,1,0:T(8,128)(2,1)S(1)}, u32[]{:S(2)}, u32[]{:S(2)}) collective-permute-start(bf16[36,64,128]{2,1,0:T(8,128)(2,1)S(1)} %pad_maximum_fusion.own_ref), channel_id=1, source_target_pairs={{0,1},{1,0},{2,3},{3,2},{4,5},{5,4},{6,7},{7,6},{8,9},{9,8},{10,11... | collective-permute-start | bytes 1769480 | tf_op jit(solution)/shard_map/ppermute | solution.py:221
  64.5 0.1 pad_add_fusion.place_ref
  64.6 0.0 copy-start.2
  64.6 0.1 copy.17.tiles_ref
  64.7 0.6 copy-done.2
  65.3 0.6 fusion.2
  65.9 0.1 broadcast_bitcast_fusion.1
  66.0 0.2 collective-permute-done.3.other_ref
  66.2 3.7 %virt_partial.1 = s16[8,80,128]{2,1,0:T(8,128)(2,1)} custom-call(s32[36,2]{1,0:T(8,128)S(1)} %copy.17.tiles_ref, s32[2]{0:T(128)S(1)} %pad_add_fusion.place_ref, bf16[36,64,128]{2,1,0:T(8,128)(2,1)S(1)} %pad_maximum_fusion.own_ref, bf16[36,64,128]{2,1,0:T(8,128)(2,1)S(1)} %collective-permute-done.3.other_ref), custom_call_target="tpu_custom_call" | custom-call | tf_op jit(solution)/shard_map/virt_partial/pallas_call | solution.py:186
  69.8 20.0 %all-to-all-done.1 = bf16[32,2,1152]{2,1,0:T(2,128)(2,1)S(1)} async-done(((bf16[32,2,1152]{2,1,0:T(2,128)(2,1)}), bf16[32,2,1152]{2,1,0:T(2,128)(2,1)S(1)}, u32[]{:S(2)}, u32[]{:S(2)}) %all-to-all-start.1) | async-done | bytes 147488 | tf_op jit(solution)/shard_map/all_to_all | solution.py:219
  89.8 3.6 %all-to-all-start = ((s16[8,80,128]{2,1,0:T(8,128)(2,1)}), s16[8,80,128]{2,1,0:T(8,128)(2,1)S(1)}, u32[]{:S(2)}, u32[]{:S(2)}) async-start(s16[8,80,128]{2,1,0:T(8,128)(2,1)} %virt_partial.1), calls=%async_computation | async-start | bytes 327680 | tf_op jit(solution)/shard_map/all_to_all | solution.py:246
  93.4 1.3 compare_select_fusion.ids_ref
  94.7 0.1 broadcast_select_fusion
  94.9 0.1 select_n.61
  95.0 0.1 reshape.155
  95.1 0.2 convolution_bitcast_fusion
  95.2 0.1 reshape.153
  95.3 15.0 %psum.7.gram_ref = f32[8,128]{1,0:T(8,128)S(1)} all-reduce(f32[8,128]{1,0:T(8,128)S(1)} %reshape.153), channel_id=1, replica_groups=mesh['groups'=2,'far'=4,'near'=8,'vir'=4,'sub'=2] {'vir','sub'}, use_global_device_ids=true, to_apply=%region_0.1 | all-reduce | flops 1024 | bytes 8192 | tf_op jit(solution)/shard_map/psum | solution.py:247
  110.4 0.0 all-to-all-done.parts_ref
  110.4 0.3 shard_map.50
  110.6 29.3 %all_to_all.20.parts_ref = s16[4,96,128]{2,1,0:T(8,128)(2,1)S(1)} all-to-all(s16[4,96,128]{2,1,0:T(8,128)(2,1)S(1)} %shard_map.50), channel_id=1, replica_groups=mesh['groups'=2,'far'=4,'near'=8,'vir'=4,'sub'=2] {'far'}, dimensions={0} | all-to-all | bytes 196608 | tf_op jit(solution)/shard_map/all_to_all | solution.py:256
  140.0 0.2 shard_map.51
  140.2 23.4 %all_to_all.21.spread_ref = s16[8,96,128]{2,1,0:T(8,128)(2,1)S(1)} all-to-all(s16[8,96,128]{2,1,0:T(8,128)(2,1)S(1)} %shard_map.51), channel_id=1, replica_groups=mesh['groups'=2,'far'=4,'near'=8,'vir'=4,'sub'=2] {'near'}, dimensions={0} | all-to-all | bytes 393216 | tf_op jit(solution)/shard_map/all_to_all | solution.py:260
  163.6 1.7 %shard_map.52 = (f32[576,128]{1,0:T(8,128)}, f32[256,256]{1,0:T(8,128)}) custom-call(s16[8,96,128]{2,1,0:T(8,128)(2,1)S(1)} %all_to_all.21.spread_ref), custom_call_target="tpu_custom_call" | custom-call | tf_op jit(solution)/shard_map/pallas_call | solution.py:126
  (5 shorter events, 0.0 us)
Async XLA Ops:
  0.6 60.1 %collective-permute-start = (bf16[9,64,128]{2,1,0:T(8,128)(2,1)}, bf16[9,64,128]{2,1,0:T(8,128)(2,1)S(1)}, u32[]{:S(2)}, u32[]{:S(2)}) collective-permute-start(bf16[9,64,128]{2,1,0:T(8,128)(2,1)} %bitcast.27), channel_id=1, source_target_pairs={{0,2},{2,4},{4,6},{6,0},{1,3},{3,5},{5,7},{7,1},{8,10},{10,12},{12... | collective-permute-start | bytes 442376 | tf_op jit(solution)/shard_map/ppermute | solution.py:215
  4.7 56.0 %collective-permute-start.1 = (bf16[9,64,128]{2,1,0:T(8,128)(2,1)}, bf16[9,64,128]{2,1,0:T(8,128)(2,1)S(1)}, u32[]{:S(2)}, u32[]{:S(2)}) collective-permute-start(bf16[9,64,128]{2,1,0:T(8,128)(2,1)} %bitcast.28), channel_id=1, source_target_pairs={{0,4},{2,6},{4,0},{6,2},{1,5},{3,7},{5,1},{7,3},{8,12},{10,14},{12... | collective-permute-start | bytes 442376 | tf_op jit(solution)/shard_map/ppermute | solution.py:215
  9.4 51.4 %collective-permute-start.2 = (bf16[9,64,128]{2,1,0:T(8,128)(2,1)}, bf16[9,64,128]{2,1,0:T(8,128)(2,1)S(1)}, u32[]{:S(2)}, u32[]{:S(2)}) collective-permute-start(bf16[9,64,128]{2,1,0:T(8,128)(2,1)} %bitcast.29), channel_id=1, source_target_pairs={{0,6},{2,0},{4,2},{6,4},{1,7},{3,1},{5,3},{7,5},{8,14},{10,8},{12,... | collective-permute-start | bytes 442376 | tf_op jit(solution)/shard_map/ppermute | solution.py:215
  14.3 46.5 %copy-start = (bf16[1,9,64,128]{3,2,1,0:T(8,128)(2,1)S(1)}, bf16[1,9,64,128]{3,2,1,0:T(8,128)(2,1)}, u32[]{:S(2)}) copy-start(bf16[1,9,64,128]{3,2,1,0:T(8,128)(2,1)} %param.3) | copy-start | bytes 442372
  14.3 75.5 %all-to-all-start.1 = ((bf16[32,2,1152]{2,1,0:T(2,128)(2,1)}), bf16[32,2,1152]{2,1,0:T(2,128)(2,1)S(1)}, u32[]{:S(2)}, u32[]{:S(2)}) async-start(bf16[32,2,1152]{2,1,0:T(2,128)(2,1)} %copy.19), calls=%async_computation.1 | async-start | bytes 294912 | tf_op jit(solution)/shard_map/all_to_all | solution.py:219
  59.9 0.7 copy-start.1
  60.9 5.3 %collective-permute-start.3 = (bf16[36,64,128]{2,1,0:T(8,128)(2,1)S(1)}, bf16[36,64,128]{2,1,0:T(8,128)(2,1)S(1)}, u32[]{:S(2)}, u32[]{:S(2)}) collective-permute-start(bf16[36,64,128]{2,1,0:T(8,128)(2,1)S(1)} %pad_maximum_fusion.own_ref), channel_id=1, source_target_pairs={{0,1},{1,0},{2,3},{3,2},{4,5},{5,4},{6,7},{7,6},{8,9},{9,8},{10,11... | collective-permute-start | bytes 1769480 | tf_op jit(solution)/shard_map/ppermute | solution.py:221
  64.6 0.7 copy-start.2
  89.8 20.5 %all-to-all-start = ((s16[8,80,128]{2,1,0:T(8,128)(2,1)}), s16[8,80,128]{2,1,0:T(8,128)(2,1)S(1)}, u32[]{:S(2)}, u32[]{:S(2)}) async-start(s16[8,80,128]{2,1,0:T(8,128)(2,1)} %virt_partial.1), calls=%async_computation | async-start | bytes 327680 | tf_op jit(solution)/shard_map/all_to_all | solution.py:246

commit v6 on v5

--- a/solution.py
+++ b/solution.py
@@ -68,12 +68,19 @@
     return (values, gram, words[count + 2 : count + 3])
 
 
-def near_kernel(parts_ref, gram_ref, ids_ref, out_ref):
+def near_kernel(place_ref, pair_ref, parts_ref, gram_ref, out_ref):
+    width = parts_ref.shape[2]
+    pair_count = width // 4
+    lane = lax.broadcasted_iota(jnp.int32, (1, width), 1)
+    quarter = lane // pair_count
+    swapped = (quarter == 1) | (quarter == 2)
+    own_ids = jnp.where(swapped, pair_ref[:, 1:2], pair_ref[:, 0:1])
+    ids = jnp.where(lane - quarter * pair_count == place_ref[2], own_ids, 0).astype(jnp.float32)
     count = parts_ref.shape[1] - GRAIN
     total, _, _ = opened(parts_ref[0], count, False)
     for k in range(1, parts_ref.shape[0]):
         total = total + opened(parts_ref[k], count, False)[0]
-    block = message(total, gram_ref[...], ids_ref[...])
+    block = message(total, gram_ref[...], ids)
     for k in range(out_ref.shape[0]):
         out_ref[k] = block
 
@@ -121,30 +128,27 @@
     occ_ref[...] = -jnp.dot(turned, inner, precision=lax.Precision.HIGHEST)
 
 
-def in_vmem(kernel, out_shape, *operands):
+def in_vmem(kernel, out_shape, *operands, place=None):
     vmem = pl.BlockSpec(memory_space=pltpu.VMEM)
+    smem = pl.BlockSpec(memory_space=pltpu.SMEM)
+    places = () if place is None else (place,)
     return pl.pallas_call(
         kernel,
         out_shape=out_shape,
-        in_specs=[vmem] * len(operands),
+        in_specs=[smem] * len(places) + [vmem] * len(operands),
         out_specs=jax.tree.map(lambda _: vmem, out_shape),
         compiler_params=pltpu.CompilerParams(vmem_limit_bytes=8 * 1024 * 1024),
-    )(*operands)
+    )(*places, *operands)
 
 
 def virt_kernel(tiles_ref, place_ref, own_ref, other_ref, out_ref, whole_ref, part_ref, slot_ref):
     slot_count, half_rows, width = own_ref.shape
     own_count = part_ref.shape[0] // half_rows
-    vir_at = place_ref[0]
+    first = place_ref[0]
     half = place_ref[1]
-    own_tiles = own_count
-    holders = slot_count // own_tiles
-    first = vir_at * own_tiles
 
     def note(s, carry):
-        steps = lax.rem(vir_at + holders - s // own_tiles, holders)
-        where = steps * own_tiles + lax.rem(s, own_tiles)
-        slot_ref[tiles_ref[s, 0] * NTV + tiles_ref[s, 1]] = where
+        slot_ref[tiles_ref[s, 0] * NTV + tiles_ref[s, 1]] = s
         return carry
 
     lax.fori_loop(0, slot_count, note, 0)
@@ -207,19 +211,13 @@
     sub_at = lax.axis_index("sub")
     pair_at = lax.axis_index(("far", "near"))
     mine = amplitudes[0]
-    holders = lax.axis_size("vir")
-
-    pieces = [mine]
-    for step in range(1, holders):
-        hops = [(k, (k + step) % holders) for k in range(holders)]
-        pieces.append(lax.ppermute(mine, "vir", hops))
     share_rows = row_dev // pair_count
     share = mine.reshape(slot_dev, pair_count, share_rows, width)
     share = jnp.transpose(share, (1, 2, 0, 3)).reshape(pair_count, share_rows, slot_dev * width)
     got = lax.all_to_all(share, ("far", "near"), split_axis=0, concat_axis=0, tiled=True)
-    own = jnp.concatenate(pieces, axis=0)
+    own = lax.all_gather(mine, "vir", axis=0, tiled=True)
     other = lax.ppermute(own, "sub", [(0, 1), (1, 0)])
-    place = jnp.stack([vir_at, sub_at]).astype(jnp.int32)
+    place = jnp.stack([vir_at * slot_dev, sub_at, pair_at]).astype(jnp.int32)
     part = virt_partial(tile_list, place, own, other, slot_dev, near)
     own_list = lax.dynamic_slice_in_dim(tile_list, vir_at * slot_dev, slot_dev, 0)
     row = sub_at * row_dev + pair_at * share_rows + jnp.arange(share_rows, dtype=jnp.int32)
@@ -234,24 +232,21 @@
         (((1,), (1,)), ((), ())),
         preferred_element_type=jnp.float32,
     )
-    lane = jnp.arange(width, dtype=jnp.int32)
-    quarter = lane // pair_count
-    swapped = (quarter == 1) | (quarter == 2)
-    own_ids = jnp.where(swapped, pair_list[0, 1], pair_list[0, 0]).astype(jnp.float32)
-    ids = jnp.where(lane % pair_count == pair_at, own_ids, 0.0)[None]
     blocks = width // pair_count
     packed_gram = local_gram.reshape(blocks, pair_count // blocks, pair_count)
     packed_gram = jnp.transpose(packed_gram, (1, 0, 2)).reshape(-1, width)
     chunk = slot_dev * row_dev // near
     near_parts = lax.all_to_all(part, "near", split_axis=0, concat_axis=0, tiled=True)
-    gram_rows = lax.psum(packed_gram, ("vir", "sub"))
+    gram_rows = lax.all_gather(packed_gram, "sub").sum(axis=0)
+    gram_rows = lax.all_gather(gram_rows, "vir").sum(axis=0)
     long_rows = chunk + 3 * GRAIN
     far_block = in_vmem(
         near_kernel,
         jax.ShapeDtypeStruct((far, long_rows, width), jnp.int16),
+        pair_list,
         near_parts,
         gram_rows,
-        ids,
+        place=place,
     )
     far_parts = lax.all_to_all(far_block, "far", split_axis=0, concat_axis=0, tiled=True)
     last_block = in_vmem(

time: 168 us -> 172 us (1.024)
  the two profiles are of different devices: /device:TPU:33 before, /device:TPU:42 now
where the time goes in v6:
time: 172 us
  blocking collectives  81.9 us (48%)
  starting transfers between devices  51.3 us (30%)
  waiting for transfers between devices  28.3 us (16%)
  Pallas kernels  6.25 us (4%)
  local copies, waits for them, and re-layouts  2.83 us (2%)
    all_to_all x1, starting transfers between devices, shards(): lax.all_to_all(share, ('far', 'near'), split_axis=0, concat_axis=0, tiled...  45.8 us
    all_to_all x1, blocking collectives, shards(): lax.all_to_all(far_block, 'far', split_axis=0, concat_axis=0, tiled=True)  33.9 us
    all_to_all x1, waiting for transfers between devices, shards(): lax.all_to_all(share, ('far', 'near'), split_axis=0, concat_axis=0, tiled...  28.3 us
    all_to_all x1, blocking collectives, shards(): lax.all_to_all(last_block, 'near', split_axis=0, concat_axis=0, tiled=True)  19.8 us
    all_gather x1, blocking collectives, shards(): own = lax.all_gather(mine, 'vir', axis=0, tiled=True)  14.3 us
    all_gather x1, blocking collectives, shards(): gram_rows = lax.all_gather(gram_rows, 'vir').sum(axis=0)  12.1 us
    all_to_all x1, starting transfers between devices, shards(): lax.all_to_all(part, 'near', split_axis=0, concat_axis=0, tiled=True)  3.59 us
    pallas_call x1, Pallas kernels, virt_partial(): pl.pallas_call(virt_kernel, out_shape=jax.ShapeDtypeStruct((near, rows //...  3.47 us
  transfers between devices with their start and end apart: 3, of which 1 were waited for; matrix products, arithmetic and copies ran while one was open for 1% of the time, Pallas kernels for 2%

profile of v6, /device:TPU:42, one launch (start us, length us, event | category | flops | bytes accessed | tf_op | source)
XLA Modules:
  0.0 171.8 jit_solution(9072624178945595453)
XLA Ops:
  0.6 0.0 copy-start.1
  0.6 14.3 %all-gather = bf16[1,36,64,128]{3,2,0,1:T(8,128)(2,1)S(1)} all-gather(bf16[1,9,64,128]{3,2,0,1:T(8,128)(2,1)} %bitcast.31), channel_id=2, replica_groups=mesh['groups'=2,'far'=4,'near'=8,'vir'=4,'sub'=2] {'vir'}, dimensions={1}, use_global_device_ids=true | all-gather | bytes 737280 | tf_op jit(solution)/shard_map/all_gather | solution.py:218
  14.9 1.9 %collective-permute-start = (bf16[36,64,128]{2,1,0:T(8,128)(2,1)S(1)}, bf16[36,64,128]{2,1,0:T(8,128)(2,1)S(1)}, u32[]{:S(2)}, u32[]{:S(2)}) collective-permute-start(bf16[36,64,128]{2,1,0:T(8,128)(2,1)S(1)} %bitcast.28), channel_id=1, source_target_pairs={{0,1},{1,0},{2,3},{3,2},{4,5},{5,4},{6,7},{7,6},{8,9},{9,8},{10,11... | collective-permute-start | bytes 1769480 | tf_op jit(solution)/shard_map/ppermute | solution.py:219
  16.9 0.0 copy-done.1
  16.9 0.1 copy.29
  17.0 0.1 reshape.78
  17.1 0.8 copy.24
  17.9 45.8 %all-to-all-start.1 = ((bf16[32,2,1152]{2,1,0:T(2,128)(2,1)}), bf16[32,2,1152]{2,1,0:T(2,128)(2,1)S(1)}, u32[]{:S(2)}, u32[]{:S(2)}) async-start(bf16[32,2,1152]{2,1,0:T(2,128)(2,1)} %copy.24), calls=%async_computation.1 | async-start | bytes 294912 | tf_op jit(solution)/shard_map/all_to_all | solution.py:217
  63.7 0.0 copy-start.2
  63.7 0.7 copy-done.2
  64.4 0.1 constant_dynamic-slice_fusion
  64.4 0.1 iota_compare_fusion
  64.5 0.1 copy.22.tiles_ref
  64.6 0.1 pad_add_fusion.place_ref
  64.7 0.1 broadcast_bitcast_fusion.1
  64.8 0.0 collective-permute-done.other_ref
  64.8 3.5 %virt_partial.1 = s16[8,80,128]{2,1,0:T(8,128)(2,1)} custom-call(s32[36,2]{1,0:T(8,128)S(1)} %copy.22.tiles_ref, s32[3]{0:T(128)S(1)} %pad_add_fusion.place_ref, bf16[36,64,128]{2,1,0:T(8,128)(2,1)S(1)} %bitcast.29, bf16[36,64,128]{2,1,0:T(8,128)(2,1)S(1)} %collective-permute-done.other_ref), custom_call_target="tpu_custom_call" | custom-call | tf_op jit(solution)/shard_map/virt_partial/pallas_call | solution.py:190
  68.2 28.3 %all-to-all-done.1 = bf16[32,2,1152]{2,1,0:T(2,128)(2,1)S(1)} async-done(((bf16[32,2,1152]{2,1,0:T(2,128)(2,1)}), bf16[32,2,1152]{2,1,0:T(2,128)(2,1)S(1)}, u32[]{:S(2)}, u32[]{:S(2)}) %all-to-all-start.1) | async-done | bytes 147488 | tf_op jit(solution)/shard_map/all_to_all | solution.py:217
  96.6 3.6 %all-to-all-start = ((s16[8,80,128]{2,1,0:T(8,128)(2,1)}), s16[8,80,128]{2,1,0:T(8,128)(2,1)S(1)}, u32[]{:S(2)}, u32[]{:S(2)}) async-start(s16[8,80,128]{2,1,0:T(8,128)(2,1)} %virt_partial.1), calls=%async_computation | async-start | bytes 327680 | tf_op jit(solution)/shard_map/all_to_all | solution.py:239
  100.2 0.1 broadcast_select_fusion
  100.3 0.1 select_n.13
  100.4 0.1 reshape.83
  100.5 0.2 convolution_bitcast_fusion
  100.7 0.1 all_gather_reshape.3
  100.8 1.8 %all_gather.13 = f32[2,8,128]{2,1,0:T(8,128)S(1)} all-gather(f32[1,8,128]{2,1,0:T(8,128)S(1)} %all_gather_reshape.3), channel_id=1, replica_groups=mesh['groups'=2,'far'=4,'near'=8,'vir'=4,'sub'=2] {'sub'}, dimensions={0}, use_global_device_ids=true | all-gather | bytes 12288 | tf_op jit(solution)/shard_map/all_gather | solution.py:240
  102.6 12.1 %all-gather.1 = f32[32,128]{1,0:T(8,128)S(1)} all-gather(f32[8,128]{1,0:T(8,128)S(1)} %reduce_sum.18), channel_id=3, replica_groups=mesh['groups'=2,'far'=4,'near'=8,'vir'=4,'sub'=2] {'vir'}, dimensions={0}, use_global_device_ids=true | all-gather | bytes 20480 | tf_op jit(solution)/shard_map/all_gather | solution.py:241
  114.7 0.0 copy-start
  114.7 0.0 all-to-all-done.parts_ref
  114.7 0.6 copy-done
  115.3 0.8 shard_map.50
  116.2 33.9 %all_to_all.20.parts_ref = s16[4,96,128]{2,1,0:T(8,128)(2,1)S(1)} all-to-all(s16[4,96,128]{2,1,0:T(8,128)(2,1)S(1)} %shard_map.50), channel_id=1, replica_groups=mesh['groups'=2,'far'=4,'near'=8,'vir'=4,'sub'=2] {'far'}, dimensions={0} | all-to-all | bytes 196608 | tf_op jit(solution)/shard_map/all_to_all | solution.py:251
  150.0 0.2 shard_map.51
  150.3 19.8 %all_to_all.21.spread_ref = s16[8,96,128]{2,1,0:T(8,128)(2,1)S(1)} all-to-all(s16[8,96,128]{2,1,0:T(8,128)(2,1)S(1)} %shard_map.51), channel_id=1, replica_groups=mesh['groups'=2,'far'=4,'near'=8,'vir'=4,'sub'=2] {'near'}, dimensions={0} | all-to-all | bytes 393216 | tf_op jit(solution)/shard_map/all_to_all | solution.py:255
  170.1 1.7 %shard_map.52 = (f32[576,128]{1,0:T(8,128)}, f32[256,256]{1,0:T(8,128)}) custom-call(s16[8,96,128]{2,1,0:T(8,128)(2,1)S(1)} %all_to_all.21.spread_ref), custom_call_target="tpu_custom_call" | custom-call | tf_op jit(solution)/shard_map/pallas_call | solution.py:135
  (7 shorter events, 0.0 us)
Async XLA Ops:
  0.6 16.3 %copy-start.1 = (bf16[1,9,64,128]{3,2,1,0:T(8,128)(2,1)S(1)}, bf16[1,9,64,128]{3,2,1,0:T(8,128)(2,1)}, u32[]{:S(2)}) copy-start(bf16[1,9,64,128]{3,2,1,0:T(8,128)(2,1)} %param.3) | copy-start | bytes 442372
  14.9 49.8 %collective-permute-start = (bf16[36,64,128]{2,1,0:T(8,128)(2,1)S(1)}, bf16[36,64,128]{2,1,0:T(8,128)(2,1)S(1)}, u32[]{:S(2)}, u32[]{:S(2)}) collective-permute-start(bf16[36,64,128]{2,1,0:T(8,128)(2,1)S(1)} %bitcast.28), channel_id=1, source_target_pairs={{0,1},{1,0},{2,3},{3,2},{4,5},{5,4},{6,7},{7,6},{8,9},{9,8},{10,11... | collective-permute-start | bytes 1769480 | tf_op jit(solution)/shard_map/ppermute | solution.py:219
  17.9 78.7 %all-to-all-start.1 = ((bf16[32,2,1152]{2,1,0:T(2,128)(2,1)}), bf16[32,2,1152]{2,1,0:T(2,128)(2,1)S(1)}, u32[]{:S(2)}, u32[]{:S(2)}) async-start(bf16[32,2,1152]{2,1,0:T(2,128)(2,1)} %copy.24), calls=%async_computation.1 | async-start | bytes 294912 | tf_op jit(solution)/shard_map/all_to_all | solution.py:217
  63.7 0.7 copy-start.2
  96.6 18.1 %all-to-all-start = ((s16[8,80,128]{2,1,0:T(8,128)(2,1)}), s16[8,80,128]{2,1,0:T(8,128)(2,1)S(1)}, u32[]{:S(2)}, u32[]{:S(2)}) async-start(s16[8,80,128]{2,1,0:T(8,128)(2,1)} %virt_partial.1), calls=%async_computation | async-start | bytes 327680 | tf_op jit(solution)/shard_map/all_to_all | solution.py:239
  114.7 0.7 copy-start

commit v7 on v6

--- a/solution.py
+++ b/solution.py
@@ -209,18 +209,26 @@
     pair_count = far * near
     vir_at = lax.axis_index("vir")
     sub_at = lax.axis_index("sub")
-    pair_at = lax.axis_index(("far", "near"))
+    spot = lax.rem(lax.axis_index(("far", "near")) + pair_count // 2, pair_count)
     mine = amplitudes[0]
     share_rows = row_dev // pair_count
     share = mine.reshape(slot_dev, pair_count, share_rows, width)
     share = jnp.transpose(share, (1, 2, 0, 3)).reshape(pair_count, share_rows, slot_dev * width)
-    got = lax.all_to_all(share, ("far", "near"), split_axis=0, concat_axis=0, tiled=True)
+    order = [(k + pair_count // 2) % pair_count for k in range(pair_count)]
+    got = lax.all_to_all(
+        share,
+        ("far", "near"),
+        split_axis=0,
+        concat_axis=0,
+        axis_index_groups=[order],
+        tiled=True,
+    )
     own = lax.all_gather(mine, "vir", axis=0, tiled=True)
     other = lax.ppermute(own, "sub", [(0, 1), (1, 0)])
-    place = jnp.stack([vir_at * slot_dev, sub_at, pair_at]).astype(jnp.int32)
+    place = jnp.stack([vir_at * slot_dev, sub_at, spot]).astype(jnp.int32)
     part = virt_partial(tile_list, place, own, other, slot_dev, near)
     own_list = lax.dynamic_slice_in_dim(tile_list, vir_at * slot_dev, slot_dev, 0)
-    row = sub_at * row_dev + pair_at * share_rows + jnp.arange(share_rows, dtype=jnp.int32)
+    row = sub_at * row_dev + spot * share_rows + jnp.arange(share_rows, dtype=jnp.int32)
     column = jnp.arange(width, dtype=jnp.int32)
     lower = column[None, None, :] <= row[:, None, None]
     diagonal = (own_list[:, 0] == own_list[:, 1])[None, :, None]

time: 172 us -> 184 us (1.070)
  the two profiles are of different devices: /device:TPU:42 before, /device:TPU:40 now
where the time goes in v7:
time: 184 us
  blocking collectives  90.9 us (49%)
  starting transfers between devices  73.3 us (40%)
  waiting for transfers between devices  9.22 us (5%)
  Pallas kernels  6.25 us (3%)
  local copies, waits for them, and re-layouts  2.83 us (2%)
    all_to_all x1, starting transfers between devices, shards(): lax.all_to_all(share, ('far', 'near'), split_axis=0, concat_axis=0, axis_...  62.8 us
    all_to_all x1, blocking collectives, shards(): lax.all_to_all(far_block, 'far', split_axis=0, concat_axis=0, tiled=True)  43.1 us
    all_to_all x1, blocking collectives, shards(): lax.all_to_all(last_block, 'near', split_axis=0, concat_axis=0, tiled=True)  19.9 us
    all_gather x1, blocking collectives, shards(): own = lax.all_gather(mine, 'vir', axis=0, tiled=True)  13.9 us
    all_gather x1, blocking collectives, shards(): gram_rows = lax.all_gather(gram_rows, 'vir').sum(axis=0)  12.2 us
    all_to_all x1, waiting for transfers between devices, shards(): lax.all_to_all(share, ('far', 'near'), split_axis=0, concat_axis=0, axis_...  9.21 us
    all_to_all x1, starting transfers between devices, shards(): lax.all_to_all(part, 'near', split_axis=0, concat_axis=0, tiled=True)  8.61 us
  transfers between devices with their start and end apart: 3, of which 1 were waited for; matrix products, arithmetic and copies ran while one was open for 1% of the time, Pallas kernels for 2%

profile of v7, /device:TPU:40, one launch (start us, length us, event | category | flops | bytes accessed | tf_op | source)
XLA Modules:
  0.0 183.8 jit_solution(14399270617337954337)
XLA Ops:
  0.6 0.0 copy-start.1
  0.6 13.9 %all-gather = bf16[1,36,64,128]{3,2,0,1:T(8,128)(2,1)S(1)} all-gather(bf16[1,9,64,128]{3,2,0,1:T(8,128)(2,1)} %bitcast.31), channel_id=2, replica_groups=mesh['groups'=2,'far'=4,'near'=8,'vir'=4,'sub'=2] {'vir'}, dimensions={1}, use_global_device_ids=true | all-gather | bytes 737280 | tf_op jit(solution)/shard_map/all_gather | solution.py:226
  14.6 1.9 %collective-permute-start = (bf16[36,64,128]{2,1,0:T(8,128)(2,1)S(1)}, bf16[36,64,128]{2,1,0:T(8,128)(2,1)S(1)}, u32[]{:S(2)}, u32[]{:S(2)}) collective-permute-start(bf16[36,64,128]{2,1,0:T(8,128)(2,1)S(1)} %bitcast.28), channel_id=1, source_target_pairs={{0,1},{1,0},{2,3},{3,2},{4,5},{5,4},{6,7},{7,6},{8,9},{9,8},{10,11... | collective-permute-start | bytes 1769480 | tf_op jit(solution)/shard_map/ppermute | solution.py:227
  16.5 0.0 copy-done.1
  16.5 0.1 copy.29
  16.6 0.1 reshape.78
  16.7 0.8 copy.24
  17.5 62.8 %all-to-all-start.1 = ((bf16[32,2,1152]{2,1,0:T(2,128)(2,1)}), bf16[32,2,1152]{2,1,0:T(2,128)(2,1)S(1)}, u32[]{:S(2)}, u32[]{:S(2)}) async-start(bf16[32,2,1152]{2,1,0:T(2,128)(2,1)} %copy.24), calls=%async_computation.1 | async-start | bytes 294912 | tf_op jit(solution)/shard_map/all_to_all | solution.py:218
  80.3 0.0 copy-start.2
  80.3 0.7 copy-done.2
  81.0 0.1 constant_dynamic-slice_fusion
  81.1 0.1 iota_compare_fusion
  81.1 0.1 copy.22.tiles_ref
  81.2 0.1 pad_add_fusion.place_ref
  81.3 0.1 broadcast_bitcast_fusion.1
  81.4 0.0 collective-permute-done.other_ref
  81.4 3.5 %virt_partial.1 = s16[8,80,128]{2,1,0:T(8,128)(2,1)} custom-call(s32[36,2]{1,0:T(8,128)S(1)} %copy.22.tiles_ref, s32[3]{0:T(128)S(1)} %pad_add_fusion.place_ref, bf16[36,64,128]{2,1,0:T(8,128)(2,1)S(1)} %bitcast.29, bf16[36,64,128]{2,1,0:T(8,128)(2,1)S(1)} %collective-permute-done.other_ref), custom_call_target="tpu_custom_call" | custom-call | tf_op jit(solution)/shard_map/virt_partial/pallas_call | solution.py:190
  84.9 9.2 %all-to-all-done.1 = bf16[32,2,1152]{2,1,0:T(2,128)(2,1)S(1)} async-done(((bf16[32,2,1152]{2,1,0:T(2,128)(2,1)}), bf16[32,2,1152]{2,1,0:T(2,128)(2,1)S(1)}, u32[]{:S(2)}, u32[]{:S(2)}) %all-to-all-start.1) | async-done | bytes 147488 | tf_op jit(solution)/shard_map/all_to_all | solution.py:218
  94.1 8.6 %all-to-all-start = ((s16[8,80,128]{2,1,0:T(8,128)(2,1)}), s16[8,80,128]{2,1,0:T(8,128)(2,1)S(1)}, u32[]{:S(2)}, u32[]{:S(2)}) async-start(s16[8,80,128]{2,1,0:T(8,128)(2,1)} %virt_partial.1), calls=%async_computation | async-start | bytes 327680 | tf_op jit(solution)/shard_map/all_to_all | solution.py:247
  102.7 0.1 broadcast_select_fusion
  102.8 0.1 select_n.13
  102.9 0.1 reshape.83
  103.0 0.2 convolution_bitcast_fusion
  103.2 0.1 all_gather_reshape.3
  103.3 1.8 %all_gather.13 = f32[2,8,128]{2,1,0:T(8,128)S(1)} all-gather(f32[1,8,128]{2,1,0:T(8,128)S(1)} %all_gather_reshape.3), channel_id=1, replica_groups=mesh['groups'=2,'far'=4,'near'=8,'vir'=4,'sub'=2] {'sub'}, dimensions={0}, use_global_device_ids=true | all-gather | bytes 12288 | tf_op jit(solution)/shard_map/all_gather | solution.py:248
  105.2 12.2 %all-gather.1 = f32[32,128]{1,0:T(8,128)S(1)} all-gather(f32[8,128]{1,0:T(8,128)S(1)} %reduce_sum.18), channel_id=3, replica_groups=mesh['groups'=2,'far'=4,'near'=8,'vir'=4,'sub'=2] {'vir'}, dimensions={0}, use_global_device_ids=true | all-gather | bytes 20480 | tf_op jit(solution)/shard_map/all_gather | solution.py:249
  117.3 0.0 copy-start
  117.3 0.0 all-to-all-done.parts_ref
  117.4 0.6 copy-done
  118.0 0.8 shard_map.50
  118.8 43.1 %all_to_all.20.parts_ref = s16[4,96,128]{2,1,0:T(8,128)(2,1)S(1)} all-to-all(s16[4,96,128]{2,1,0:T(8,128)(2,1)S(1)} %shard_map.50), channel_id=1, replica_groups=mesh['groups'=2,'far'=4,'near'=8,'vir'=4,'sub'=2] {'far'}, dimensions={0} | all-to-all | bytes 196608 | tf_op jit(solution)/shard_map/all_to_all | solution.py:259
  161.9 0.2 shard_map.51
  162.1 19.9 %all_to_all.21.spread_ref = s16[8,96,128]{2,1,0:T(8,128)(2,1)S(1)} all-to-all(s16[8,96,128]{2,1,0:T(8,128)(2,1)S(1)} %shard_map.51), channel_id=1, replica_groups=mesh['groups'=2,'far'=4,'near'=8,'vir'=4,'sub'=2] {'near'}, dimensions={0} | all-to-all | bytes 393216 | tf_op jit(solution)/shard_map/all_to_all | solution.py:263
  182.0 1.7 shard_map.52
  (7 shorter events, 0.0 us)
Async XLA Ops:
  0.6 15.9 %copy-start.1 = (bf16[1,9,64,128]{3,2,1,0:T(8,128)(2,1)S(1)}, bf16[1,9,64,128]{3,2,1,0:T(8,128)(2,1)}, u32[]{:S(2)}) copy-start(bf16[1,9,64,128]{3,2,1,0:T(8,128)(2,1)} %param.3) | copy-start | bytes 442372
  14.6 66.8 %collective-permute-start = (bf16[36,64,128]{2,1,0:T(8,128)(2,1)S(1)}, bf16[36,64,128]{2,1,0:T(8,128)(2,1)S(1)}, u32[]{:S(2)}, u32[]{:S(2)}) collective-permute-start(bf16[36,64,128]{2,1,0:T(8,128)(2,1)S(1)} %bitcast.28), channel_id=1, source_target_pairs={{0,1},{1,0},{2,3},{3,2},{4,5},{5,4},{6,7},{7,6},{8,9},{9,8},{10,11... | collective-permute-start | bytes 1769480 | tf_op jit(solution)/shard_map/ppermute | solution.py:227
  17.5 76.6 %all-to-all-start.1 = ((bf16[32,2,1152]{2,1,0:T(2,128)(2,1)}), bf16[32,2,1152]{2,1,0:T(2,128)(2,1)S(1)}, u32[]{:S(2)}, u32[]{:S(2)}) async-start(bf16[32,2,1152]{2,1,0:T(2,128)(2,1)} %copy.24), calls=%async_computation.1 | async-start | bytes 294912 | tf_op jit(solution)/shard_map/all_to_all | solution.py:218
  80.3 0.7 copy-start.2
  94.1 23.3 %all-to-all-start = ((s16[8,80,128]{2,1,0:T(8,128)(2,1)}), s16[8,80,128]{2,1,0:T(8,128)(2,1)S(1)}, u32[]{:S(2)}, u32[]{:S(2)}) async-start(s16[8,80,128]{2,1,0:T(8,128)(2,1)} %virt_partial.1), calls=%async_computation | async-start | bytes 327680 | tf_op jit(solution)/shard_map/all_to_all | solution.py:247
  117.3 0.7 copy-start

commit v8 on v6

--- a/solution.py
+++ b/solution.py
@@ -236,7 +236,7 @@
     packed_gram = local_gram.reshape(blocks, pair_count // blocks, pair_count)
     packed_gram = jnp.transpose(packed_gram, (1, 0, 2)).reshape(-1, width)
     chunk = slot_dev * row_dev // near
-    near_parts = lax.all_to_all(part, "near", split_axis=0, concat_axis=0, tiled=True)
+    near_parts = exchanged(part, "near", near // 2)
     gram_rows = lax.all_gather(packed_gram, "sub").sum(axis=0)
     gram_rows = lax.all_gather(gram_rows, "vir").sum(axis=0)
     long_rows = chunk + 3 * GRAIN
@@ -248,11 +248,11 @@
         gram_rows,
         place=place,
     )
-    far_parts = lax.all_to_all(far_block, "far", split_axis=0, concat_axis=0, tiled=True)
+    far_parts = exchanged(far_block, "far", far // 2)
     last_block = in_vmem(
         far_kernel, jax.ShapeDtypeStruct((near, long_rows, width), jnp.int16), far_parts
     )
-    spread = lax.all_to_all(last_block, "near", split_axis=0, concat_axis=0, tiled=True)
+    spread = exchanged(last_block, "near", near // 2)
     virt_rows, p_occ = in_vmem(
         finish_kernel,
         (
@@ -264,6 +264,14 @@
     return (virt_rows.reshape(slot_dev, row_dev, width), p_occ)
 
 
+def exchanged(array, axis, start):
+    size = lax.axis_size(axis)
+    order = [(start + k) % size for k in range(size)]
+    return lax.all_to_all(
+        array, axis, split_axis=0, concat_axis=0, axis_index_groups=[order], tiled=True
+    )
+
+
 def solution(mesh):
     groups, pair, vir, sub = (mesh.shape[name] for name in ("groups", "pair", "vir", "sub"))
     split = Mesh(

time: 172 us -> 164 us (0.953)
  blocking collectives: 81.9 us -> 70.3 us
  starting transfers between devices: 51.3 us -> 54.9 us
    all_to_all x2, blocking collectives: 53.7 us -> 42.1 us  [exchanged(): lax.all_to_all(array, axis, split_axis=0, concat_axis=0, axis_index_group...]
    all_to_all x1, starting transfers between devices: 3.59 us -> 7.22 us  [exchanged(): lax.all_to_all(array, axis, split_axis=0, concat_axis=0, axis_index_group...]
where the time goes in v8:
time: 164 us
  blocking collectives  70.3 us (43%)
  starting transfers between devices  54.9 us (33%)
  waiting for transfers between devices  28.3 us (17%)
  Pallas kernels  6.25 us (4%)
  local copies, waits for them, and re-layouts  2.83 us (2%)
    all_to_all x1, starting transfers between devices, shards(): lax.all_to_all(share, ('far', 'near'), split_axis=0, concat_axis=0, tiled...  45.8 us
    all_to_all x2, blocking collectives, exchanged(): lax.all_to_all(array, axis, split_axis=0, concat_axis=0, axis_index_group...  42.1 us
    all_to_all x1, waiting for transfers between devices, shards(): lax.all_to_all(share, ('far', 'near'), split_axis=0, concat_axis=0, tiled...  28.3 us
    all_gather x1, blocking collectives, shards(): own = lax.all_gather(mine, 'vir', axis=0, tiled=True)  14.3 us
    all_gather x1, blocking collectives, shards(): gram_rows = lax.all_gather(gram_rows, 'vir').sum(axis=0)  12.1 us
    all_to_all x1, starting transfers between devices, exchanged(): lax.all_to_all(array, axis, split_axis=0, concat_axis=0, axis_index_group...  7.22 us
    pallas_call x1, Pallas kernels, virt_partial(): pl.pallas_call(virt_kernel, out_shape=jax.ShapeDtypeStruct((near, rows //...  3.47 us
  transfers between devices with their start and end apart: 3, of which 1 were waited for; matrix products, arithmetic and copies ran while one was open for 1% of the time, Pallas kernels for 2%

profile of v8, /device:TPU:42, one launch (start us, length us, event | category | flops | bytes accessed | tf_op | source)
XLA Modules:
  0.0 163.9 jit_solution(8104183854423436283)
XLA Ops:
  0.6 0.0 copy-start.1
  0.6 14.3 %all-gather = bf16[1,36,64,128]{3,2,0,1:T(8,128)(2,1)S(1)} all-gather(bf16[1,9,64,128]{3,2,0,1:T(8,128)(2,1)} %bitcast.31), channel_id=2, replica_groups=mesh['groups'=2,'far'=4,'near'=8,'vir'=4,'sub'=2] {'vir'}, dimensions={1}, use_global_device_ids=true | all-gather | bytes 737280 | tf_op jit(solution)/shard_map/all_gather | solution.py:218
  14.9 1.9 %collective-permute-start = (bf16[36,64,128]{2,1,0:T(8,128)(2,1)S(1)}, bf16[36,64,128]{2,1,0:T(8,128)(2,1)S(1)}, u32[]{:S(2)}, u32[]{:S(2)}) collective-permute-start(bf16[36,64,128]{2,1,0:T(8,128)(2,1)S(1)} %bitcast.28), channel_id=1, source_target_pairs={{0,1},{1,0},{2,3},{3,2},{4,5},{5,4},{6,7},{7,6},{8,9},{9,8},{10,11... | collective-permute-start | bytes 1769480 | tf_op jit(solution)/shard_map/ppermute | solution.py:219
  16.9 0.0 copy-done.1
  16.9 0.1 copy.29
  17.0 0.1 reshape.78
  17.1 0.8 copy.24
  17.9 45.8 %all-to-all-start.1 = ((bf16[32,2,1152]{2,1,0:T(2,128)(2,1)}), bf16[32,2,1152]{2,1,0:T(2,128)(2,1)S(1)}, u32[]{:S(2)}, u32[]{:S(2)}) async-start(bf16[32,2,1152]{2,1,0:T(2,128)(2,1)} %copy.24), calls=%async_computation.1 | async-start | bytes 294912 | tf_op jit(solution)/shard_map/all_to_all | solution.py:217
  63.7 0.0 copy-start.2
  63.7 0.7 copy-done.2
  64.4 0.1 constant_dynamic-slice_fusion
  64.4 0.1 iota_compare_fusion
  64.5 0.1 copy.22.tiles_ref
  64.6 0.1 pad_add_fusion.place_ref
  64.7 0.1 broadcast_bitcast_fusion.1
  64.8 0.0 collective-permute-done.other_ref
  64.8 3.5 %virt_partial.1 = s16[8,80,128]{2,1,0:T(8,128)(2,1)} custom-call(s32[36,2]{1,0:T(8,128)S(1)} %copy.22.tiles_ref, s32[3]{0:T(128)S(1)} %pad_add_fusion.place_ref, bf16[36,64,128]{2,1,0:T(8,128)(2,1)S(1)} %bitcast.29, bf16[36,64,128]{2,1,0:T(8,128)(2,1)S(1)} %collective-permute-done.other_ref), custom_call_target="tpu_custom_call" | custom-call | tf_op jit(solution)/shard_map/virt_partial/pallas_call | solution.py:190
  68.2 28.3 %all-to-all-done.1 = bf16[32,2,1152]{2,1,0:T(2,128)(2,1)S(1)} async-done(((bf16[32,2,1152]{2,1,0:T(2,128)(2,1)}), bf16[32,2,1152]{2,1,0:T(2,128)(2,1)S(1)}, u32[]{:S(2)}, u32[]{:S(2)}) %all-to-all-start.1) | async-done | bytes 147488 | tf_op jit(solution)/shard_map/all_to_all | solution.py:217
  96.6 7.2 %all-to-all-start = ((s16[8,80,128]{2,1,0:T(8,128)(2,1)}), s16[8,80,128]{2,1,0:T(8,128)(2,1)S(1)}, u32[]{:S(2)}, u32[]{:S(2)}) async-start(s16[8,80,128]{2,1,0:T(8,128)(2,1)} %virt_partial.1), calls=%async_computation | async-start | bytes 327680 | tf_op jit(solution)/shard_map/all_to_all | solution.py:270
  103.8 0.1 broadcast_select_fusion
  103.9 0.1 select_n.13
  104.0 0.1 reshape.83
  104.1 0.2 convolution_bitcast_fusion
  104.3 0.1 all_gather_reshape.3
  104.4 1.8 %all_gather.13 = f32[2,8,128]{2,1,0:T(8,128)S(1)} all-gather(f32[1,8,128]{2,1,0:T(8,128)S(1)} %all_gather_reshape.3), channel_id=1, replica_groups=mesh['groups'=2,'far'=4,'near'=8,'vir'=4,'sub'=2] {'sub'}, dimensions={0}, use_global_device_ids=true | all-gather | bytes 12288 | tf_op jit(solution)/shard_map/all_gather | solution.py:240
  106.3 12.1 %all-gather.1 = f32[32,128]{1,0:T(8,128)S(1)} all-gather(f32[8,128]{1,0:T(8,128)S(1)} %reduce_sum.18), channel_id=3, replica_groups=mesh['groups'=2,'far'=4,'near'=8,'vir'=4,'sub'=2] {'vir'}, dimensions={0}, use_global_device_ids=true | all-gather | bytes 20480 | tf_op jit(solution)/shard_map/all_gather | solution.py:241
  118.3 0.0 copy-start
  118.3 0.0 all-to-all-done.parts_ref
  118.3 0.6 copy-done
  119.0 0.8 shard_map.50
  119.8 28.4 %all_to_all.20.parts_ref = s16[4,96,128]{2,1,0:T(8,128)(2,1)S(1)} all-to-all(s16[4,96,128]{2,1,0:T(8,128)(2,1)S(1)} %shard_map.50), channel_id=1, replica_groups={{128,192,0,64},{129,193,1,65},{130,194,2,66},{131,195,3,67},{132,196,4,..., dimensions={0} | all-to-all | bytes 196608 | tf_op jit(solution)/shard_map/all_to_all | solution.py:270
  148.1 0.2 shard_map.51
  148.4 13.7 %all_to_all.21.spread_ref = s16[8,96,128]{2,1,0:T(8,128)(2,1)S(1)} all-to-all(s16[8,96,128]{2,1,0:T(8,128)(2,1)S(1)} %shard_map.51), channel_id=1, replica_groups={{32,40,48,56,0,8,16,24},{33,41,49,57,1,9,17,25},{34,42,50,58,2,10,18,26..., dimensions={0} | all-to-all | bytes 393216 | tf_op jit(solution)/shard_map/all_to_all | solution.py:270
  162.1 1.7 %shard_map.52 = (f32[576,128]{1,0:T(8,128)}, f32[256,256]{1,0:T(8,128)}) custom-call(s16[8,96,128]{2,1,0:T(8,128)(2,1)S(1)} %all_to_all.21.spread_ref), custom_call_target="tpu_custom_call" | custom-call | tf_op jit(solution)/shard_map/pallas_call | solution.py:135
  (7 shorter events, 0.0 us)
Async XLA Ops:
  0.6 16.3 %copy-start.1 = (bf16[1,9,64,128]{3,2,1,0:T(8,128)(2,1)S(1)}, bf16[1,9,64,128]{3,2,1,0:T(8,128)(2,1)}, u32[]{:S(2)}) copy-start(bf16[1,9,64,128]{3,2,1,0:T(8,128)(2,1)} %param.3) | copy-start | bytes 442372
  14.9 49.8 %collective-permute-start = (bf16[36,64,128]{2,1,0:T(8,128)(2,1)S(1)}, bf16[36,64,128]{2,1,0:T(8,128)(2,1)S(1)}, u32[]{:S(2)}, u32[]{:S(2)}) collective-permute-start(bf16[36,64,128]{2,1,0:T(8,128)(2,1)S(1)} %bitcast.28), channel_id=1, source_target_pairs={{0,1},{1,0},{2,3},{3,2},{4,5},{5,4},{6,7},{7,6},{8,9},{9,8},{10,11... | collective-permute-start | bytes 1769480 | tf_op jit(solution)/shard_map/ppermute | solution.py:219
  17.9 78.7 %all-to-all-start.1 = ((bf16[32,2,1152]{2,1,0:T(2,128)(2,1)}), bf16[32,2,1152]{2,1,0:T(2,128)(2,1)S(1)}, u32[]{:S(2)}, u32[]{:S(2)}) async-start(bf16[32,2,1152]{2,1,0:T(2,128)(2,1)} %copy.24), calls=%async_computation.1 | async-start | bytes 294912 | tf_op jit(solution)/shard_map/all_to_all | solution.py:217
  63.7 0.7 copy-start.2
  96.6 21.8 %all-to-all-start = ((s16[8,80,128]{2,1,0:T(8,128)(2,1)}), s16[8,80,128]{2,1,0:T(8,128)(2,1)S(1)}, u32[]{:S(2)}, u32[]{:S(2)}) async-start(s16[8,80,128]{2,1,0:T(8,128)(2,1)} %virt_partial.1), calls=%async_computation | async-start | bytes 327680 | tf_op jit(solution)/shard_map/all_to_all | solution.py:270
  118.3 0.7 copy-start

commit v9 on v8

--- a/solution.py
+++ b/solution.py
@@ -10,6 +10,7 @@
 OCC = 256
 NTV = 8
 NEAR = 8
+LEAD = 2
 GRAIN = 8
 STEPS = 256.0
 TOP = 32767.0
@@ -68,19 +69,12 @@
     return (values, gram, words[count + 2 : count + 3])
 
 
-def near_kernel(place_ref, pair_ref, parts_ref, gram_ref, out_ref):
-    width = parts_ref.shape[2]
-    pair_count = width // 4
-    lane = lax.broadcasted_iota(jnp.int32, (1, width), 1)
-    quarter = lane // pair_count
-    swapped = (quarter == 1) | (quarter == 2)
-    own_ids = jnp.where(swapped, pair_ref[:, 1:2], pair_ref[:, 0:1])
-    ids = jnp.where(lane - quarter * pair_count == place_ref[2], own_ids, 0).astype(jnp.float32)
+def near_kernel(parts_ref, gram_ref, ids_ref, out_ref):
     count = parts_ref.shape[1] - GRAIN
     total, _, _ = opened(parts_ref[0], count, False)
     for k in range(1, parts_ref.shape[0]):
         total = total + opened(parts_ref[k], count, False)[0]
-    block = message(total, gram_ref[...], ids)
+    block = message(total, gram_ref[...], ids_ref[...])
     for k in range(out_ref.shape[0]):
         out_ref[k] = block
 
@@ -128,20 +122,20 @@
     occ_ref[...] = -jnp.dot(turned, inner, precision=lax.Precision.HIGHEST)
 
 
-def in_vmem(kernel, out_shape, *operands, place=None):
+def in_vmem(kernel, out_shape, *operands):
     vmem = pl.BlockSpec(memory_space=pltpu.VMEM)
-    smem = pl.BlockSpec(memory_space=pltpu.SMEM)
-    places = () if place is None else (place,)
     return pl.pallas_call(
         kernel,
         out_shape=out_shape,
-        in_specs=[smem] * len(places) + [vmem] * len(operands),
+        in_specs=[vmem] * len(operands),
         out_specs=jax.tree.map(lambda _: vmem, out_shape),
         compiler_params=pltpu.CompilerParams(vmem_limit_bytes=8 * 1024 * 1024),
-    )(*places, *operands)
-
-
-def virt_kernel(tiles_ref, place_ref, own_ref, other_ref, out_ref, whole_ref, part_ref, slot_ref):
+    )(*operands)
+
+
+def virt_kernel(
+    tiles_ref, place_ref, pair_ref, own_ref, other_ref, out_ref, ids_ref, whole_ref, part_ref, slot_ref
+):
     slot_count, half_rows, width = own_ref.shape
     own_count = part_ref.shape[0] // half_rows
     first = place_ref[0]
@@ -180,18 +174,28 @@
     chunk = part_ref.shape[0] // out_ref.shape[0]
     for k in range(out_ref.shape[0]):
         out_ref[k] = message(part_ref[k * chunk : (k + 1) * chunk])
-
-
-def virt_partial(tile_list, place, own, other, own_count, near):
+    pair_count = width // 4
+    lane = lax.broadcasted_iota(jnp.int32, (1, width), 1)
+    quarter = lane // pair_count
+    swapped = (quarter == 1) | (quarter == 2)
+    own_ids = jnp.where(swapped, pair_ref[:, 1:2], pair_ref[:, 0:1])
+    here = lane - quarter * pair_count == place_ref[2]
+    ids_ref[...] = jnp.where(here, own_ids, 0).astype(jnp.float32)
+
+
+def virt_partial(tile_list, place, pair_list, own, other, own_count, near):
     _, half_rows, width = own.shape
     rows = own_count * half_rows
     smem = pl.BlockSpec(memory_space=pltpu.SMEM)
     vmem = pl.BlockSpec(memory_space=pltpu.VMEM)
     return pl.pallas_call(
         virt_kernel,
-        out_shape=jax.ShapeDtypeStruct((near, rows // near + GRAIN, width), jnp.int16),
-        in_specs=[smem, smem, vmem, vmem],
-        out_specs=vmem,
+        out_shape=(
+            jax.ShapeDtypeStruct((near, rows // near + GRAIN, width), jnp.int16),
+            jax.ShapeDtypeStruct((1, width), jnp.float32),
+        ),
+        in_specs=[smem, smem, vmem, vmem, vmem],
+        out_specs=(vmem, vmem),
         scratch_shapes=[
             pltpu.VMEM((NTV, width, NTV * width), jnp.bfloat16),
             pltpu.VMEM((rows, width), jnp.float32),
@@ -199,7 +203,7 @@
         ],
         compiler_params=pltpu.CompilerParams(vmem_limit_bytes=24 * 1024 * 1024),
         name="virt_partial",
-    )(tile_list, place, own, other)
+    )(tile_list, place, pair_list, own, other)
 
 
 def shards(amplitudes, pair_list, tile_list):
@@ -209,16 +213,24 @@
     pair_count = far * near
     vir_at = lax.axis_index("vir")
     sub_at = lax.axis_index("sub")
-    pair_at = lax.axis_index(("far", "near"))
+    pair_at = lax.rem(lax.axis_index(("far", "near")) + LEAD, pair_count)
     mine = amplitudes[0]
     share_rows = row_dev // pair_count
     share = mine.reshape(slot_dev, pair_count, share_rows, width)
     share = jnp.transpose(share, (1, 2, 0, 3)).reshape(pair_count, share_rows, slot_dev * width)
-    got = lax.all_to_all(share, ("far", "near"), split_axis=0, concat_axis=0, tiled=True)
+    order = [(k + pair_count - LEAD) % pair_count for k in range(pair_count)]
+    got = lax.all_to_all(
+        share,
+        ("far", "near"),
+        split_axis=0,
+        concat_axis=0,
+        axis_index_groups=[order],
+        tiled=True,
+    )
     own = lax.all_gather(mine, "vir", axis=0, tiled=True)
     other = lax.ppermute(own, "sub", [(0, 1), (1, 0)])
     place = jnp.stack([vir_at * slot_dev, sub_at, pair_at]).astype(jnp.int32)
-    part = virt_partial(tile_list, place, own, other, slot_dev, near)
+    part, ids = virt_partial(tile_list, place, pair_list, own, other, slot_dev, near)
     own_list = lax.dynamic_slice_in_dim(tile_list, vir_at * slot_dev, slot_dev, 0)
     row = sub_at * row_dev + pair_at * share_rows + jnp.arange(share_rows, dtype=jnp.int32)
     column = jnp.arange(width, dtype=jnp.int32)
@@ -237,16 +249,14 @@
     packed_gram = jnp.transpose(packed_gram, (1, 0, 2)).reshape(-1, width)
     chunk = slot_dev * row_dev // near
     near_parts = exchanged(part, "near", near // 2)
-    gram_rows = lax.all_gather(packed_gram, "sub").sum(axis=0)
-    gram_rows = lax.all_gather(gram_rows, "vir").sum(axis=0)
+    gram_rows = lax.psum(packed_gram, ("vir", "sub"))
     long_rows = chunk + 3 * GRAIN
     far_block = in_vmem(
         near_kernel,
         jax.ShapeDtypeStruct((far, long_rows, width), jnp.int16),
-        pair_list,
         near_parts,
         gram_rows,
-        place=place,
+        ids,
     )
     far_parts = exchanged(far_block, "far", far // 2)
     last_block = in_vmem(

time: 164 us -> 146 us (0.89)
  the two profiles are of different devices: /device:TPU:42 before, /device:TPU:40 now
where the time goes in v9:
time: 146 us; the launch traced here: 145 us
  blocking collectives  70.8 us (48%)
  starting transfers between devices  56.2 us (38%)
  waiting for transfers between devices  8.19 us (6%)
  Pallas kernels  5.71 us (4%)
  local copies, waits for them, and re-layouts  3.1 us (2%)
    all_to_all x1, starting transfers between devices, shards(): lax.all_to_all(share, ('far', 'near'), split_axis=0, concat_axis=0, axis_...  46.9 us
    all_to_all x2, blocking collectives, exchanged(): lax.all_to_all(array, axis, split_axis=0, concat_axis=0, axis_index_group...  43.7 us
    all_gather x1, blocking collectives, shards(): own = lax.all_gather(mine, 'vir', axis=0, tiled=True)  13.6 us
    psum x1, blocking collectives, shards(): gram_rows = lax.psum(packed_gram, ('vir', 'sub'))  13.6 us
    all_to_all x1, starting transfers between devices, exchanged(): lax.all_to_all(array, axis, split_axis=0, concat_axis=0, axis_index_group...  7.33 us
    all_to_all x1, waiting for transfers between devices, shards(): lax.all_to_all(share, ('far', 'near'), split_axis=0, concat_axis=0, axis_...  7.27 us
    pallas_call x1, Pallas kernels, virt_partial(): pl.pallas_call(virt_kernel, out_shape=(jax.ShapeDtypeStruct((near, rows /...  3.47 us
  transfers between devices with their start and end apart: 3, of which 2 were waited for; matrix products, arithmetic and copies ran while one was open for 1% of the time, Pallas kernels for 2%

profile of v9, /device:TPU:40, one launch (start us, length us, event | category | flops | bytes accessed | tf_op | source)
XLA Modules:
  0.0 145.2 jit_solution(5286057959753139377)
XLA Ops:
  0.6 1.0 copy.25
  1.7 0.1 reshape.81
  1.7 0.8 copy.20
  2.5 0.0 copy-start.1
  2.5 46.9 %all-to-all-start.1 = ((bf16[32,2,1152]{2,1,0:T(2,128)(2,1)}), bf16[32,2,1152]{2,1,0:T(2,128)(2,1)S(1)}, u32[]{:S(2)}, u32[]{:S(2)}) async-start(bf16[32,2,1152]{2,1,0:T(2,128)(2,1)} %copy.20), calls=%async_computation.1 | async-start | bytes 294912 | tf_op jit(solution)/shard_map/all_to_all | solution.py:222
  49.4 0.0 copy-done.1
  49.4 13.6 %all-gather = bf16[1,36,64,128]{3,2,0,1:T(8,128)(2,1)S(1)} all-gather(bf16[1,9,64,128]{3,2,0,1:T(8,128)(2,1)S(1)} %bitcast.30), channel_id=2, replica_groups=mesh['groups'=2,'far'=4,'near'=8,'vir'=4,'sub'=2] {'vir'}, dimensions={1}, use_global_device_ids=true | all-gather | bytes 737280 | tf_op jit(solution)/shard_map/all_gather | solution.py:230
  63.0 1.9 %collective-permute-start = (bf16[36,64,128]{2,1,0:T(8,128)(2,1)S(1)}, bf16[36,64,128]{2,1,0:T(8,128)(2,1)S(1)}, u32[]{:S(2)}, u32[]{:S(2)}) collective-permute-start(bf16[36,64,128]{2,1,0:T(8,128)(2,1)S(1)} %bitcast.26), channel_id=1, source_target_pairs={{0,1},{1,0},{2,3},{3,2},{4,5},{5,4},{6,7},{7,6},{8,9},{9,8},{10,11... | collective-permute-start | bytes 1769480 | tf_op jit(solution)/shard_map/ppermute | solution.py:231
  65.0 0.1 iota_compare_fusion
  65.0 0.1 pad_add_fusion.place_ref
  65.1 0.0 copy-start.2
  65.1 0.7 copy-done.2
  65.8 0.1 copy.18.tiles_ref
  65.9 0.1 constant_dynamic-slice_fusion
  66.0 0.0 copy-start
  66.0 0.9 collective-permute-done.other_ref
  66.9 0.0 copy-done
  66.9 3.5 %virt_partial.1 = (s16[8,80,128]{2,1,0:T(8,128)(2,1)}, f32[1,128]{1,0:T(1,128)S(1)}) custom-call(s32[36,2]{1,0:T(8,128)S(1)} %copy.18.tiles_ref, s32[3]{0:T(128)S(1)} %pad_add_fusion.place_ref, s32[1,2]{1,0:T(1,128)S(1)} %copy-done, bf16[36,64,128]{2,1,0:T(8,128)(2,1)S(1)} %bitcast.27, bf16[36,64,128]{2,1,0:T(8,128)(2,1)S(1)} %collective-permute-done.other_ref), custom_call_target="tpu_custom_call" | custom-call | tf_op jit(solution)/shard_map/virt_partial/pallas_call | solution.py:191
  70.4 7.3 %all-to-all-done.1 = bf16[32,2,1152]{2,1,0:T(2,128)(2,1)S(1)} async-done(((bf16[32,2,1152]{2,1,0:T(2,128)(2,1)}), bf16[32,2,1152]{2,1,0:T(2,128)(2,1)S(1)}, u32[]{:S(2)}, u32[]{:S(2)}) %all-to-all-start.1) | async-done | bytes 147488 | tf_op jit(solution)/shard_map/all_to_all | solution.py:222
  77.7 7.3 %all-to-all-start = ((s16[8,80,128]{2,1,0:T(8,128)(2,1)}), s16[8,80,128]{2,1,0:T(8,128)(2,1)S(1)}, u32[]{:S(2)}, u32[]{:S(2)}) async-start(s16[8,80,128]{2,1,0:T(8,128)(2,1)} %get-tuple-element.6), calls=%async_computation | async-start | bytes 327680 | tf_op jit(solution)/shard_map/all_to_all | solution.py:280
  85.0 0.1 broadcast_bitcast_fusion.1
  85.1 0.1 broadcast_select_fusion
  85.2 0.1 select_n.13
  85.3 0.1 reshape.86
  85.4 0.2 convolution_bitcast_fusion
  85.6 0.1 reshape.83
  85.7 13.6 %psum.7.gram_ref = f32[8,128]{1,0:T(8,128)S(1)} all-reduce(f32[8,128]{1,0:T(8,128)S(1)} %reshape.83), channel_id=1, replica_groups=mesh['groups'=2,'far'=4,'near'=8,'vir'=4,'sub'=2] {'vir','sub'}, use_global_device_ids=true, to_apply=%region_0.1 | all-reduce | flops 1024 | bytes 8192 | tf_op jit(solution)/shard_map/psum | solution.py:252
  99.2 0.0 all-to-all-done.parts_ref
  99.2 0.3 shard_map.50
  99.5 30.0 %all_to_all.20.parts_ref = s16[4,96,128]{2,1,0:T(8,128)(2,1)S(1)} all-to-all(s16[4,96,128]{2,1,0:T(8,128)(2,1)S(1)} %shard_map.50), channel_id=1, replica_groups={{128,192,0,64},{129,193,1,65},{130,194,2,66},{131,195,3,67},{132,196,4,..., dimensions={0} | all-to-all | bytes 196608 | tf_op jit(solution)/shard_map/all_to_all | solution.py:280
  129.5 0.2 shard_map.51
  129.7 13.7 %all_to_all.21.spread_ref = s16[8,96,128]{2,1,0:T(8,128)(2,1)S(1)} all-to-all(s16[8,96,128]{2,1,0:T(8,128)(2,1)S(1)} %shard_map.51), channel_id=1, replica_groups={{32,40,48,56,0,8,16,24},{33,41,49,57,1,9,17,25},{34,42,50,58,2,10,18,26..., dimensions={0} | all-to-all | bytes 393216 | tf_op jit(solution)/shard_map/all_to_all | solution.py:280
  143.5 1.7 %shard_map.52 = (f32[576,128]{1,0:T(8,128)}, f32[256,256]{1,0:T(8,128)}) custom-call(s16[8,96,128]{2,1,0:T(8,128)(2,1)S(1)} %all_to_all.21.spread_ref), custom_call_target="tpu_custom_call" | custom-call | tf_op jit(solution)/shard_map/pallas_call | solution.py:127
  (5 shorter events, 0.0 us)
Async XLA Ops:
  2.5 46.9 %copy-start.1 = (bf16[1,9,64,128]{3,2,1,0:T(8,128)(2,1)S(1)}, bf16[1,9,64,128]{3,2,1,0:T(8,128)(2,1)}, u32[]{:S(2)}) copy-start(bf16[1,9,64,128]{3,2,1,0:T(8,128)(2,1)} %param.3) | copy-start | bytes 442372
  2.5 75.1 %all-to-all-start.1 = ((bf16[32,2,1152]{2,1,0:T(2,128)(2,1)}), bf16[32,2,1152]{2,1,0:T(2,128)(2,1)S(1)}, u32[]{:S(2)}, u32[]{:S(2)}) async-start(bf16[32,2,1152]{2,1,0:T(2,128)(2,1)} %copy.20), calls=%async_computation.1 | async-start | bytes 294912 | tf_op jit(solution)/shard_map/all_to_all | solution.py:222
  63.0 3.9 %collective-permute-start = (bf16[36,64,128]{2,1,0:T(8,128)(2,1)S(1)}, bf16[36,64,128]{2,1,0:T(8,128)(2,1)S(1)}, u32[]{:S(2)}, u32[]{:S(2)}) collective-permute-start(bf16[36,64,128]{2,1,0:T(8,128)(2,1)S(1)} %bitcast.26), channel_id=1, source_target_pairs={{0,1},{1,0},{2,3},{3,2},{4,5},{5,4},{6,7},{7,6},{8,9},{9,8},{10,11... | collective-permute-start | bytes 1769480 | tf_op jit(solution)/shard_map/ppermute | solution.py:231
  65.1 0.7 copy-start.2
  66.0 0.9 copy-start
  77.7 21.6 %all-to-all-start = ((s16[8,80,128]{2,1,0:T(8,128)(2,1)}), s16[8,80,128]{2,1,0:T(8,128)(2,1)S(1)}, u32[]{:S(2)}, u32[]{:S(2)}) async-start(s16[8,80,128]{2,1,0:T(8,128)(2,1)} %get-tuple-element.6), calls=%async_computation | async-start | bytes 327680 | tf_op jit(solution)/shard_map/all_to_all | solution.py:280

commit v10 on v9

--- a/solution.py
+++ b/solution.py
@@ -20,7 +20,7 @@
 def coded(values):
     largest = jnp.max(jnp.abs(values), axis=1, keepdims=True)
     k = jnp.floor(jnp.log2(jnp.maximum(largest, FLOOR)) * STEPS) + 2.0
-    return (values * (jnp.exp2(k * (-1.0 / STEPS)) * TOP), k)
+    return (values * jnp.exp2(k * (-1.0 / STEPS)) * TOP, k)
 
 
 def rounded(values):
@@ -40,7 +40,7 @@
 
 
 def scale_of(row, count):
-    return jnp.exp2(as_column(row, count) * (1.0 / STEPS)) * (1.0 / TOP)
+    return jnp.exp2(as_column(row, count) * (1.0 / STEPS))
 
 
 def message(values, gram=None, ids=None):
@@ -60,12 +60,12 @@
 
 def opened(block, count, with_gram):
     words = block.astype(jnp.int32).astype(jnp.float32)
-    values = words[:count] * scale_of(words[count : count + 1], count)
+    values = words[:count] * (1.0 / TOP) * scale_of(words[count : count + 1], count)
     if not with_gram:
         return (values, None, None)
     high = words[count + GRAIN : count + 2 * GRAIN]
     low = words[count + 2 * GRAIN : count + 3 * GRAIN]
-    gram = (high + low * (1.0 / TOP)) * scale_of(words[count + 1 : count + 2], GRAIN)
+    gram = (high + low * (1.0 / TOP)) * (1.0 / TOP) * scale_of(words[count + 1 : count + 2], GRAIN)
     return (values, gram, words[count + 2 : count + 3])
 
 
@@ -217,7 +217,7 @@
     mine = amplitudes[0]
     share_rows = row_dev // pair_count
     share = mine.reshape(slot_dev, pair_count, share_rows, width)
-    share = jnp.transpose(share, (1, 2, 0, 3)).reshape(pair_count, share_rows, slot_dev * width)
+    share = jnp.transpose(share, (1, 0, 2, 3))
     order = [(k + pair_count - LEAD) % pair_count for k in range(pair_count)]
     got = lax.all_to_all(
         share,
@@ -234,9 +234,9 @@
     own_list = lax.dynamic_slice_in_dim(tile_list, vir_at * slot_dev, slot_dev, 0)
     row = sub_at * row_dev + pair_at * share_rows + jnp.arange(share_rows, dtype=jnp.int32)
     column = jnp.arange(width, dtype=jnp.int32)
-    lower = column[None, None, :] <= row[:, None, None]
-    diagonal = (own_list[:, 0] == own_list[:, 1])[None, :, None]
-    keep = jnp.logical_not(diagonal & lower).reshape(1, share_rows * slot_dev * width)
+    lower = column[None, None, :] <= row[None, :, None]
+    diagonal = (own_list[:, 0] == own_list[:, 1])[:, None, None]
+    keep = jnp.logical_not(diagonal & lower).reshape(1, slot_dev * share_rows * width)
     rows = got.reshape(pair_count, share_rows * slot_dev * width)
     local_gram = lax.dot_general(
         jnp.where(keep, rows, jnp.zeros((), rows.dtype)),

time: 146 us -> 145 us (level)
  no operation moved by 1% of the time
where the time goes in v10:
time: 145 us
  blocking collectives  70.8 us (49%)
  starting transfers between devices  56.1 us (39%)
  waiting for transfers between devices  8.3 us (6%)
  Pallas kernels  5.72 us (4%)
  local copies, waits for them, and re-layouts  2.74 us (2%)
    all_to_all x1, starting transfers between devices, shards(): lax.all_to_all(share, ('far', 'near'), split_axis=0, concat_axis=0, axis_...  46.9 us
    all_to_all x2, blocking collectives, exchanged(): lax.all_to_all(array, axis, split_axis=0, concat_axis=0, axis_index_group...  43.7 us
    all_gather x1, blocking collectives, shards(): own = lax.all_gather(mine, 'vir', axis=0, tiled=True)  13.6 us
    psum x1, blocking collectives, shards(): gram_rows = lax.psum(packed_gram, ('vir', 'sub'))  13.6 us
    all_to_all x1, starting transfers between devices, exchanged(): lax.all_to_all(array, axis, split_axis=0, concat_axis=0, axis_index_group...  7.33 us
    all_to_all x1, waiting for transfers between devices, shards(): lax.all_to_all(share, ('far', 'near'), split_axis=0, concat_axis=0, axis_...  7.26 us
    pallas_call x1, Pallas kernels, virt_partial(): pl.pallas_call(virt_kernel, out_shape=(jax.ShapeDtypeStruct((near, rows /...  3.47 us
  transfers between devices with their start and end apart: 3, of which 2 were waited for; matrix products, arithmetic and copies ran while one was open for 1% of the time, Pallas kernels for 2%

profile of v10, /device:TPU:40, one launch (start us, length us, event | category | flops | bytes accessed | tf_op | source)
XLA Modules:
  0.0 145.0 jit_solution(14672575640999960020)
XLA Ops:
  0.6 1.7 %copy.13 = bf16[9,32,2,128]{3,2,0,1:T(2,128)(2,1)} copy(bf16[9,32,2,128]{3,2,1,0:T(2,128)(2,1)} %bitcast.18) | data formatting | bytes 294912 | tf_op jit(solution)/shard_map/reshape;squeeze | solution.py:219
  2.3 0.0 copy-start.1
  2.3 46.9 %all-to-all-start.1 = ((bf16[32,9,2,128]{3,2,1,0:T(2,128)(2,1)}), bf16[32,9,2,128]{3,2,1,0:T(2,128)(2,1)S(1)}, u32[]{:S(2)}, u32[]{:S(2)}) async-start(bf16[32,9,2,128]{3,2,1,0:T(2,128)(2,1)} %bitcast.15), calls=%async_computation.1 | async-start | bytes 294912 | tf_op jit(solution)/shard_map/all_to_all | solution.py:222
  49.2 0.0 copy-done.1
  49.2 13.6 %all-gather = bf16[1,36,64,128]{3,2,0,1:T(8,128)(2,1)S(1)} all-gather(bf16[1,9,64,128]{3,2,0,1:T(8,128)(2,1)S(1)} %bitcast.19), channel_id=2, replica_groups=mesh['groups'=2,'far'=4,'near'=8,'vir'=4,'sub'=2] {'vir'}, dimensions={1}, use_global_device_ids=true | all-gather | bytes 737280 | tf_op jit(solution)/shard_map/all_gather | solution.py:230
  62.8 1.9 %collective-permute-start = (bf16[36,64,128]{2,1,0:T(8,128)(2,1)S(1)}, bf16[36,64,128]{2,1,0:T(8,128)(2,1)S(1)}, u32[]{:S(2)}, u32[]{:S(2)}) collective-permute-start(bf16[36,64,128]{2,1,0:T(8,128)(2,1)S(1)} %bitcast.16), channel_id=1, source_target_pairs={{0,1},{1,0},{2,3},{3,2},{4,5},{5,4},{6,7},{7,6},{8,9},{9,8},{10,11... | collective-permute-start | bytes 1769480 | tf_op jit(solution)/shard_map/ppermute | solution.py:231
  64.7 0.0 copy-start.2
  64.7 0.7 copy-done.2
  65.4 0.1 copy.9.tiles_ref
  65.5 0.1 pad_add_fusion.place_ref
  65.6 0.0 copy-start
  65.6 0.1 constant_dynamic-slice_fusion
  65.7 1.0 collective-permute-done.other_ref
  66.7 0.0 copy-done
  66.7 3.5 %virt_partial.1 = (s16[8,80,128]{2,1,0:T(8,128)(2,1)}, f32[1,128]{1,0:T(1,128)S(1)}) custom-call(s32[36,2]{1,0:T(8,128)S(1)} %copy.9.tiles_ref, s32[3]{0:T(128)S(1)} %pad_add_fusion.place_ref, s32[1,2]{1,0:T(1,128)S(1)} %copy-done, bf16[36,64,128]{2,1,0:T(8,128)(2,1)S(1)} %bitcast.17, bf16[36,64,128]{2,1,0:T(8,128)(2,1)S(1)} %collective-permute-done.other_ref), custom_call_target="tpu_custom_call" | custom-call | tf_op jit(solution)/shard_map/virt_partial/pallas_call | solution.py:191
  70.2 7.3 %all-to-all-done.1 = bf16[32,9,2,128]{3,2,1,0:T(2,128)(2,1)S(1)} async-done(((bf16[32,9,2,128]{3,2,1,0:T(2,128)(2,1)}), bf16[32,9,2,128]{3,2,1,0:T(2,128)(2,1)S(1)}, u32[]{:S(2)}, u32[]{:S(2)}) %all-to-all-start.1) | async-done | bytes 147488 | tf_op jit(solution)/shard_map/all_to_all | solution.py:222
  77.4 7.3 %all-to-all-start = ((s16[8,80,128]{2,1,0:T(8,128)(2,1)}), s16[8,80,128]{2,1,0:T(8,128)(2,1)S(1)}, u32[]{:S(2)}, u32[]{:S(2)}) async-start(s16[8,80,128]{2,1,0:T(8,128)(2,1)} %get-tuple-element.6), calls=%async_computation | async-start | bytes 327680 | tf_op jit(solution)/shard_map/all_to_all | solution.py:280
  84.8 0.1 iota_compare_fusion
  84.9 0.1 and_not_fusion
  84.9 0.1 broadcast_select_fusion
  85.1 0.1 select_n.13
  85.1 0.1 reshape.80
  85.2 0.2 convolution_bitcast_fusion
  85.4 0.1 reshape.77
  85.5 13.6 %psum.7.gram_ref = f32[8,128]{1,0:T(8,128)S(1)} all-reduce(f32[8,128]{1,0:T(8,128)S(1)} %reshape.77), channel_id=1, replica_groups=mesh['groups'=2,'far'=4,'near'=8,'vir'=4,'sub'=2] {'vir','sub'}, use_global_device_ids=true, to_apply=%region_0.1 | all-reduce | flops 1024 | bytes 8192 | tf_op jit(solution)/shard_map/psum | solution.py:252
  99.0 0.0 all-to-all-done.parts_ref
  99.0 0.3 shard_map.50
  99.3 30.0 %all_to_all.20.parts_ref = s16[4,96,128]{2,1,0:T(8,128)(2,1)S(1)} all-to-all(s16[4,96,128]{2,1,0:T(8,128)(2,1)S(1)} %shard_map.50), channel_id=1, replica_groups={{128,192,0,64},{129,193,1,65},{130,194,2,66},{131,195,3,67},{132,196,4,..., dimensions={0} | all-to-all | bytes 196608 | tf_op jit(solution)/shard_map/all_to_all | solution.py:280
  129.3 0.2 shard_map.51
  129.5 13.7 %all_to_all.21.spread_ref = s16[8,96,128]{2,1,0:T(8,128)(2,1)S(1)} all-to-all(s16[8,96,128]{2,1,0:T(8,128)(2,1)S(1)} %shard_map.51), channel_id=1, replica_groups={{32,40,48,56,0,8,16,24},{33,41,49,57,1,9,17,25},{34,42,50,58,2,10,18,26..., dimensions={0} | all-to-all | bytes 393216 | tf_op jit(solution)/shard_map/all_to_all | solution.py:280
  143.3 1.7 %shard_map.52 = (f32[576,128]{1,0:T(8,128)}, f32[256,256]{1,0:T(8,128)}) custom-call(s16[8,96,128]{2,1,0:T(8,128)(2,1)S(1)} %all_to_all.21.spread_ref), custom_call_target="tpu_custom_call" | custom-call | tf_op jit(solution)/shard_map/pallas_call | solution.py:127
  (3 shorter events, 0.0 us)
Async XLA Ops:
  2.3 46.9 %copy-start.1 = (bf16[1,9,64,128]{3,2,1,0:T(8,128)(2,1)S(1)}, bf16[1,9,64,128]{3,2,1,0:T(8,128)(2,1)}, u32[]{:S(2)}) copy-start(bf16[1,9,64,128]{3,2,1,0:T(8,128)(2,1)} %param.3) | copy-start | bytes 442372
  2.3 75.1 %all-to-all-start.1 = ((bf16[32,9,2,128]{3,2,1,0:T(2,128)(2,1)}), bf16[32,9,2,128]{3,2,1,0:T(2,128)(2,1)S(1)}, u32[]{:S(2)}, u32[]{:S(2)}) async-start(bf16[32,9,2,128]{3,2,1,0:T(2,128)(2,1)} %bitcast.15), calls=%async_computation.1 | async-start | bytes 294912 | tf_op jit(solution)/shard_map/all_to_all | solution.py:222
  62.8 3.9 %collective-permute-start = (bf16[36,64,128]{2,1,0:T(8,128)(2,1)S(1)}, bf16[36,64,128]{2,1,0:T(8,128)(2,1)S(1)}, u32[]{:S(2)}, u32[]{:S(2)}) collective-permute-start(bf16[36,64,128]{2,1,0:T(8,128)(2,1)S(1)} %bitcast.16), channel_id=1, source_target_pairs={{0,1},{1,0},{2,3},{3,2},{4,5},{5,4},{6,7},{7,6},{8,9},{9,8},{10,11... | collective-permute-start | bytes 1769480 | tf_op jit(solution)/shard_map/ppermute | solution.py:231
  64.7 0.7 copy-start.2
  65.6 1.1 copy-start
  77.4 21.6 %all-to-all-start = ((s16[8,80,128]{2,1,0:T(8,128)(2,1)}), s16[8,80,128]{2,1,0:T(8,128)(2,1)S(1)}, u32[]{:S(2)}, u32[]{:S(2)}) async-start(s16[8,80,128]{2,1,0:T(8,128)(2,1)} %get-tuple-element.6), calls=%async_computation | async-start | bytes 327680 | tf_op jit(solution)/shard_map/all_to_all | solution.py:280

commit v11 on v10

--- a/solution.py
+++ b/solution.py
@@ -92,16 +92,26 @@
         out_ref[k] = block
 
 
-def finish_kernel(spread_ref, virt_ref, occ_ref):
-    near, _, width = spread_ref.shape
+def finish_kernel(spread_ref, virt_ref, gram_ref, ids_ref):
+    near, _, _ = spread_ref.shape
     chunk = virt_ref.shape[0] // near
-    pair_count = width // 4
     packed, ids = 0.0, 0.0
     for k in range(near):
         values, gram, some_ids = opened(spread_ref[k], chunk, True)
         virt_ref[k * chunk : (k + 1) * chunk] = values
         packed = packed + gram
         ids = ids + some_ids
+    gram_ref[...] = packed
+    ids_ref[...] = ids
+
+
+def occ_kernel(both_ref, ids_ref, occ_ref):
+    packed = both_ref[0]
+    for k in range(1, both_ref.shape[0]):
+        packed = packed + both_ref[k]
+    ids = ids_ref[...]
+    width = ids.shape[1]
+    pair_count = width // 4
     gram = jnp.concatenate(
         [packed[:, k : k + pair_count] for k in range(0, width, pair_count)], axis=0
     )
@@ -249,7 +259,7 @@
     packed_gram = jnp.transpose(packed_gram, (1, 0, 2)).reshape(-1, width)
     chunk = slot_dev * row_dev // near
     near_parts = exchanged(part, "near", near // 2)
-    gram_rows = lax.psum(packed_gram, ("vir", "sub"))
+    gram_rows = lax.psum(packed_gram, "vir")
     long_rows = chunk + 3 * GRAIN
     far_block = in_vmem(
         near_kernel,
@@ -263,14 +273,17 @@
         far_kernel, jax.ShapeDtypeStruct((near, long_rows, width), jnp.int16), far_parts
     )
     spread = exchanged(last_block, "near", near // 2)
-    virt_rows, p_occ = in_vmem(
+    virt_rows, gram_part, all_ids = in_vmem(
         finish_kernel,
         (
             jax.ShapeDtypeStruct((near * chunk, width), jnp.float32),
-            jax.ShapeDtypeStruct((OCC, OCC), jnp.float32),
+            jax.ShapeDtypeStruct((GRAIN, width), jnp.float32),
+            jax.ShapeDtypeStruct((1, width), jnp.float32),
         ),
         spread,
     )
+    both = lax.all_gather(gram_part, "sub")
+    p_occ = in_vmem(occ_kernel, jax.ShapeDtypeStruct((OCC, OCC), jnp.float32), both, all_ids)
     return (virt_rows.reshape(slot_dev, row_dev, width), p_occ)
 
 

time: 145 us -> 143 us (0.986)
  the two profiles are of different devices: /device:TPU:40 before, /device:TPU:33 now
where the time goes in v11:
time: 143 us
  blocking collectives  67.8 us (47%)
  starting transfers between devices  59.3 us (41%)
  Pallas kernels  6.45 us (5%)
  waiting for transfers between devices  5.34 us (4%)
  local copies, waits for them, and re-layouts  2.74 us (2%)
    all_to_all x1, starting transfers between devices, shards(): lax.all_to_all(share, ('far', 'near'), split_axis=0, concat_axis=0, axis_...  47.4 us
    all_to_all x2, blocking collectives, exchanged(): lax.all_to_all(array, axis, split_axis=0, concat_axis=0, axis_index_group...  37.7 us
    all_gather x1, blocking collectives, shards(): own = lax.all_gather(mine, 'vir', axis=0, tiled=True)  12.4 us
    psum x1, blocking collectives, shards(): gram_rows = lax.psum(packed_gram, 'vir')  9.16 us
    all_gather x1, blocking collectives, shards(): both = lax.all_gather(gram_part, 'sub')  8.5 us
    all_to_all x1, starting transfers between devices, exchanged(): lax.all_to_all(array, axis, split_axis=0, concat_axis=0, axis_index_group...  7.85 us
    all_to_all x1, waiting for transfers between devices, shards(): lax.all_to_all(share, ('far', 'near'), split_axis=0, concat_axis=0, axis_...  4.67 us
    ppermute x1, starting transfers between devices, shards(): other = lax.ppermute(own, 'sub', [(0, 1), (1, 0)])  3.99 us
  transfers between devices with their start and end apart: 3, of which 2 were waited for; matrix products, arithmetic and copies ran while one was open for 1% of the time, Pallas kernels for 2%

profile of v11, /device:TPU:33, one launch (start us, length us, event | category | flops | bytes accessed | tf_op | source)
XLA Modules:
  0.0 142.8 jit_solution(8515731603669857779)
XLA Ops:
  0.6 1.7 %copy.13 = bf16[9,32,2,128]{3,2,0,1:T(2,128)(2,1)} copy(bf16[9,32,2,128]{3,2,1,0:T(2,128)(2,1)} %bitcast.20) | data formatting | bytes 294912 | tf_op jit(solution)/shard_map/reshape;squeeze | solution.py:229
  2.3 0.0 copy-start.1
  2.3 47.4 %all-to-all-start.1 = ((bf16[32,9,2,128]{3,2,1,0:T(2,128)(2,1)}), bf16[32,9,2,128]{3,2,1,0:T(2,128)(2,1)S(1)}, u32[]{:S(2)}, u32[]{:S(2)}) async-start(bf16[32,9,2,128]{3,2,1,0:T(2,128)(2,1)} %bitcast.16), calls=%async_computation.1 | async-start | bytes 294912 | tf_op jit(solution)/shard_map/all_to_all | solution.py:232
  49.7 0.0 copy-done.1
  49.7 12.4 %all-gather = bf16[1,36,64,128]{3,2,0,1:T(8,128)(2,1)S(1)} all-gather(bf16[1,9,64,128]{3,2,0,1:T(8,128)(2,1)S(1)} %bitcast.21), channel_id=2, replica_groups=mesh['groups'=2,'far'=4,'near'=8,'vir'=4,'sub'=2] {'vir'}, dimensions={1}, use_global_device_ids=true | all-gather | bytes 737280 | tf_op jit(solution)/shard_map/all_gather | solution.py:240
  62.1 4.0 %collective-permute-start = (bf16[36,64,128]{2,1,0:T(8,128)(2,1)S(1)}, bf16[36,64,128]{2,1,0:T(8,128)(2,1)S(1)}, u32[]{:S(2)}, u32[]{:S(2)}) collective-permute-start(bf16[36,64,128]{2,1,0:T(8,128)(2,1)S(1)} %bitcast.17), channel_id=1, source_target_pairs={{0,1},{1,0},{2,3},{3,2},{4,5},{5,4},{6,7},{7,6},{8,9},{9,8},{10,11... | collective-permute-start | bytes 1769480 | tf_op jit(solution)/shard_map/ppermute | solution.py:241
  66.1 0.0 copy-start.2
  66.2 0.7 copy-done.2
  66.8 0.1 copy.9.tiles_ref
  66.9 0.1 pad_add_fusion.place_ref
  67.0 0.0 copy-start
  67.0 0.1 constant_dynamic-slice_fusion
  67.1 0.7 collective-permute-done.other_ref
  67.8 0.0 copy-done
  67.8 3.5 %virt_partial.1 = (s16[8,80,128]{2,1,0:T(8,128)(2,1)}, f32[1,128]{1,0:T(1,128)S(1)}) custom-call(s32[36,2]{1,0:T(8,128)S(1)} %copy.9.tiles_ref, s32[3]{0:T(128)S(1)} %pad_add_fusion.place_ref, s32[1,2]{1,0:T(1,128)S(1)} %copy-done, bf16[36,64,128]{2,1,0:T(8,128)(2,1)S(1)} %bitcast.18, bf16[36,64,128]{2,1,0:T(8,128)(2,1)S(1)} %collective-permute-done.other_ref), custom_call_target="tpu_custom_call" | custom-call | tf_op jit(solution)/shard_map/virt_partial/pallas_call | solution.py:201
  71.2 4.7 %all-to-all-done.1 = bf16[32,9,2,128]{3,2,1,0:T(2,128)(2,1)S(1)} async-done(((bf16[32,9,2,128]{3,2,1,0:T(2,128)(2,1)}), bf16[32,9,2,128]{3,2,1,0:T(2,128)(2,1)S(1)}, u32[]{:S(2)}, u32[]{:S(2)}) %all-to-all-start.1) | async-done | bytes 147488 | tf_op jit(solution)/shard_map/all_to_all | solution.py:232
  75.9 7.9 %all-to-all-start = ((s16[8,80,128]{2,1,0:T(8,128)(2,1)}), s16[8,80,128]{2,1,0:T(8,128)(2,1)S(1)}, u32[]{:S(2)}, u32[]{:S(2)}) async-start(s16[8,80,128]{2,1,0:T(8,128)(2,1)} %get-tuple-element.7), calls=%async_computation | async-start | bytes 327680 | tf_op jit(solution)/shard_map/all_to_all | solution.py:293
  83.8 0.1 iota_compare_fusion
  83.8 0.1 and_not_fusion
  83.9 0.1 broadcast_select_fusion
  84.1 0.1 select_n.13
  84.1 0.1 reshape.81
  84.2 0.2 convolution_bitcast_fusion
  84.4 0.1 reshape.77
  84.5 9.2 %psum.7.gram_ref = f32[8,128]{1,0:T(8,128)S(1)} all-reduce(f32[8,128]{1,0:T(8,128)S(1)} %reshape.77), channel_id=1, replica_groups=mesh['groups'=2,'far'=4,'near'=8,'vir'=4,'sub'=2] {'vir'}, use_global_device_ids=true, to_apply=%region_0.1 | all-reduce | flops 1024 | bytes 8192 | tf_op jit(solution)/shard_map/psum | solution.py:262
  93.6 0.0 all-to-all-done.parts_ref
  93.6 0.3 shard_map.50
  93.9 24.8 %all_to_all.20.parts_ref = s16[4,96,128]{2,1,0:T(8,128)(2,1)S(1)} all-to-all(s16[4,96,128]{2,1,0:T(8,128)(2,1)S(1)} %shard_map.50), channel_id=1, replica_groups={{128,192,0,64},{129,193,1,65},{130,194,2,66},{131,195,3,67},{132,196,4,..., dimensions={0} | all-to-all | bytes 196608 | tf_op jit(solution)/shard_map/all_to_all | solution.py:293
  118.7 0.2 shard_map.51
  118.9 12.9 %all_to_all.21.spread_ref = s16[8,96,128]{2,1,0:T(8,128)(2,1)S(1)} all-to-all(s16[8,96,128]{2,1,0:T(8,128)(2,1)S(1)} %shard_map.51), channel_id=1, replica_groups={{32,40,48,56,0,8,16,24},{33,41,49,57,1,9,17,25},{34,42,50,58,2,10,18,26..., dimensions={0} | all-to-all | bytes 393216 | tf_op jit(solution)/shard_map/all_to_all | solution.py:293
  131.9 0.9 shard_map.52
  132.7 8.5 %all-gather.1 = f32[16,128]{1,0:T(8,128)S(1)} all-gather(f32[8,128]{1,0:T(8,128)S(1)} %get-tuple-element.10), channel_id=3, replica_groups=mesh['groups'=2,'far'=4,'near'=8,'vir'=4,'sub'=2] {'sub'}, dimensions={0}, use_global_device_ids=true | all-gather | bytes 12288 | tf_op jit(solution)/shard_map/all_gather | solution.py:285
  141.2 1.6 %shard_map.53 = f32[256,256]{1,0:T(8,128)} custom-call(f32[2,8,128]{2,1,0:T(8,128)S(1)} %bitcast.19, f32[1,128]{1,0:T(1,128)S(1)} %get-tuple-element.11.ids_ref), custom_call_target="tpu_custom_call" | custom-call | tf_op jit(solution)/shard_map/pallas_call | solution.py:137
  (3 shorter events, 0.0 us)
Async XLA Ops:
  2.3 47.4 %copy-start.1 = (bf16[1,9,64,128]{3,2,1,0:T(8,128)(2,1)S(1)}, bf16[1,9,64,128]{3,2,1,0:T(8,128)(2,1)}, u32[]{:S(2)}) copy-start(bf16[1,9,64,128]{3,2,1,0:T(8,128)(2,1)} %param.3) | copy-start | bytes 442372
  2.3 73.6 %all-to-all-start.1 = ((bf16[32,9,2,128]{3,2,1,0:T(2,128)(2,1)}), bf16[32,9,2,128]{3,2,1,0:T(2,128)(2,1)S(1)}, u32[]{:S(2)}, u32[]{:S(2)}) async-start(bf16[32,9,2,128]{3,2,1,0:T(2,128)(2,1)} %bitcast.16), calls=%async_computation.1 | async-start | bytes 294912 | tf_op jit(solution)/shard_map/all_to_all | solution.py:232
  62.1 5.6 %collective-permute-start = (bf16[36,64,128]{2,1,0:T(8,128)(2,1)S(1)}, bf16[36,64,128]{2,1,0:T(8,128)(2,1)S(1)}, u32[]{:S(2)}, u32[]{:S(2)}) collective-permute-start(bf16[36,64,128]{2,1,0:T(8,128)(2,1)S(1)} %bitcast.17), channel_id=1, source_target_pairs={{0,1},{1,0},{2,3},{3,2},{4,5},{5,4},{6,7},{7,6},{8,9},{9,8},{10,11... | collective-permute-start | bytes 1769480 | tf_op jit(solution)/shard_map/ppermute | solution.py:241
  66.1 0.7 copy-start.2
  67.0 0.7 copy-start
  75.9 17.7 %all-to-all-start = ((s16[8,80,128]{2,1,0:T(8,128)(2,1)}), s16[8,80,128]{2,1,0:T(8,128)(2,1)S(1)}, u32[]{:S(2)}, u32[]{:S(2)}) async-start(s16[8,80,128]{2,1,0:T(8,128)(2,1)} %get-tuple-element.7), calls=%async_computation | async-start | bytes 327680 | tf_op jit(solution)/shard_map/all_to_all | solution.py:293
